TPU v7x, 128 devices: a whole 4x4x4 slice. The times are simulated.
128 devices in a mesh: obl: 16 (over y, z), scn: 8 (over x, core).
Axes of the slice: x: 4, y: 4, z: 4, core: 2. Of those that a mesh axis runs over, the one named last changes fastest.
Arguments:
- factors: bfloat16 [32768, 128], P('scn'), may hold values from -6 to 6
- idiosyncratic: bfloat16 [32768, 32768], P('obl', 'scn'), may hold values from -6 to 6
- loadings: bfloat16 [32768, 128], P('obl'), may hold values from -0.375 to 0.375
- rating: int32 [32768], P('obl'), may hold values from 0 to 15
- barrier: float32 [16], replicated, may hold values from 1 to 3
- loss_given: float32 [32768], P('obl'), may hold values from 0.2 to 0.9
- sector: int32 [32768], P('obl'), may hold values from 0 to 15, as said below
- allowed: int32 [256, 16], replicated, may hold values from 0 to 1, as said below
- holdings: float32 [32768, 256], P('obl'), may hold values from 0.1 to 10
Outputs:
- positions: float32 [32768, 256], P('obl')
- shortfall: float32 [2, 256], replicated
Inputs may be any that keep to these rules, and one draw needn't show every extreme that they name: Each sector holds exactly 2048 obligors. `allowed`: every mandate allows at least one sector.
All inputs are finite; a program needn't handle non-finite values.
Results may differ from a plain program's by a relative error of at most 0.0003.
Values may be sent and summed in bfloat16 or wider, within the bound.
No kernel may reach another device: no remote copies, remote signals or barrier semaphores. Data moves between devices by JAX's collectives and lax.ppermute only.
A program may use at most 128 MiB of HBM per device.

v0:
```python
import functools

import jax
import jax.numpy as jnp
from jax import lax
from jax.sharding import Mesh
from jax.sharding import PartitionSpec as P

STEPS = 2
OBL = ("obl_0", "obl_1")


IDIO_SCALE = 0.8
SHARP = 2.0
LEVEL = 0.99
QUANTILE = 2.326
SMOOTH = 0.5
EPSILON = 1e-06
STEP_RATE = 8.0


def one_axis_at_a_time(array, axes):
    return functools.reduce(lax.psum, axes, array)


def copy_for_each(array, axis):
    devices = lax.axis_size(axis)
    return lax.all_to_all(
        jnp.broadcast_to(array[None], (devices, *array.shape)), axis, 0, 0, tiled=True
    )


def over_copies(array, axis):
    everything = copy_for_each(array, axis)
    return jnp.sum(everything, axis=0)


def together(arrays, axis):
    vector, at, outs = (jnp.concatenate([a.reshape(-1) for a in arrays]), 0, [])
    running = over_copies(vector, axis)
    for a in arrays:
        outs.append(running[at : at + a.size].reshape(a.shape))
        at += a.size
    return tuple(outs)


def filled_up(lines, devices):
    spare = -len(lines) % devices
    return jnp.pad(lines, [(0, spare)] + [(0, 0)] * (lines.ndim - 1))


def total_of(array, axis):
    lines = array.reshape(-1, *array.shape[1:][-1:])
    own = lax.psum_scatter(
        filled_up(lines, lax.axis_size(axis)), axis, scatter_dimension=0, tiled=True
    )
    whole = lax.all_gather(own, axis).reshape(-1, *lines.shape[1:])
    return lax.slice_in_dim(whole, 0, len(lines)).reshape(array.shape)


def tail_terms(losses, center, spread, tail_scale):
    deviation = jnp.sqrt(spread + EPSILON)
    thresh = center + QUANTILE * deviation
    smooth_width = SMOOTH * deviation
    scaled = (losses - thresh) / smooth_width
    tail_weight = (jax.nn.sigmoid(scaled) * tail_scale).astype(jnp.bfloat16)
    return (scaled, thresh, smooth_width, tail_weight)


def on_device(
    factors, idiosyncratic, loadings, rating, barrier, loss_given, sector, allowed, holdings
):
    obl_dev = idiosyncratic.shape[0]
    scn_dev = idiosyncratic.shape[1]
    obligors = obl_dev * lax.axis_size(OBL)
    scenarios = scn_dev * lax.axis_size("scn")
    tail_scale = 1.0 / ((1.0 - LEVEL) * scenarios)
    sector_hot = (sector[:, None] == jnp.arange(allowed.shape[1])[None, :]).astype(jnp.float32)
    eligible = lax.dot_general(
        sector_hot,
        allowed.astype(jnp.float32),
        (((1,), (1,)), ((), ())),
        precision=lax.Precision.HIGHEST,
    )
    rating_hot = (rating[:, None] == jnp.arange(barrier.shape[0])[None, :]).astype(jnp.float32)
    barrier_rows = jnp.dot(rating_hot, barrier, precision=lax.Precision.HIGHEST)
    systematic = lax.dot_general(
        loadings, factors, (((1,), (1,)), ((), ())), preferred_element_type=jnp.float32
    )
    latent = systematic + IDIO_SCALE * idiosyncratic.astype(jnp.float32)
    default_prob = jax.nn.sigmoid((latent - barrier_rows[:, None]) * SHARP).astype(jnp.bfloat16)
    weighted = eligible * holdings
    totals = one_axis_at_a_time(jnp.sum(weighted, 0), OBL)
    positions = obligors * weighted / totals
    results = []
    for iteration in range(STEPS):
        exposure = (loss_given[:, None] * positions / obligors).astype(jnp.bfloat16)
        partial_value = lax.dot_general(
            default_prob, exposure, (((0,), (0,)), ((), ())), preferred_element_type=jnp.float32
        )
        losses = lax.psum(partial_value, OBL)
        first, second = together((jnp.sum(losses, 0), jnp.sum(losses * losses, 0)), "scn")
        center = first / scenarios
        spread = second / scenarios - center * center
        scaled, thresh, smooth_width, tail_weight = tail_terms(losses, center, spread, tail_scale)
        tail_sum = over_copies(jnp.sum(jax.nn.softplus(scaled), 0), "scn")
        results.append(thresh + smooth_width * (tail_sum * tail_scale))
        gradient = jnp.dot(default_prob, tail_weight, preferred_element_type=jnp.float32)
        gradient = total_of(gradient, "scn")
        gradient = loss_given[:, None] * eligible * gradient
        unnorm = positions * jnp.exp(-STEP_RATE * gradient)
        totals = one_axis_at_a_time(jnp.sum(unnorm, 0), OBL)
        positions = obligors * unnorm / totals
    return (positions, jnp.stack(results))


def solution(mesh):
    finer = Mesh(mesh.devices.reshape(4, 4, mesh.shape["scn"]), ("obl_0", "obl_1", "scn"))
    in_specs = (
        P("scn", None),
        P(OBL, "scn"),
        P(OBL, None),
        P(OBL),
        P(),
        P(OBL),
        P(OBL),
        P(),
        P(OBL, None),
    )
    out_specs = (P(OBL, None), P())
    return jax.shard_map(
        on_device, mesh=finer, in_specs=in_specs, out_specs=out_specs, check_vma=False
    )
```

profile of v0, /device:TPU:0, one launch (start us, length us, event | category | flops | bytes accessed | tf_op | source)
XLA Modules:
  0.0 505.9 jit_solution(1851774986560804028)
XLA Ops:
  7.2 2.7 multiply_reduce_fusion.2
  9.9 10.9 %psum.56 = f32[256]{0:T(256)S(1)} all-reduce(f32[256]{0:T(256)S(1)} %get-tuple-element.14), channel_id=1, replica_groups=mesh['obl_0'=4,'obl_1'=4,'scn'=8] {'obl_0'}, use_global_device_ids=true, to_apply=%region_1.0 | all-reduce | flops 256 | bytes 2048 | tf_op jit(solution)/shard_map/psum | solution.py:23
  20.8 11.8 %psum.57 = f32[256]{0:T(256)S(1)} all-reduce(f32[256]{0:T(256)S(1)} %psum.56), channel_id=1, replica_groups=mesh['obl_0'=4,'obl_1'=4,'scn'=8] {'obl_1'}, use_global_device_ids=true, to_apply=%region_2.0 | all-reduce | flops 256 | bytes 2048 | tf_op jit(solution)/shard_map/psum | solution.py:23
  32.5 0.7 fusion.15
  33.3 16.5 %divide_convert_fusion = bf16[2048,4096]{1,0:T(8,128)(2,1)} fusion(bf16[2048,4096]{1,0:T(8,128)(2,1)} %param.10, f32[2048]{0:T(1024)S(1)} %bitcast.14, bf16[2048,128]{1,0:T(8,128)(2,1)} %param.11, bf16[4096,128]{1,0:T(8,128)(2,1)S(1)} %copy-done), kind=kOutput, calls=%fused_computation | convolution fusion | flops 2222981120 | bytes 35135488 | tf_op jit(solution)/shard_map/dot_general | solution.py:87
  49.8 13.6 %fusion.8 = f32[4096,256]{1,0:T(8,128)} fusion(bf16[2048,4096]{1,0:T(8,128)(2,1)} %divide_convert_fusion, f32[2048]{0:T(1024)S(1)} %copy-done.2, f32[256]{0:T(256)S(1)} %psum.57, f32[2048,256]{1,0:T(8,128)S(1)} %get-tuple-element.15, f32[2048,256]{1,0:T(8,128)} %param.17), kind=kOutput, calls=%fused_computation.24 | convolution fusion | flops 4298113024 | bytes 25175040 | tf_op jit(solution)/shard_map/dot_general | solution.py:98
  63.5 100.8 %all-reduce.3.cloned.1.call-done = f32[4096,256]{1,0:T(8,128)} async-done(((f32[4096,256]{1,0:T(8,128)}), f32[4096,256]{1,0:T(8,128)}) %all-reduce.3.cloned.1.call-update) | async-done | bytes 4194320 | tf_op jit(solution)/shard_map/psum | solution.py:101
  164.3 2.7 fusion.29
  167.0 9.4 %all_to_all.24 = f32[8,1,512]{2,1,0:T(1,128)S(1)} all-to-all(f32[8,1,512]{2,1,0:T(1,128)S(1)} %broadcast_in_dim.8), channel_id=1, replica_groups=mesh['obl_0'=4,'obl_1'=4,'scn'=8] {'scn'}, dimensions={0} | all-to-all | bytes 32768 | tf_op jit(solution)/shard_map/all_to_all | solution.py:28
  176.5 13.1 %fusion.2 = f32[2048,256]{1,0:T(8,128)} fusion(bf16[2048,4096]{1,0:T(8,128)(2,1)} %divide_convert_fusion, f32[4096,256]{1,0:T(8,128)} %all-reduce.3.cloned.1.call-done, f32[256]{0:T(256)S(1)} %broadcast_multiply_fusion.1, f32[256]{0:T(256)S(1)} %get-tuple-element.12), kind=kOutput, calls=%fused_computation.11 | convolution fusion | flops 4302307328 | bytes 23070720 | tf_op jit(solution)/shard_map/dot_general | solution.py:108
  189.7 31.7 %reduce-scatter.3.cloned.1.call-done = f32[256,256]{1,0:T(8,128)} async-done(((f32[2048,256]{1,0:T(8,128)}), f32[256,256]{1,0:T(8,128)}) %reduce-scatter.3.cloned.1.call-update) | async-done | bytes 262160 | tf_op jit(solution)/shard_map/reduce_scatter | solution.py:54
  221.5 25.9 %all-gather.5.cloned.1.call-done = f32[2048,256]{1,0:T(8,128)} async-done(((f32[256,256]{1,0:T(8,128)}), f32[2048,256]{1,0:T(8,128)}) %all-gather.5.cloned.1.call-update) | async-done | bytes 2097168 | tf_op jit(solution)/shard_map/all_gather | solution.py:57
  247.4 4.3 fusion.31
  251.7 10.4 %psum.59 = f32[256]{0:T(256)S(1)} all-reduce(f32[256]{0:T(256)S(1)} %get-tuple-element.10), channel_id=1, replica_groups=mesh['obl_0'=4,'obl_1'=4,'scn'=8] {'obl_0'}, use_global_device_ids=true, to_apply=%region_9.10 | all-reduce | flops 256 | bytes 2048 | tf_op jit(solution)/shard_map/psum | solution.py:23
  262.1 10.7 %psum.60 = f32[256]{0:T(256)S(1)} all-reduce(f32[256]{0:T(256)S(1)} %psum.59), channel_id=1, replica_groups=mesh['obl_0'=4,'obl_1'=4,'scn'=8] {'obl_1'}, use_global_device_ids=true, to_apply=%region_10.11 | all-reduce | flops 256 | bytes 2048 | tf_op jit(solution)/shard_map/psum | solution.py:23
  272.8 13.6 %fusion.9 = f32[4096,256]{1,0:T(8,128)} fusion(bf16[2048,4096]{1,0:T(8,128)(2,1)} %divide_convert_fusion, f32[2048]{0:T(1024)S(1)} %copy-done.2, f32[2048,256]{1,0:T(8,128)} %get-tuple-element.11, f32[256]{0:T(256)S(1)} %psum.60), kind=kOutput, calls=%fused_computation.25 | convolution fusion | flops 4297588736 | bytes 23077888 | tf_op jit(solution)/shard_map/dot_general | solution.py:98
  286.6 99.7 %all-reduce.5.cloned.1.call-done = f32[4096,256]{1,0:T(8,128)} async-done(((f32[4096,256]{1,0:T(8,128)}), f32[4096,256]{1,0:T(8,128)}) %all-reduce.5.cloned.1.call-update) | async-done | bytes 4194320 | tf_op jit(solution)/shard_map/psum | solution.py:101
  386.3 2.7 fusion.28
  389.1 9.4 %all_to_all.25 = f32[8,1,512]{2,1,0:T(1,128)S(1)} all-to-all(f32[8,1,512]{2,1,0:T(1,128)S(1)} %broadcast_in_dim.9), channel_id=1, replica_groups=mesh['obl_0'=4,'obl_1'=4,'scn'=8] {'scn'}, dimensions={0} | all-to-all | bytes 32768 | tf_op jit(solution)/shard_map/all_to_all | solution.py:28
  398.5 13.2 %fusion.3 = f32[2048,256]{1,0:T(8,128)} fusion(bf16[2048,4096]{1,0:T(8,128)(2,1)} %divide_convert_fusion, f32[4096,256]{1,0:T(8,128)} %all-reduce.5.cloned.1.call-done, f32[256]{0:T(256)S(1)} %broadcast_multiply_fusion, f32[256]{0:T(256)S(1)} %get-tuple-element.8), kind=kOutput, calls=%fused_computation.12 | convolution fusion | flops 4302307328 | bytes 23070720 | tf_op jit(solution)/shard_map/dot_general | solution.py:108
  411.8 31.8 %reduce-scatter.5.cloned.1.call-done = f32[256,256]{1,0:T(8,128)} async-done(((f32[2048,256]{1,0:T(8,128)}), f32[256,256]{1,0:T(8,128)}) %reduce-scatter.5.cloned.1.call-update) | async-done | bytes 262160 | tf_op jit(solution)/shard_map/reduce_scatter | solution.py:54
  443.6 4.8 fusion
  448.4 7.7 %all_to_all.26 = f32[8,1,256]{2,1,0:T(1,128)S(1)} all-to-all(f32[8,1,256]{2,1,0:T(1,128)S(1)} %broadcast_in_dim.10), channel_id=1, replica_groups=mesh['obl_0'=4,'obl_1'=4,'scn'=8] {'scn'}, dimensions={0} | all-to-all | bytes 16384 | tf_op jit(solution)/shard_map/all_to_all | solution.py:28
  456.1 4.8 fusion.1
  460.9 0.6 broadcast_in_dim.11
  461.5 3.3 all-to-all-start.3
  464.8 5.2 %all-to-all-done.3 = f32[8,1,256]{2,1,0:T(1,128)S(1)} async-done(((f32[8,1,256]{2,1,0:T(1,128)}), f32[8,1,256]{2,1,0:T(1,128)S(1)}, u32[]{:S(2)}, u32[]{:S(2)}) %all-to-all-start.3) | async-done | bytes 8224 | tf_op jit(solution)/shard_map/all_to_all | solution.py:28
  470.0 0.6 pad_maximum_fusion.2
  470.6 4.3 fusion.30
  474.9 10.4 %psum.62 = f32[256]{0:T(256)S(1)} all-reduce(f32[256]{0:T(256)S(1)} %get-tuple-element.6), channel_id=1, replica_groups=mesh['obl_0'=4,'obl_1'=4,'scn'=8] {'obl_0'}, use_global_device_ids=true, to_apply=%region_17.18 | all-reduce | flops 256 | bytes 2048 | tf_op jit(solution)/shard_map/psum | solution.py:23
  485.4 10.7 %psum.63 = f32[256]{0:T(256)S(1)} all-reduce(f32[256]{0:T(256)S(1)} %psum.62), channel_id=1, replica_groups=mesh['obl_0'=4,'obl_1'=4,'scn'=8] {'obl_1'}, use_global_device_ids=true, to_apply=%region_18.19 | all-reduce | flops 256 | bytes 2048 | tf_op jit(solution)/shard_map/psum | solution.py:23
  496.0 3.1 multiply_divide_fusion
  (38 shorter events, 0.8 us)
Async XLA Ops:
  7.2 26.1 %copy-start = (bf16[4096,128]{1,0:T(8,128)(2,1)S(1)}, bf16[4096,128]{1,0:T(8,128)(2,1)}, u32[]{:S(2)}) copy-start(bf16[4096,128]{1,0:T(8,128)(2,1)} %param.9) | copy-start | bytes 3145732
  7.2 25.3 %copy-start.4 = (f32[16]{0:T(128)S(1)}, f32[16]{0:T(128)}, u32[]{:S(2)}) copy-start(f32[16]{0:T(128)} %param.13) | copy-start | bytes 196
  7.2 25.3 %copy-start.3 = (s32[2048]{0:T(1024)S(1)}, s32[2048]{0:T(1024)}, u32[]{:S(2)}) copy-start(s32[2048]{0:T(1024)} %param.12) | copy-start | bytes 24580
  7.2 157.1 %all-reduce.3.cloned.1.call-start = ((), (), s32[]{:S(2)}) async-start(), calls=%async_computation.6 | async-start | bytes 8388608 | tf_op jit(solution)/shard_map/psum | solution.py:101
  33.2 16.5 %copy-start.2 = (f32[2048]{0:T(1024)S(1)}, f32[2048]{0:T(1024)}, u32[]{:S(2)}) copy-start(f32[2048]{0:T(1024)} %param.14) | copy-start | bytes 24580
  63.4 158.0 %reduce-scatter.3.cloned.1.call-start = ((), (), s32[]{:S(2)}) async-start(), calls=%async_computation.7 | async-start | bytes 2359296 | tf_op jit(solution)/shard_map/reduce_scatter | solution.py:54
  189.7 57.7 %all-gather.5.cloned.1.call-start = ((), (), s32[]{:S(2)}) async-start(), calls=%async_computation.10 | async-start | bytes 2359296 | tf_op jit(solution)/shard_map/all_gather | solution.py:57
  221.5 164.8 %all-reduce.5.cloned.1.call-start = ((), (), s32[]{:S(2)}) async-start(), calls=%async_computation.8 | async-start | bytes 8388608 | tf_op jit(solution)/shard_map/psum | solution.py:101
  286.4 157.3 %reduce-scatter.5.cloned.1.call-start = ((), (), s32[]{:S(2)}) async-start(), calls=%async_computation.9 | async-start | bytes 2359296 | tf_op jit(solution)/shard_map/reduce_scatter | solution.py:54
  411.8 58.9 %all-gather.7.cloned.1.call-start = ((), (), s32[]{:S(2)}) async-start(), calls=%async_computation.11 | async-start | bytes 2359296 | tf_op jit(solution)/shard_map/all_gather | solution.py:57
  461.5 8.5 %all-to-all-start.3 = ((f32[8,1,256]{2,1,0:T(1,128)}), f32[8,1,256]{2,1,0:T(1,128)S(1)}, u32[]{:S(2)}, u32[]{:S(2)}) async-start(f32[8,1,256]{2,1,0:T(1,128)} %broadcast_in_dim.11), calls=%async_computation.5 | async-start | bytes 16384 | tf_op jit(solution)/shard_map/all_to_all | solution.py:28
  470.6 28.5 %copy-start.1 = (bf16[4096,128]{1,0:T(8,128)(2,1)S(1)}, bf16[4096,128]{1,0:T(8,128)(2,1)}, u32[]{:S(2)}) copy-start(bf16[4096,128]{1,0:T(8,128)(2,1)} %param.9) | copy-start | bytes 3145732
Sparse Core Ops, SparseCore 0:
  63.5 100.6 all-reduce.2
  189.8 31.5 reduce-scatter.2
  223.2 24.1 all-gather.4
  286.5 99.7 all-reduce.4
  411.9 31.6 reduce-scatter.4
  445.2 24.0 all-gather.6
where the time goes:
time: 507 us; the launch traced here: 506 us
  waiting for transfers between devices  295 us (58%)
  blocking collectives  91.3 us (18%)
  matrix products  73.4 us (14%)
  other arithmetic  27.4 us (5%)
  between operations  14.2 us (3%)
    psum x2, waiting for transfers between devices, on_device(): losses = lax.psum(partial_value, OBL)  200 us
    psum x6, blocking collectives, one_axis_at_a_time(): return functools.reduce(lax.psum, axes, array)  64.8 us
    reduce_scatter x2, waiting for transfers between devices, total_of(): lax.psum_scatter(filled_up(lines, lax.axis_size(axis)), axis, scatter_dim...  63.5 us
    dot_general x2, matrix products, on_device(): lax.dot_general(default_prob, exposure, (((0,), (0,)), ((), ())), preferr...  27.2 us
    all_to_all x3, blocking collectives, copy_for_each(): lax.all_to_all(jnp.broadcast_to(array[None], (devices, *array.shape)), ax...  26.5 us
    dot_general x2, matrix products, on_device(): jnp.dot(default_prob, tail_weight, preferred_element_type=jnp.float32)  26.4 us
    all_gather x2, waiting for transfers between devices, total_of(): whole = lax.all_gather(own, axis).reshape(-1, *lines.shape[1:])  25.9 us
    dot_general x1, matrix products, on_device(): lax.dot_general(loadings, factors, (((1,), (1,)), ((), ())), preferred_el...  16.5 us
  transfers between devices with their start and end apart: 7, of which 6 were waited for; matrix products, arithmetic and copies ran while one was open for 2% of the time, Pallas kernels for 0%

commit v1 on v0

v1 whole, which is shorter than its diff:
```python
import functools

import jax
import jax.numpy as jnp
from jax import lax
from jax.experimental import pallas as pl
from jax.experimental.pallas import tpu as pltpu
from jax.sharding import Mesh
from jax.sharding import PartitionSpec as P

STEPS = 2
OBL = ("y", "z")
SCN = ("x", "c")
IDIO_SCALE = 0.8
LEVEL = 0.99
QUANTILE = 2.326
SMOOTH = 0.5
EPSILON = 1e-06
STEP_RATE = 8.0
HEAD = 16
SPAN = 127.0
INTERPRET = False

f32 = jnp.float32
bf16 = jnp.bfloat16


def call(kernel, grid, in_specs, out_specs, out_shape, scratch=(), prefetch=0, flops=0, nbytes=0, name=None):
    spec = pltpu.PrefetchScalarGridSpec(
        num_scalar_prefetch=prefetch, grid=grid, in_specs=in_specs, out_specs=out_specs, scratch_shapes=list(scratch)
    )
    return pl.pallas_call(
        kernel,
        grid_spec=spec,
        out_shape=out_shape,
        compiler_params=pltpu.CompilerParams(vmem_limit_bytes=56 * 1024 * 1024),
        cost_estimate=pl.CostEstimate(flops=int(flops), bytes_accessed=int(nbytes), transcendentals=0),
        interpret=INTERPRET,
        name=name,
    )


def split3(value):
    a = value.astype(bf16)
    rest = value - a.astype(f32)
    b = rest.astype(bf16)
    c = (rest - b.astype(f32)).astype(bf16)
    return [a.astype(f32), b.astype(f32), c.astype(f32)]


def join3(head, at):
    return head[at : at + 1] + head[at + 1 : at + 2] + head[at + 2 : at + 3]


def encode(values, extra):
    low = jnp.min(values, axis=0, keepdims=True)
    high = jnp.max(values, axis=0, keepdims=True)
    span = jnp.maximum(jnp.maximum(high - low, jnp.abs(low) * (1.0 / 64.0)), 1e-30)
    base = low.astype(bf16).astype(f32)
    span = (span * 1.02).astype(bf16).astype(f32)
    code = jnp.exp((values - base) * (SPAN / span) - 0.5 * SPAN).astype(bf16)
    rows = [base, span]
    for row in extra:
        rows += split3(row)
    rows.append(jnp.zeros((HEAD - len(rows), values.shape[1]), f32))
    return code, jnp.concatenate(rows, axis=0).astype(bf16)


def decode(code, head):
    base, span = head[0:1], head[1:2]
    return (base + 0.5 * span) + jnp.log(code.astype(f32)) * (span * (1.0 / SPAN))


def setup_kernel(hold_ref, lgd_ref, sector_ref, allowed_ref, weighted_ref, elig_ref, expot_ref, tot_ref):
    hot = (sector_ref[...] == lax.broadcasted_iota(jnp.int32, (1, allowed_ref.shape[0]), 1)).astype(bf16)
    elig = jnp.dot(hot, allowed_ref[...], preferred_element_type=f32)
    weighted = elig * hold_ref[...]
    weighted_ref[...] = weighted
    elig_ref[...] = elig.astype(bf16)
    expot_ref[...] = jnp.transpose(weighted * lgd_ref[...]).astype(bf16)

    @pl.when(pl.program_id(0) == 0)
    def _():
        tot_ref[...] = jnp.zeros_like(tot_ref)

    tot_ref[0:1] += jnp.sum(weighted, axis=0, keepdims=True)


def first_losses_kernel(load_ref, fac_ref, idio_ref, expot_ref, tot_ref, p_ref, pay_ref, acc_ref):
    rows = fac_ref.shape[0]
    block = min(256, load_ref.shape[0])
    acc_ref[...] = jnp.zeros_like(acc_ref)
    for i in range(load_ref.shape[0] // block):
        sl = slice(i * block, (i + 1) * block)
        systematic = lax.dot_general(
            load_ref[sl], fac_ref[...], (((1,), (1,)), ((), ())), preferred_element_type=f32
        )
        prob = (0.5 * jnp.tanh(systematic + IDIO_SCALE * idio_ref[sl].astype(f32)) + 0.5).astype(bf16)
        p_ref[sl] = prob
        acc_ref[...] += jnp.dot(expot_ref[:, sl], prob, preferred_element_type=f32)
    code, head = encode(jnp.transpose(acc_ref[...]), [tot_ref[0:1]])
    pay_ref[0, 0:rows] = code
    pay_ref[0, rows : rows + HEAD] = head


def losses_kernel(p_ref, expot_ref, tot_ref, pay_ref):
    rows = p_ref.shape[1]
    losses = jnp.dot(expot_ref[...], p_ref[...], preferred_element_type=f32)
    code, head = encode(jnp.transpose(losses), [tot_ref[0:1]])
    pay_ref[0, 0:rows] = code
    pay_ref[0, rows : rows + HEAD] = head


def chunk_kernel(pay_ref, out_ref, acc_ref, tot_ref):
    step = pl.program_id(0)
    rows = acc_ref.shape[0]

    @pl.when(step == 0)
    def _():
        acc_ref[...] = jnp.zeros_like(acc_ref)
        tot_ref[...] = jnp.zeros_like(tot_ref)

    total = jnp.zeros_like(acc_ref)
    norm = jnp.zeros((1, acc_ref.shape[1]), f32)
    for k in range(pay_ref.shape[0]):
        head = pay_ref[k, rows : rows + HEAD].astype(f32)
        total += decode(pay_ref[k, 0:rows], head)
        norm += join3(head, 2)
    acc_ref[...] += total
    tot_ref[0:1] += norm

    @pl.when(step == pl.num_programs(0) - 1)
    def _():
        losses = acc_ref[...] / tot_ref[0:1]
        mean = jnp.sum(losses, axis=0, keepdims=True) * (1.0 / rows)
        off = losses - mean
        second = jnp.sum(off * off, axis=0, keepdims=True)
        code, head = encode(losses, [mean, second])
        for k in range(out_ref.shape[0]):
            out_ref[k, 0:rows] = code
            out_ref[k, rows : rows + HEAD] = head


def tail_kernel(tail_scale, pay_ref, stat_ref, weight_ref, soft_ref):
    rows = weight_ref.shape[0]
    head = pay_ref[0, rows : rows + HEAD].astype(f32)
    losses = decode(pay_ref[0, 0:rows], head)
    scaled = (losses - stat_ref[0:1]) * stat_ref[1:2]
    weight_ref[...] = (tail_scale / (1.0 + jnp.exp(-scaled))).astype(bf16)
    soft = jnp.maximum(scaled, 0.0) + jnp.log(1.0 + jnp.exp(-jnp.abs(scaled)))

    @pl.when(pl.program_id(0) == 0)
    def _():
        soft_ref[...] = jnp.zeros_like(soft_ref)

    soft_ref[0:1] += jnp.sum(soft, axis=0, keepdims=True)


def gradient_kernel(half_ref, p_ref, weight_ref, out_ref):
    out_ref[...] = jnp.dot(p_ref[...], weight_ref[...], preferred_element_type=f32)


def pair_kernel(own_ref, other_ref, soft_ref, soft_other_ref, pay_ref):
    rows = own_ref.shape[0]
    code, head = encode(own_ref[...] + other_ref[...], [soft_ref[0:1] + soft_other_ref[0:1]])
    pay_ref[0, 0:rows] = code
    pay_ref[0, rows : rows + HEAD] = head


def whole_kernel(pay_ref, out_ref, soft_ref):
    rows = pay_ref.shape[1] - HEAD
    total = jnp.zeros((rows, pay_ref.shape[2]), f32)
    soft = jnp.zeros((1, pay_ref.shape[2]), f32)
    for k in range(pay_ref.shape[0]):
        head = pay_ref[k, rows : rows + HEAD].astype(f32)
        total += decode(pay_ref[k, 0:rows], head)
        soft += join3(head, 2)
    soft_ref[...] = jnp.broadcast_to(soft, soft_ref.shape)
    code, head = encode(total, [])
    for k in range(out_ref.shape[0]):
        out_ref[k, 0:rows] = code
        out_ref[k, rows : rows + HEAD] = head


def update_kernel(core_ref, own_ref, other_ref, prev_ref, lgd_ref, elig_ref, unnorm_ref, expot_ref, tot_ref):
    rows = prev_ref.shape[0]
    step = pl.program_id(0)
    mine = (step // (pl.num_programs(0) // 2)) == core_ref[0]
    pay = jnp.where(mine, own_ref[0], other_ref[0])
    gradient = decode(pay[0:rows], pay[rows : rows + HEAD].astype(f32))
    gradient = lgd_ref[...] * elig_ref[...].astype(f32) * gradient
    unnorm = prev_ref[...] * jnp.exp(-STEP_RATE * gradient)
    unnorm_ref[...] = unnorm
    expot_ref[...] = jnp.transpose(unnorm * lgd_ref[...]).astype(bf16)

    @pl.when(step == 0)
    def _():
        tot_ref[...] = jnp.zeros_like(tot_ref)

    tot_ref[0:1] += jnp.sum(unnorm, axis=0, keepdims=True)


def scale_kernel(unnorm_ref, tot_ref, out_ref):
    out_ref[...] = unnorm_ref[...] * tot_ref[0:1]


def whole(shape):
    return pl.BlockSpec(shape, lambda *_: (0,) * len(shape))


def rounded(value):
    return lax.reduce_precision(value, 8, 7)


def on_device(factors, idiosyncratic, loadings, rating, barrier, loss_given, sector, allowed, holdings):
    sds = jax.ShapeDtypeStruct
    n_obl, n_x, n_c = lax.axis_size(OBL), lax.axis_size("x"), lax.axis_size("c")
    obl_dev, scn_dev = idiosyncratic.shape
    mandates = holdings.shape[1]
    obligors = obl_dev * n_obl
    scenarios = scn_dev * n_x * n_c
    tail_scale = 1.0 / ((1.0 - LEVEL) * scenarios)
    rs, ro = scn_dev // n_obl, obl_dev // (n_x * n_c)
    ps, po = rs + HEAD, ro + HEAD
    half = obl_dev // n_c
    core = lax.axis_index("c").astype(jnp.int32).reshape(1)
    lgd = loss_given[:, None]
    row8 = sds((8, mandates), f32)

    hot = rating[:, None] == jnp.arange(barrier.shape[0])[None, :]
    bar = jnp.sum(jnp.where(hot, barrier[None, :], 0.0), axis=1)
    bar_a = rounded(bar)
    bar_b = rounded(bar - bar_a)
    bar_c = bar - bar_a - bar_b
    parts = -jnp.stack([bar_a, bar_b, bar_c], axis=1)
    fdim = factors.shape[1]
    load_aug = jnp.concatenate([loadings, jnp.pad(parts, ((0, 0), (0, 125))).astype(bf16)], axis=1)
    ones = (jnp.arange(128) < 3).astype(bf16)
    fac_aug = jnp.concatenate([factors, jnp.broadcast_to(ones, (scn_dev, 128))], axis=1)

    blk = pl.BlockSpec((ro, mandates), lambda i, *_: (i, 0))
    col = pl.BlockSpec((ro, 1), lambda i, *_: (i, 0))
    colt = pl.BlockSpec((mandates, ro), lambda i, *_: (0, i))
    n_ro = obl_dev // ro
    prev, elig, expot, tot = call(
        setup_kernel,
        (n_ro,),
        [blk, col, col, whole((allowed.shape[1], mandates))],
        [blk, blk, colt, whole((8, mandates))],
        [sds((obl_dev, mandates), f32), sds((obl_dev, mandates), bf16), sds((mandates, obl_dev), bf16), row8],
        nbytes=obl_dev * mandates * 12,
        name="setup",
    )(holdings, lgd, sector[:, None], allowed.T.astype(bf16))

    results = []
    prob = None
    for iteration in range(STEPS):
        pay_shape = sds((n_obl, ps, mandates), bf16)
        pay_spec = pl.BlockSpec((1, ps, mandates), lambda i, *_: (i, 0, 0))
        if iteration == 0:
            prob, pay = call(
                first_losses_kernel,
                (n_obl,),
                [
                    whole((obl_dev, fdim + 128)),
                    pl.BlockSpec((rs, fdim + 128), lambda i: (i, 0)),
                    pl.BlockSpec((obl_dev, rs), lambda i: (0, i)),
                    whole((mandates, obl_dev)),
                    whole((8, mandates)),
                ],
                [pl.BlockSpec((obl_dev, rs), lambda i: (0, i)), pay_spec],
                [sds((obl_dev, scn_dev), bf16), pay_shape],
                scratch=[pltpu.VMEM((mandates, rs), f32)],
                flops=4 * obl_dev * scn_dev * mandates,
                nbytes=obl_dev * scn_dev * 4,
                name="first_losses",
            )(load_aug, fac_aug, idiosyncratic, expot, tot)
        else:
            pay = call(
                losses_kernel,
                (n_obl,),
                [
                    pl.BlockSpec((obl_dev, rs), lambda i: (0, i)),
                    whole((mandates, obl_dev)),
                    whole((8, mandates)),
                ],
                pay_spec,
                pay_shape,
                flops=2 * obl_dev * scn_dev * mandates,
                nbytes=obl_dev * scn_dev * 2,
                name="losses",
            )(prob, expot, tot)
        pay = lax.all_to_all(pay, OBL, 0, 0, tiled=True)
        group = max(1, n_obl // 4)
        pay = call(
            chunk_kernel,
            (n_obl // group,),
            [pl.BlockSpec((group, ps, mandates), lambda i: (i, 0, 0))],
            whole((n_obl, ps, mandates)),
            pay_shape,
            scratch=[pltpu.VMEM((rs, mandates), f32), pltpu.VMEM((8, mandates), f32)],
            nbytes=n_obl * ps * mandates * 4,
            name="chunk",
        )(pay)
        pay = lax.all_to_all(pay, OBL, 0, 0, tiled=True)

        heads = pay[:, rs : rs + 8].astype(f32)
        means = heads[:, 2] + heads[:, 3] + heads[:, 4]
        seconds = heads[:, 5] + heads[:, 6] + heads[:, 7]
        mean = jnp.sum(means, 0) / n_obl
        second = jnp.sum(seconds, 0) + rs * jnp.sum(jnp.square(means - mean), 0)
        both = jnp.broadcast_to(jnp.stack([mean, second])[None], (n_x * n_c, 2, mandates))
        both = lax.all_to_all(both, SCN, 0, 0, tiled=True)
        means, seconds = both[:, 0], both[:, 1]
        center = jnp.sum(means, 0) / (n_x * n_c)
        spread = (jnp.sum(seconds, 0) + scn_dev * jnp.sum(jnp.square(means - center), 0)) / scenarios
        deviation = jnp.sqrt(spread + EPSILON)
        thresh = center + QUANTILE * deviation
        width = SMOOTH * deviation
        stat = jnp.concatenate([jnp.stack([thresh, 1.0 / width]), jnp.zeros((6, mandates), f32)])

        weight, soft = call(
            functools.partial(tail_kernel, tail_scale),
            (n_obl,),
            [pay_spec, whole((8, mandates))],
            [pl.BlockSpec((rs, mandates), lambda i: (i, 0)), whole((8, mandates))],
            [sds((scn_dev, mandates), bf16), row8],
            nbytes=scn_dev * mandates * 4,
            name="tail",
        )(pay, stat)
        gblock = min(256, half)
        n_half = half // gblock

        def gradient_of(which):
            return call(
                gradient_kernel,
                (n_half,),
                [
                    pl.BlockSpec((gblock, scn_dev), lambda i, h: (h[0] * n_half + i, 0)),
                    whole((scn_dev, mandates)),
                ],
                pl.BlockSpec((gblock, mandates), lambda i, h: (i, 0)),
                sds((half, mandates), f32),
                prefetch=1,
                flops=2 * half * scn_dev * mandates,
                nbytes=half * scn_dev * 2,
                name="gradient",
            )(which, prob, weight)

        swap = [(0, 1), (1, 0)]
        sent = lax.ppermute(gradient_of(1 - core), "c", swap)
        soft_other = lax.ppermute(soft, "c", swap)
        kept = gradient_of(core)
        gpay_shape = sds((n_x, po, mandates), bf16)
        gpay_spec = pl.BlockSpec((1, po, mandates), lambda i, *_: (i, 0, 0))
        pay = call(
            pair_kernel,
            (n_x,),
            [blk, blk, whole((8, mandates)), whole((8, mandates))],
            gpay_spec,
            gpay_shape,
            nbytes=half * mandates * 10,
            name="pair",
        )(kept, sent, soft, soft_other)
        pay = lax.all_to_all(pay, "x", 0, 0, tiled=True)
        pay, soft = call(
            whole_kernel,
            (1,),
            [whole((n_x, po, mandates))],
            [whole((n_x, po, mandates)), whole((8, mandates))],
            [gpay_shape, row8],
            nbytes=half * mandates * 4,
            name="whole",
        )(pay)
        results.append(thresh + width * (soft[0] * tail_scale))
        pay = lax.all_to_all(pay, "x", 0, 0, tiled=True)
        other = lax.ppermute(pay, "c", swap)
        gspec = pl.BlockSpec((1, po, mandates), lambda i, *_: (i % n_x, 0, 0))
        prev, expot, tot = call(
            update_kernel,
            (n_ro,),
            [gspec, gspec, blk, col, blk],
            [blk, colt, whole((8, mandates))],
            [sds((obl_dev, mandates), f32), sds((mandates, obl_dev), bf16), row8],
            prefetch=1,
            nbytes=obl_dev * mandates * 14,
            name="update",
        )(core, pay, other, prev, lgd, elig)

    totals = lax.all_to_all(jnp.broadcast_to(tot[None], (n_obl, 8, mandates)), OBL, 0, 0, tiled=True)
    factor = obligors / jnp.sum(totals, axis=0)
    positions = call(
        scale_kernel,
        (max(1, obl_dev // 512),),
        [pl.BlockSpec((min(512, obl_dev), mandates), lambda i: (i, 0)), whole((8, mandates))],
        pl.BlockSpec((min(512, obl_dev), mandates), lambda i: (i, 0)),
        sds((obl_dev, mandates), f32),
        nbytes=obl_dev * mandates * 8,
        name="scale",
    )(prev, factor)
    return (positions, jnp.stack(results))


def solution(mesh):
    n_obl, n_scn = mesh.shape["obl"], mesh.shape["scn"]
    side = 1
    while side * side < n_obl:
        side *= 2
    fine = Mesh(mesh.devices.reshape(side, n_obl // side, n_scn // 2, 2), ("y", "z", "x", "c"))
    in_specs = (P(SCN, None), P(OBL, SCN), P(OBL, None), P(OBL), P(), P(OBL), P(OBL), P(), P(OBL, None))
    return jax.shard_map(on_device, mesh=fine, in_specs=in_specs, out_specs=(P(OBL, None), P()), check_vma=False)
```

time: 507 us -> 387 us (0.76)
  waiting for transfers between devices: 295 us -> 15 us
  Pallas kernels: 0 us -> 138 us
  blocking collectives: 91.3 us -> 200 us
  matrix products: 73.4 us -> 0 us
  other arithmetic: 27.4 us -> 8.74 us
  between operations: 14.2 us -> 0.83 us
  local copies, waits for them, and re-layouts: 0.66 us -> 11.6 us
  starting transfers between devices: 3.72 us -> 8.96 us
    psum x2 -> x0, waiting for transfers between devices: 200 us -> none  [on_device(): losses = lax.psum(partial_value, OBL)]
    all_to_all x3 -> x9, blocking collectives: 26.5 us -> 200 us  [the longest x4 138 us: on_device(): pay = lax.all_to_all(pay, OBL, 0, 0, tiled=True)]
    pallas_call x0 -> x18, Pallas kernels: none -> 138 us  [the longest x4 27.8 us: gradient_of(): call(gradient_kernel, (n_half,), [pl.BlockSpec((gblock, scn_dev), lambda...]
    dot_general x7 -> x0, matrix products: 73.4 us -> none  [the longest x2 27.2 us: on_device(): lax.dot_general(default_prob, exposure, (((0,), (0,)), ((), ())), preferr...]
    psum x6 -> x0, blocking collectives: 64.8 us -> none  [one_axis_at_a_time(): return functools.reduce(lax.psum, axes, array)]
    reduce_scatter x2 -> x0, waiting for transfers between devices: 63.5 us -> none  [total_of(): lax.psum_scatter(filled_up(lines, lax.axis_size(axis)), axis, scatter_dim...]
    all_gather x2 -> x0, waiting for transfers between devices: 25.9 us -> none  [total_of(): whole = lax.all_gather(own, axis).reshape(-1, *lines.shape[1:])]
    reduce_sum x10, other arithmetic: 23.7 us -> 1.24 us  [the longest x1 0.87 us: on_device(): bar = jnp.sum(jnp.where(hot, barrier[None, :], 0.0), axis=1)]
  transfers between devices with their start and end apart: 7 -> 8, of which waited for: 6 -> 4; matrix products, arithmetic and copies ran while one was open for 2% -> 1% of each run, Pallas kernels for 0% -> 4%
where the time goes in v1:
time: 387 us; the launch traced here: 383 us
  blocking collectives  200 us (52%)
  Pallas kernels  138 us (36%)
  waiting for transfers between devices  15 us (4%)
  local copies, waits for them, and re-layouts  11.6 us (3%)
  starting transfers between devices  8.96 us (2%)
  other arithmetic  8.74 us (2%)
    all_to_all x4, blocking collectives, on_device(): pay = lax.all_to_all(pay, OBL, 0, 0, tiled=True)  138 us
    all_to_all x4, blocking collectives, on_device(): pay = lax.all_to_all(pay, 'x', 0, 0, tiled=True)  55 us
    pallas_call x4, Pallas kernels, gradient_of(): call(gradient_kernel, (n_half,), [pl.BlockSpec((gblock, scn_dev), lambda...  27.8 us
    pallas_call x1, Pallas kernels, on_device(): call(first_losses_kernel, (n_obl,), [whole((obl_dev, fdim + 128)), pl.Blo...  23.7 us
    pallas_call x2, Pallas kernels, on_device(): call(functools.partial(tail_kernel, tail_scale), (n_obl,), [pay_spec, who...  21.7 us
    pallas_call x1, Pallas kernels, on_device(): call(losses_kernel, (n_obl,), [pl.BlockSpec((obl_dev, rs), lambda i: (0,...  17.3 us
    pallas_call x2, Pallas kernels, on_device(): call(update_kernel, (n_ro,), [gspec, gspec, blk, col, blk], [blk, colt, w...  15.3 us
    pallas_call x2, Pallas kernels, on_device(): call(chunk_kernel, (n_obl // group,), [pl.BlockSpec((group, ps, mandates)...  9.02 us
  transfers between devices with their start and end apart: 8, of which 4 were waited for; matrix products, arithmetic and copies ran while one was open for 1% of the time, Pallas kernels for 4%

profile of v1, /device:TPU:0, one launch (start us, length us, event | category | flops | bytes accessed | tf_op | source)
XLA Modules:
  0.0 383.4 jit_solution(15743280222327812011)
XLA Ops:
  1.9 2.2 copy.37.lgd_ref
  9.6 7.6 %setup.1 = (f32[2048,256]{1,0:T(8,128)}, bf16[2048,256]{1,0:T(8,128)(2,1)}, bf16[256,2048]{1,0:T(8,128)(2,1)}, f32[8,256]{1,0:T(8,128)}) custom-call(f32[2048,256]{1,0:T(8,128)} %hold_ref.1, f32[2048,1]{1,0:T(8,128)} %copy.37.lgd_ref, s32[2048,1]{1,0:T(8,128)} %copy.38.sector_ref, bf16[16,256]{1,0:T(8,128)(2,1)} %convert_bitcast_fusion.allowed_ref), custom_call_target="tpu_custom_call" | custom-call | bytes 6291456 | tf_op jit(solution)/shard_map/setup/pallas_call | solution.py:245
  17.1 23.7 %first_losses.1 = (bf16[2048,4096]{1,0:T(8,128)(2,1)}, bf16[16,272,256]{2,1,0:T(8,128)(2,1)}) custom-call(bf16[2048,256]{1,0:T(8,128)(2,1)} %fusion.1.load_ref, bf16[4096,256]{1,0:T(8,128)(2,1)} %pad_maximum_fusion.fac_ref, bf16[2048,4096]{1,0:T(8,128)(2,1)} %idio_ref.1, bf16[256,2048]{1,0:T(8,128)(2,1)} %get-tuple-element.21.expot_ref, ...), custom_call_target="tpu_custom_call" | custom-call | flops 8589934592 | bytes 33554432 | tf_op jit(solution)/shard_map/first_losses/pallas_call | solution.py:261
  40.9 38.1 %all_to_all.55.pay_ref = bf16[16,272,256]{2,1,0:T(8,128)(2,1)} all-to-all(bf16[16,272,256]{2,1,0:T(8,128)(2,1)} %get-tuple-element.24), channel_id=1, replica_groups=mesh['y'=4,'z'=4,'x'=4,'c'=2] {'y','z'}, dimensions={0} | all-to-all | bytes 4456448 | tf_op jit(solution)/shard_map/all_to_all | solution.py:293
  79.0 4.5 %chunk.2 = bf16[16,272,256]{2,1,0:T(8,128)(2,1)} custom-call(bf16[16,272,256]{2,1,0:T(8,128)(2,1)} %all_to_all.55.pay_ref), custom_call_target="tpu_custom_call" | custom-call | bytes 4456448 | tf_op jit(solution)/shard_map/chunk/pallas_call | solution.py:295
  83.5 32.2 %all_to_all.56.pay_ref = bf16[16,272,256]{2,1,0:T(8,128)(2,1)S(1)} all-to-all(bf16[16,272,256]{2,1,0:T(8,128)(2,1)} %chunk.2), channel_id=1, replica_groups=mesh['y'=4,'z'=4,'x'=4,'c'=2] {'y','z'}, dimensions={0} | all-to-all | bytes 4456448 | tf_op jit(solution)/shard_map/all_to_all | solution.py:305
  116.6 4.3 %all-to-all-start.2 = ((f32[8,2,256]{2,1,0:T(2,128)}), f32[8,2,256]{2,1,0:T(2,128)S(1)}, u32[]{:S(2)}, u32[]{:S(2)}) async-start(f32[8,2,256]{2,1,0:T(2,128)} %broadcast_in_dim.29), calls=%async_computation.2 | async-start | bytes 32768 | tf_op jit(solution)/shard_map/all_to_all | solution.py:313
  121.0 5.3 %all-to-all-done.2 = f32[8,2,256]{2,1,0:T(2,128)S(1)} async-done(((f32[8,2,256]{2,1,0:T(2,128)}), f32[8,2,256]{2,1,0:T(2,128)S(1)}, u32[]{:S(2)}, u32[]{:S(2)}) %all-to-all-start.2) | async-done | bytes 16416 | tf_op jit(solution)/shard_map/all_to_all | solution.py:313
  127.1 10.8 %tail.2 = (bf16[4096,256]{1,0:T(8,128)(2,1)}, f32[8,256]{1,0:T(8,128)}) custom-call(bf16[16,272,256]{2,1,0:T(8,128)(2,1)} %copy-done, f32[8,256]{1,0:T(8,128)} %maximum_maximum_fusion.stat_ref), custom_call_target="tpu_custom_call" | custom-call | bytes 4194304 | tf_op jit(solution)/shard_map/tail/pallas_call | solution.py:322
  137.9 7.0 %gradient.5 = f32[1024,256]{1,0:T(8,128)} custom-call(s32[1]{0:T(128)S(6)} %sub.67.half_ref, bf16[2048,4096]{1,0:T(8,128)(2,1)} %get-tuple-element.23.p_ref, bf16[4096,256]{1,0:T(8,128)(2,1)} %get-tuple-element.25.weight_ref), custom_call_target="tpu_custom_call" | custom-call | flops 2147483648 | bytes 8388608 | tf_op jit(solution)/shard_map/gradient/pallas_call | solution.py:335
  145.4 6.9 %gradient.4.own_ref = f32[1024,256]{1,0:T(8,128)} custom-call(s32[1]{0:T(128)} %bitcast.half_ref.core_ref, bf16[2048,4096]{1,0:T(8,128)(2,1)} %get-tuple-element.23.p_ref, bf16[4096,256]{1,0:T(8,128)(2,1)} %get-tuple-element.25.weight_ref), custom_call_target="tpu_custom_call" | custom-call | flops 2147483648 | bytes 8388608 | tf_op jit(solution)/shard_map/gradient/pallas_call | solution.py:335
  153.9 3.6 pair.2
  157.5 14.6 %all_to_all.57.pay_ref = bf16[4,272,256]{2,1,0:T(8,128)(2,1)} all-to-all(bf16[4,272,256]{2,1,0:T(8,128)(2,1)} %pair.2), channel_id=1, replica_groups=mesh['y'=4,'z'=4,'x'=4,'c'=2] {'x'}, dimensions={0} | all-to-all | bytes 1114112 | tf_op jit(solution)/shard_map/all_to_all | solution.py:365
  172.1 2.2 whole.2
  174.3 12.9 %all_to_all.58.own_ref = bf16[4,272,256]{2,1,0:T(8,128)(2,1)S(1)} all-to-all(bf16[4,272,256]{2,1,0:T(8,128)(2,1)} %get-tuple-element.27), channel_id=1, replica_groups=mesh['y'=4,'z'=4,'x'=4,'c'=2] {'x'}, dimensions={0} | all-to-all | bytes 1114112 | tf_op jit(solution)/shard_map/all_to_all | solution.py:376
  190.0 7.6 %update.2 = (f32[2048,256]{1,0:T(8,128)}, bf16[256,2048]{1,0:T(8,128)(2,1)}, f32[8,256]{1,0:T(8,128)}) custom-call(s32[1]{0:T(128)} %bitcast.half_ref.core_ref, bf16[4,272,256]{2,1,0:T(8,128)(2,1)} %copy-done.3, bf16[4,272,256]{2,1,0:T(8,128)(2,1)} %copy-done.8, f32[2048,256]{1,0:T(8,128)} %get-tuple-element.28.prev_ref, f32[2048,1]{1,0:T(8,128)} %copy.37.lgd_ref, ...), custom_call_target="tpu_custom_call" | custom-call | bytes 7340032 | tf_op jit(solution)/shard_map/update/pallas_call | solution.py:379
  197.6 17.3 %losses.1 = bf16[16,272,256]{2,1,0:T(8,128)(2,1)} custom-call(bf16[2048,4096]{1,0:T(8,128)(2,1)} %get-tuple-element.23.p_ref, bf16[256,2048]{1,0:T(8,128)(2,1)} %get-tuple-element.30.expot_ref, f32[8,256]{1,0:T(8,128)} %get-tuple-element.31.tot_ref), custom_call_target="tpu_custom_call" | custom-call | flops 4294967296 | bytes 16777216 | tf_op jit(solution)/shard_map/losses/pallas_call | solution.py:279
  214.9 34.6 %all_to_all.59.pay_ref = bf16[16,272,256]{2,1,0:T(8,128)(2,1)} all-to-all(bf16[16,272,256]{2,1,0:T(8,128)(2,1)} %losses.1), channel_id=1, replica_groups=mesh['y'=4,'z'=4,'x'=4,'c'=2] {'y','z'}, dimensions={0} | all-to-all | bytes 4456448 | tf_op jit(solution)/shard_map/all_to_all | solution.py:293
  249.5 4.5 %chunk.3 = bf16[16,272,256]{2,1,0:T(8,128)(2,1)} custom-call(bf16[16,272,256]{2,1,0:T(8,128)(2,1)} %all_to_all.59.pay_ref), custom_call_target="tpu_custom_call" | custom-call | bytes 4456448 | tf_op jit(solution)/shard_map/chunk/pallas_call | solution.py:295
  254.0 32.8 %all_to_all.60.pay_ref = bf16[16,272,256]{2,1,0:T(8,128)(2,1)S(1)} all-to-all(bf16[16,272,256]{2,1,0:T(8,128)(2,1)} %chunk.3), channel_id=1, replica_groups=mesh['y'=4,'z'=4,'x'=4,'c'=2] {'y','z'}, dimensions={0} | all-to-all | bytes 4456448 | tf_op jit(solution)/shard_map/all_to_all | solution.py:305
  287.0 7.7 %all_to_all.61 = f32[8,2,256]{2,1,0:T(2,128)S(1)} all-to-all(f32[8,2,256]{2,1,0:T(2,128)S(1)} %broadcast_in_dim.52), channel_id=1, replica_groups=mesh['y'=4,'z'=4,'x'=4,'c'=2] {'x','c'}, dimensions={0} | all-to-all | bytes 32768 | tf_op jit(solution)/shard_map/all_to_all | solution.py:313
  295.5 10.8 %tail.3 = (bf16[4096,256]{1,0:T(8,128)(2,1)}, f32[8,256]{1,0:T(8,128)}) custom-call(bf16[16,272,256]{2,1,0:T(8,128)(2,1)} %copy-done.1, f32[8,256]{1,0:T(8,128)} %maximum_maximum_fusion.1.stat_ref), custom_call_target="tpu_custom_call" | custom-call | bytes 4194304 | tf_op jit(solution)/shard_map/tail/pallas_call | solution.py:322
  306.3 7.0 %gradient.7 = f32[1024,256]{1,0:T(8,128)} custom-call(s32[1]{0:T(128)S(6)} %sub.67.half_ref, bf16[2048,4096]{1,0:T(8,128)(2,1)} %get-tuple-element.23.p_ref, bf16[4096,256]{1,0:T(8,128)(2,1)} %get-tuple-element.32.weight_ref), custom_call_target="tpu_custom_call" | custom-call | flops 2147483648 | bytes 8388608 | tf_op jit(solution)/shard_map/gradient/pallas_call | solution.py:335
  313.8 6.9 %gradient.6.own_ref = f32[1024,256]{1,0:T(8,128)} custom-call(s32[1]{0:T(128)} %bitcast.half_ref.core_ref, bf16[2048,4096]{1,0:T(8,128)(2,1)} %get-tuple-element.23.p_ref, bf16[4096,256]{1,0:T(8,128)(2,1)} %get-tuple-element.32.weight_ref), custom_call_target="tpu_custom_call" | custom-call | flops 2147483648 | bytes 8388608 | tf_op jit(solution)/shard_map/gradient/pallas_call | solution.py:335
  322.4 3.6 pair.3
  326.0 14.6 %all_to_all.62.pay_ref = bf16[4,272,256]{2,1,0:T(8,128)(2,1)} all-to-all(bf16[4,272,256]{2,1,0:T(8,128)(2,1)} %pair.3), channel_id=1, replica_groups=mesh['y'=4,'z'=4,'x'=4,'c'=2] {'x'}, dimensions={0} | all-to-all | bytes 1114112 | tf_op jit(solution)/shard_map/all_to_all | solution.py:365
  340.6 2.2 whole.3
  342.8 12.9 %all_to_all.63.own_ref = bf16[4,272,256]{2,1,0:T(8,128)(2,1)S(1)} all-to-all(bf16[4,272,256]{2,1,0:T(8,128)(2,1)} %get-tuple-element.34), channel_id=1, replica_groups=mesh['y'=4,'z'=4,'x'=4,'c'=2] {'x'}, dimensions={0} | all-to-all | bytes 1114112 | tf_op jit(solution)/shard_map/all_to_all | solution.py:376
  358.5 7.6 %update.3 = (f32[2048,256]{1,0:T(8,128)}, bf16[256,2048]{1,0:T(8,128)(2,1)}, f32[8,256]{1,0:T(8,128)}) custom-call(s32[1]{0:T(128)} %bitcast.half_ref.core_ref, bf16[4,272,256]{2,1,0:T(8,128)(2,1)} %copy-done.2, bf16[4,272,256]{2,1,0:T(8,128)(2,1)} %copy-done.7, f32[2048,256]{1,0:T(8,128)} %get-tuple-element.35.prev_ref, f32[2048,1]{1,0:T(8,128)} %copy.37.lgd_ref, ...), custom_call_target="tpu_custom_call" | custom-call | bytes 7340032 | tf_op jit(solution)/shard_map/update/pallas_call | solution.py:379
  367.5 3.6 all-to-all-start.10
  372.4 6.6 %all-to-all-done.10 = f32[16,8,256]{2,1,0:T(8,128)S(1)} async-done(((f32[16,8,256]{2,1,0:T(8,128)}), f32[16,8,256]{2,1,0:T(8,128)S(1)}, u32[]{:S(2)}, u32[]{:S(2)}) %all-to-all-start.10) | async-done | bytes 131104 | tf_op jit(solution)/shard_map/all_to_all | solution.py:390
  379.6 3.8 scale.1
  (86 shorter events, 22.4 us)
Async XLA Ops:
  0.6 5.5 %copy-start.10 = (s32[256,16]{0,1:T(8,128)S(1)}, s32[256,16]{0,1:T(8,128)}, u32[]{:S(2)}) copy-start(s32[256,16]{0,1:T(8,128)} %param.16) | copy-start | bytes 49156
  0.6 6.1 %copy-start.9 = (bf16[2048,128]{1,0:T(8,128)(2,1)S(1)}, bf16[2048,128]{1,0:T(8,128)(2,1)}, u32[]{:S(2)}) copy-start(bf16[2048,128]{1,0:T(8,128)(2,1)} %param.11) | copy-start | bytes 1572868
  1.9 6.0 %copy-start.4 = (bf16[4096,128]{1,0:T(8,128)(2,1)S(1)}, bf16[4096,128]{1,0:T(8,128)(2,1)}, u32[]{:S(2)}) copy-start(bf16[4096,128]{1,0:T(8,128)(2,1)} %param.9) | copy-start | bytes 3145732
  115.7 11.4 %copy-start = (bf16[16,272,256]{2,1,0:T(8,128)(2,1)}, bf16[16,272,256]{2,1,0:T(8,128)(2,1)S(1)}, u32[]{:S(2)}) copy-start(bf16[16,272,256]{2,1,0:T(8,128)(2,1)S(1)} %all_to_all.56.pay_ref) | copy-start | bytes 6684676
  116.6 9.7 %all-to-all-start.2 = ((f32[8,2,256]{2,1,0:T(2,128)}), f32[8,2,256]{2,1,0:T(2,128)S(1)}, u32[]{:S(2)}, u32[]{:S(2)}) async-start(f32[8,2,256]{2,1,0:T(2,128)} %broadcast_in_dim.29), calls=%async_computation.2 | async-start | bytes 32768 | tf_op jit(solution)/shard_map/all_to_all | solution.py:313
  137.9 7.0 %copy-start.12 = (f32[8,256]{1,0:T(8,128)S(1)}, f32[8,256]{1,0:T(8,128)}, u32[]{:S(2)}) copy-start(f32[8,256]{1,0:T(8,128)} %get-tuple-element.26.soft_ref) | copy-start | bytes 24580
  144.9 7.5 %collective-permute-start = (f32[1024,256]{1,0:T(8,128)}, f32[1024,256]{1,0:T(8,128)S(1)}, u32[]{:S(2)}, u32[]{:S(2)}) collective-permute-start(f32[1024,256]{1,0:T(8,128)} %gradient.5), channel_id=1, source_target_pairs={{0,1},{1,0},{2,3},{3,2},{4,5},{5,4},{6,7},{7,6},{8,9},{9,8},{10,11... | collective-permute-start | bytes 3145736 | tf_op jit(solution)/shard_map/ppermute | solution.py:351
  144.9 7.4 %collective-permute-start.1 = (f32[8,256]{1,0:T(8,128)S(1)}, f32[8,256]{1,0:T(8,128)S(1)}, u32[]{:S(2)}, u32[]{:S(2)}) collective-permute-start(f32[8,256]{1,0:T(8,128)S(1)} %copy-done.12), channel_id=1, source_target_pairs={{0,1},{1,0},{2,3},{3,2},{4,5},{5,4},{6,7},{7,6},{8,9},{9,8},{10,11... | collective-permute-start | bytes 24584 | tf_op jit(solution)/shard_map/ppermute | solution.py:352
  152.3 0.6 copy-start.14
  152.9 1.0 copy-start.6
  187.2 2.0 copy-start.3
  187.2 2.0 collective-permute-start.2
  189.2 0.8 copy-start.8
  286.8 8.7 %copy-start.1 = (bf16[16,272,256]{2,1,0:T(8,128)(2,1)}, bf16[16,272,256]{2,1,0:T(8,128)(2,1)S(1)}, u32[]{:S(2)}) copy-start(bf16[16,272,256]{2,1,0:T(8,128)(2,1)S(1)} %all_to_all.60.pay_ref) | copy-start | bytes 6684676
  306.3 7.0 %copy-start.11 = (f32[8,256]{1,0:T(8,128)S(1)}, f32[8,256]{1,0:T(8,128)}, u32[]{:S(2)}) copy-start(f32[8,256]{1,0:T(8,128)} %get-tuple-element.33.soft_ref) | copy-start | bytes 24580
  313.3 7.5 %collective-permute-start.3 = (f32[1024,256]{1,0:T(8,128)}, f32[1024,256]{1,0:T(8,128)S(1)}, u32[]{:S(2)}, u32[]{:S(2)}) collective-permute-start(f32[1024,256]{1,0:T(8,128)} %gradient.7), channel_id=1, source_target_pairs={{0,1},{1,0},{2,3},{3,2},{4,5},{5,4},{6,7},{7,6},{8,9},{9,8},{10,11... | collective-permute-start | bytes 3145736 | tf_op jit(solution)/shard_map/ppermute | solution.py:351
  313.3 7.4 %collective-permute-start.4 = (f32[8,256]{1,0:T(8,128)S(1)}, f32[8,256]{1,0:T(8,128)S(1)}, u32[]{:S(2)}, u32[]{:S(2)}) collective-permute-start(f32[8,256]{1,0:T(8,128)S(1)} %copy-done.11), channel_id=1, source_target_pairs={{0,1},{1,0},{2,3},{3,2},{4,5},{5,4},{6,7},{7,6},{8,9},{9,8},{10,11... | collective-permute-start | bytes 24584 | tf_op jit(solution)/shard_map/ppermute | solution.py:352
  320.7 0.6 copy-start.13
  321.3 1.0 copy-start.5
  355.7 2.0 copy-start.2
  355.7 2.0 collective-permute-start.5
  357.7 0.8 copy-start.7
  367.5 11.5 %all-to-all-start.10 = ((f32[16,8,256]{2,1,0:T(8,128)}), f32[16,8,256]{2,1,0:T(8,128)S(1)}, u32[]{:S(2)}, u32[]{:S(2)}) async-start(f32[16,8,256]{2,1,0:T(8,128)} %broadcast_in_dim.53), calls=%async_computation.10 | async-start | bytes 262144 | tf_op jit(solution)/shard_map/all_to_all | solution.py:390

commit v2 on v1

--- a/solution.py
+++ b/solution.py
@@ -33,7 +33,7 @@
         kernel,
         grid_spec=spec,
         out_shape=out_shape,
-        compiler_params=pltpu.CompilerParams(vmem_limit_bytes=56 * 1024 * 1024),
+        compiler_params=pltpu.CompilerParams(vmem_limit_bytes=24 * 1024 * 1024),
         cost_estimate=pl.CostEstimate(flops=int(flops), bytes_accessed=int(nbytes), transcendentals=0),
         interpret=INTERPRET,
         name=name,
@@ -71,13 +71,26 @@
     return (base + 0.5 * span) + jnp.log(code.astype(f32)) * (span * (1.0 / SPAN))
 
 
-def setup_kernel(hold_ref, lgd_ref, sector_ref, allowed_ref, weighted_ref, elig_ref, expot_ref, tot_ref):
-    hot = (sector_ref[...] == lax.broadcasted_iota(jnp.int32, (1, allowed_ref.shape[0]), 1)).astype(bf16)
-    elig = jnp.dot(hot, allowed_ref[...], preferred_element_type=f32)
-    weighted = elig * hold_ref[...]
-    weighted_ref[...] = weighted
-    elig_ref[...] = elig.astype(bf16)
-    expot_ref[...] = jnp.transpose(weighted * lgd_ref[...]).astype(bf16)
+def setup_kernel(hold_ref, lgd_ref, sector_ref, rating_ref, allowed_ref, load_ref, weighted_ref, lge_ref, aug_ref, expot_ref, tot_ref):
+    rows = sector_ref.shape[1]
+    sectors = allowed_ref.shape[1]
+    here = pl.ds(pl.multiple_of(pl.program_id(0) * rows, rows), rows)
+    allowed = allowed_ref[...].astype(f32)
+    hot = (lax.broadcasted_iota(jnp.int32, (sectors, rows), 0) == sector_ref[...]).astype(f32)
+    lgd = lgd_ref[...]
+    parts = jnp.concatenate([hot * part for part in split3(lgd)], axis=0)
+    dims = (((0,), (1,)), ((), ()))
+    elig = lax.dot_general(hot.astype(bf16), allowed.astype(bf16), dims, preferred_element_type=f32)
+    thrice = jnp.concatenate([allowed] * 3, axis=1)
+    lge = lax.dot_general(parts.astype(bf16), thrice.astype(bf16), dims, preferred_element_type=f32)
+    hold = hold_ref[...]
+    weighted = elig * hold
+    weighted_ref[here] = weighted
+    lge_ref[here] = lge
+    expot_ref[:, here] = jnp.transpose(lge * hold).astype(bf16)
+    lane = lax.broadcasted_iota(jnp.int32, (128, rows), 0)
+    rated = ((lane % 16 == rating_ref[...]) & (lane < 48)).astype(f32)
+    aug_ref[here] = jnp.concatenate([load_ref[...], jnp.transpose(rated).astype(bf16)], axis=1)
 
     @pl.when(pl.program_id(0) == 0)
     def _():
@@ -86,29 +99,31 @@
     tot_ref[0:1] += jnp.sum(weighted, axis=0, keepdims=True)
 
 
-def first_losses_kernel(load_ref, fac_ref, idio_ref, expot_ref, tot_ref, p_ref, pay_ref, acc_ref):
-    rows = fac_ref.shape[0]
+def put_chunks(losses, tot_ref, pay_ref):
+    rows = pay_ref.shape[1] - HEAD
+    for k in range(pay_ref.shape[0]):
+        code, head = encode(jnp.transpose(losses[:, k * rows : (k + 1) * rows]), [tot_ref[0:1]])
+        pay_ref[k, 0:rows] = code
+        pay_ref[k, rows : rows + HEAD] = head
+
+
+def first_losses_kernel(load_ref, fac_ref, bar_ref, idio_ref, expot_ref, tot_ref, p_ref, pay_ref):
+    wide = fac_ref.shape[0]
+    cols = pl.ds(pl.multiple_of(pl.program_id(0) * wide, wide), wide)
     block = min(256, load_ref.shape[0])
-    acc_ref[...] = jnp.zeros_like(acc_ref)
+    fac = jnp.concatenate([fac_ref[...], jnp.broadcast_to(bar_ref[...], (wide, 128))], axis=1)
     for i in range(load_ref.shape[0] // block):
         sl = slice(i * block, (i + 1) * block)
-        systematic = lax.dot_general(
-            load_ref[sl], fac_ref[...], (((1,), (1,)), ((), ())), preferred_element_type=f32
-        )
-        prob = (0.5 * jnp.tanh(systematic + IDIO_SCALE * idio_ref[sl].astype(f32)) + 0.5).astype(bf16)
-        p_ref[sl] = prob
-        acc_ref[...] += jnp.dot(expot_ref[:, sl], prob, preferred_element_type=f32)
-    code, head = encode(jnp.transpose(acc_ref[...]), [tot_ref[0:1]])
-    pay_ref[0, 0:rows] = code
-    pay_ref[0, rows : rows + HEAD] = head
+        latent = lax.dot_general(load_ref[sl], fac, (((1,), (1,)), ((), ())), preferred_element_type=f32)
+        prob = 0.5 * jnp.tanh(latent + IDIO_SCALE * idio_ref[sl].astype(f32)) + 0.5
+        p_ref[sl, cols] = prob.astype(bf16)
+    put_chunks(jnp.dot(expot_ref[...], p_ref[:, cols], preferred_element_type=f32), tot_ref, pay_ref)
 
 
 def losses_kernel(p_ref, expot_ref, tot_ref, pay_ref):
-    rows = p_ref.shape[1]
-    losses = jnp.dot(expot_ref[...], p_ref[...], preferred_element_type=f32)
-    code, head = encode(jnp.transpose(losses), [tot_ref[0:1]])
-    pay_ref[0, 0:rows] = code
-    pay_ref[0, rows : rows + HEAD] = head
+    wide = pay_ref.shape[0] * (pay_ref.shape[1] - HEAD)
+    cols = pl.ds(pl.multiple_of(pl.program_id(0) * wide, wide), wide)
+    put_chunks(jnp.dot(expot_ref[...], p_ref[:, cols], preferred_element_type=f32), tot_ref, pay_ref)
 
 
 def chunk_kernel(pay_ref, out_ref, acc_ref, tot_ref):
@@ -142,27 +157,41 @@
 
 
 def tail_kernel(tail_scale, pay_ref, stat_ref, weight_ref, soft_ref):
-    rows = weight_ref.shape[0]
-    head = pay_ref[0, rows : rows + HEAD].astype(f32)
-    losses = decode(pay_ref[0, 0:rows], head)
-    scaled = (losses - stat_ref[0:1]) * stat_ref[1:2]
-    weight_ref[...] = (tail_scale / (1.0 + jnp.exp(-scaled))).astype(bf16)
-    soft = jnp.maximum(scaled, 0.0) + jnp.log(1.0 + jnp.exp(-jnp.abs(scaled)))
-
-    @pl.when(pl.program_id(0) == 0)
+    count, rows = pay_ref.shape[0], pay_ref.shape[1] - HEAD
+    step = pl.program_id(0)
+
+    @pl.when(step == 0)
     def _():
         soft_ref[...] = jnp.zeros_like(soft_ref)
 
-    soft_ref[0:1] += jnp.sum(soft, axis=0, keepdims=True)
+    for k in range(count):
+        head = pay_ref[k, rows : rows + HEAD].astype(f32)
+        losses = decode(pay_ref[k, 0:rows], head)
+        scaled = (losses - stat_ref[0:1]) * stat_ref[1:2]
+        small = jnp.exp(-jnp.abs(scaled))
+        grown = 1.0 + small
+        sigmoid = jnp.where(scaled >= 0.0, tail_scale, tail_scale * small) / grown
+        at = pl.multiple_of((step * count + k) * rows, rows)
+        weight_ref[pl.ds(at, rows)] = sigmoid.astype(bf16)
+        up = jnp.maximum(scaled, 0.0).reshape(rows // 8, 8, -1).sum(axis=0)
+        tile = grown.reshape(rows // 8, 8, -1)
+        for _ in range(5):
+            if tile.shape[0] % 2 == 0:
+                tile = tile[: tile.shape[0] // 2] * tile[tile.shape[0] // 2 :]
+        soft_ref[...] += up + jnp.log(tile).sum(axis=0)
 
 
 def gradient_kernel(half_ref, p_ref, weight_ref, out_ref):
-    out_ref[...] = jnp.dot(p_ref[...], weight_ref[...], preferred_element_type=f32)
+    rows = out_ref.shape[0]
+    at = (half_ref[0] * pl.num_programs(0) + pl.program_id(0)) * rows
+    out_ref[...] = jnp.dot(
+        p_ref[pl.ds(pl.multiple_of(at, rows), rows)], weight_ref[...], preferred_element_type=f32
+    )
 
 
 def pair_kernel(own_ref, other_ref, soft_ref, soft_other_ref, pay_ref):
     rows = own_ref.shape[0]
-    code, head = encode(own_ref[...] + other_ref[...], [soft_ref[0:1] + soft_other_ref[0:1]])
+    code, head = encode(own_ref[...] + other_ref[...], [jnp.sum(soft_ref[...] + soft_other_ref[...], axis=0, keepdims=True)])
     pay_ref[0, 0:rows] = code
     pay_ref[0, rows : rows + HEAD] = head
 
@@ -182,16 +211,17 @@
         out_ref[k, rows : rows + HEAD] = head
 
 
-def update_kernel(core_ref, own_ref, other_ref, prev_ref, lgd_ref, elig_ref, unnorm_ref, expot_ref, tot_ref):
-    rows = prev_ref.shape[0]
+def update_kernel(core_ref, own_ref, other_ref, prev_ref, lge_ref, unnorm_ref, expot_ref, tot_ref):
+    rows = own_ref.shape[1] - HEAD
     step = pl.program_id(0)
+    here = pl.ds(pl.multiple_of(step * rows, rows), rows)
     mine = (step // (pl.num_programs(0) // 2)) == core_ref[0]
     pay = jnp.where(mine, own_ref[0], other_ref[0])
     gradient = decode(pay[0:rows], pay[rows : rows + HEAD].astype(f32))
-    gradient = lgd_ref[...] * elig_ref[...].astype(f32) * gradient
-    unnorm = prev_ref[...] * jnp.exp(-STEP_RATE * gradient)
-    unnorm_ref[...] = unnorm
-    expot_ref[...] = jnp.transpose(unnorm * lgd_ref[...]).astype(bf16)
+    lge = lge_ref[here]
+    unnorm = prev_ref[here] * jnp.exp(lge * (-STEP_RATE * gradient))
+    unnorm_ref[here] = unnorm
+    expot_ref[:, here] = jnp.transpose(unnorm * lge).astype(bf16)
 
     @pl.when(step == 0)
     def _():
@@ -200,8 +230,38 @@
     tot_ref[0:1] += jnp.sum(unnorm, axis=0, keepdims=True)
 
 
+def last_update_kernel(core_ref, own_ref, other_ref, prev_ref, lge_ref, unnorm_ref, tot_ref):
+    rows = own_ref.shape[1] - HEAD
+    step = pl.program_id(0)
+    here = pl.ds(pl.multiple_of(step * rows, rows), rows)
+    mine = (step // (pl.num_programs(0) // 2)) == core_ref[0]
+    pay = jnp.where(mine, own_ref[0], other_ref[0])
+    gradient = decode(pay[0:rows], pay[rows : rows + HEAD].astype(f32))
+    unnorm = prev_ref[here] * jnp.exp(lge_ref[here] * (-STEP_RATE * gradient))
+    unnorm_ref[here] = unnorm
+
+    @pl.when(step == 0)
+    def _():
+        tot_ref[...] = jnp.zeros_like(tot_ref)
+
+    tot_ref[0:1] += jnp.sum(unnorm, axis=0, keepdims=True)
+
+
 def scale_kernel(unnorm_ref, tot_ref, out_ref):
-    out_ref[...] = unnorm_ref[...] * tot_ref[0:1]
+    rows = out_ref.shape[0]
+    here = pl.ds(pl.multiple_of(pl.program_id(0) * rows, rows), rows)
+    out_ref[...] = unnorm_ref[here] * tot_ref[0:1]
+
+
+VMEM = pl.BlockSpec(memory_space=pltpu.VMEM)
+
+
+def near(array):
+    return array if INTERPRET else pltpu.with_memory_space_constraint(array, pltpu.VMEM)
+
+
+def near_shape(shape, dtype):
+    return jax.ShapeDtypeStruct(shape, dtype) if INTERPRET else pltpu.VMEM(shape, dtype)
 
 
 def whole(shape):
@@ -224,72 +284,71 @@
     ps, po = rs + HEAD, ro + HEAD
     half = obl_dev // n_c
     core = lax.axis_index("c").astype(jnp.int32).reshape(1)
-    lgd = loss_given[:, None]
     row8 = sds((8, mandates), f32)
-
-    hot = rating[:, None] == jnp.arange(barrier.shape[0])[None, :]
-    bar = jnp.sum(jnp.where(hot, barrier[None, :], 0.0), axis=1)
-    bar_a = rounded(bar)
-    bar_b = rounded(bar - bar_a)
-    bar_c = bar - bar_a - bar_b
-    parts = -jnp.stack([bar_a, bar_b, bar_c], axis=1)
+    ratings = barrier.shape[0]
+    bar_a = rounded(barrier)
+    bar_b = rounded(barrier - bar_a)
+    bar_c = barrier - bar_a - bar_b
+    bars = -jnp.concatenate([bar_a, bar_b, bar_c])
+    bars = jnp.pad(bars, (0, 128 - 3 * ratings)).astype(bf16)[None, :]
     fdim = factors.shape[1]
-    load_aug = jnp.concatenate([loadings, jnp.pad(parts, ((0, 0), (0, 125))).astype(bf16)], axis=1)
-    ones = (jnp.arange(128) < 3).astype(bf16)
-    fac_aug = jnp.concatenate([factors, jnp.broadcast_to(ones, (scn_dev, 128))], axis=1)
 
     blk = pl.BlockSpec((ro, mandates), lambda i, *_: (i, 0))
-    col = pl.BlockSpec((ro, 1), lambda i, *_: (i, 0))
-    colt = pl.BlockSpec((mandates, ro), lambda i, *_: (0, i))
+    line = pl.BlockSpec((1, ro), lambda i, *_: (0, i))
     n_ro = obl_dev // ro
-    prev, elig, expot, tot = call(
+    prev, lge, aug, expot, tot = call(
         setup_kernel,
         (n_ro,),
-        [blk, col, col, whole((allowed.shape[1], mandates))],
-        [blk, blk, colt, whole((8, mandates))],
-        [sds((obl_dev, mandates), f32), sds((obl_dev, mandates), bf16), sds((mandates, obl_dev), bf16), row8],
+        [blk, line, line, line, whole(allowed.shape), pl.BlockSpec((ro, fdim), lambda i: (i, 0))],
+        [VMEM, VMEM, VMEM, VMEM, whole((8, mandates))],
+        [
+            near_shape((obl_dev, mandates), f32),
+            near_shape((obl_dev, mandates), f32),
+            near_shape((obl_dev, fdim + 128), bf16),
+            near_shape((mandates, obl_dev), bf16),
+            row8,
+        ],
         nbytes=obl_dev * mandates * 12,
         name="setup",
-    )(holdings, lgd, sector[:, None], allowed.T.astype(bf16))
+    )(holdings, loss_given[None, :], sector[None, :], rating[None, :], allowed, loadings)
+    lge = near(lge)
 
     results = []
     prob = None
     for iteration in range(STEPS):
         pay_shape = sds((n_obl, ps, mandates), bf16)
         pay_spec = pl.BlockSpec((1, ps, mandates), lambda i, *_: (i, 0, 0))
+        pair_spec = pl.BlockSpec((2, ps, mandates), lambda i, *_: (i, 0, 0))
         if iteration == 0:
             prob, pay = call(
                 first_losses_kernel,
-                (n_obl,),
+                (n_obl // 2,),
                 [
-                    whole((obl_dev, fdim + 128)),
-                    pl.BlockSpec((rs, fdim + 128), lambda i: (i, 0)),
-                    pl.BlockSpec((obl_dev, rs), lambda i: (0, i)),
-                    whole((mandates, obl_dev)),
+                    VMEM,
+                    pl.BlockSpec((2 * rs, fdim), lambda i: (i, 0)),
+                    whole((1, 128)),
+                    pl.BlockSpec((obl_dev, 2 * rs), lambda i: (0, i)),
+                    VMEM,
                     whole((8, mandates)),
                 ],
-                [pl.BlockSpec((obl_dev, rs), lambda i: (0, i)), pay_spec],
-                [sds((obl_dev, scn_dev), bf16), pay_shape],
-                scratch=[pltpu.VMEM((mandates, rs), f32)],
+                [VMEM, pair_spec],
+                [near_shape((obl_dev, scn_dev), bf16), pay_shape],
                 flops=4 * obl_dev * scn_dev * mandates,
                 nbytes=obl_dev * scn_dev * 4,
                 name="first_losses",
-            )(load_aug, fac_aug, idiosyncratic, expot, tot)
+            )(near(aug), factors, bars, idiosyncratic, near(expot), tot)
+            prob = near(prob)
         else:
             pay = call(
                 losses_kernel,
-                (n_obl,),
-                [
-                    pl.BlockSpec((obl_dev, rs), lambda i: (0, i)),
-                    whole((mandates, obl_dev)),
-                    whole((8, mandates)),
-                ],
-                pay_spec,
+                (n_obl // 2,),
+                [VMEM, VMEM, whole((8, mandates))],
+                pair_spec,
                 pay_shape,
                 flops=2 * obl_dev * scn_dev * mandates,
                 nbytes=obl_dev * scn_dev * 2,
                 name="losses",
-            )(prob, expot, tot)
+            )(prob, near(expot), tot)
         pay = lax.all_to_all(pay, OBL, 0, 0, tiled=True)
         group = max(1, n_obl // 4)
         pay = call(
@@ -321,24 +380,21 @@
 
         weight, soft = call(
             functools.partial(tail_kernel, tail_scale),
-            (n_obl,),
-            [pay_spec, whole((8, mandates))],
-            [pl.BlockSpec((rs, mandates), lambda i: (i, 0)), whole((8, mandates))],
-            [sds((scn_dev, mandates), bf16), row8],
+            (n_obl // 4,),
+            [pl.BlockSpec((4, ps, mandates), lambda i: (i, 0, 0)), whole((8, mandates))],
+            [VMEM, whole((8, mandates))],
+            [near_shape((scn_dev, mandates), bf16), row8],
             nbytes=scn_dev * mandates * 4,
             name="tail",
         )(pay, stat)
-        gblock = min(256, half)
-        n_half = half // gblock
+        weight = near(weight)
+        gblock = min(512, half)
 
         def gradient_of(which):
             return call(
                 gradient_kernel,
-                (n_half,),
-                [
-                    pl.BlockSpec((gblock, scn_dev), lambda i, h: (h[0] * n_half + i, 0)),
-                    whole((scn_dev, mandates)),
-                ],
+                (half // gblock,),
+                [VMEM, VMEM],
                 pl.BlockSpec((gblock, mandates), lambda i, h: (i, 0)),
                 sds((half, mandates), f32),
                 prefetch=1,
@@ -376,28 +432,32 @@
         pay = lax.all_to_all(pay, "x", 0, 0, tiled=True)
         other = lax.ppermute(pay, "c", swap)
         gspec = pl.BlockSpec((1, po, mandates), lambda i, *_: (i % n_x, 0, 0))
-        prev, expot, tot = call(
-            update_kernel,
+        last = iteration == STEPS - 1
+        outs = call(
+            last_update_kernel if last else update_kernel,
             (n_ro,),
-            [gspec, gspec, blk, col, blk],
-            [blk, colt, whole((8, mandates))],
-            [sds((obl_dev, mandates), f32), sds((mandates, obl_dev), bf16), row8],
+            [gspec, gspec, VMEM, VMEM],
+            [VMEM] + [VMEM] * (not last) + [whole((8, mandates))],
+            [near_shape((obl_dev, mandates), f32)]
+            + [near_shape((mandates, obl_dev), bf16)] * (not last)
+            + [row8],
             prefetch=1,
             nbytes=obl_dev * mandates * 14,
             name="update",
-        )(core, pay, other, prev, lgd, elig)
+        )(core, pay, other, near(prev), lge)
+        prev, expot, tot = outs[0], outs[-2], outs[-1]
 
     totals = lax.all_to_all(jnp.broadcast_to(tot[None], (n_obl, 8, mandates)), OBL, 0, 0, tiled=True)
     factor = obligors / jnp.sum(totals, axis=0)
     positions = call(
         scale_kernel,
         (max(1, obl_dev // 512),),
-        [pl.BlockSpec((min(512, obl_dev), mandates), lambda i: (i, 0)), whole((8, mandates))],
+        [VMEM, whole((8, mandates))],
         pl.BlockSpec((min(512, obl_dev), mandates), lambda i: (i, 0)),
         sds((obl_dev, mandates), f32),
         nbytes=obl_dev * mandates * 8,
         name="scale",
-    )(prev, factor)
+    )(near(prev), factor)
     return (positions, jnp.stack(results))
 
 

time: 387 us -> 297 us (0.77)
  Pallas kernels: 138 us -> 54.4 us
  local copies, waits for them, and re-layouts: 11.6 us -> 21.1 us
  blocking collectives: 200 us -> 193 us
  other arithmetic: 8.74 us -> 1.98 us
    pallas_call x12, Pallas kernels: 117 us -> 50.2 us  [the longest x1 17 us: on_device(): call(first_losses_kernel, (n_obl // 2,), [VMEM, pl.BlockSpec((2 * rs, fdi...]
    unnamed x30 -> x33, local copies, waits for them, and re-layouts: 4.82 us -> 19.7 us
    pallas_call x2, Pallas kernels: 9.02 us -> 2.41 us  [on_device(): call(chunk_kernel, (n_obl // group,), [pl.BlockSpec((group, ps, mandates)...]
    pallas_call x2, Pallas kernels: 7.29 us -> 1.11 us  [on_device(): call(pair_kernel, (n_x,), [blk, blk, whole((8, mandates)), whole((8, mand...]
    all_to_all x4, blocking collectives: 55 us -> 49.8 us  [on_device(): pay = lax.all_to_all(pay, 'x', 0, 0, tiled=True)]
    broadcast_in_dim x2 -> x1, local copies, waits for them, and re-layouts: 4.22 us -> 0.01 us  [on_device(): bars = jnp.pad(bars, (0, 128 - 3 * ratings)).astype(bf16)[None, :]]
  transfers between devices with their start and end apart: 8 -> 8, of which waited for: 4 -> 4; matrix products, arithmetic and copies ran while one was open for 1% -> 0% of each run, Pallas kernels for 4% -> 2%
where the time goes in v2:
time: 297 us
  blocking collectives  193 us (65%)
  Pallas kernels  54.4 us (18%)
  local copies, waits for them, and re-layouts  21.1 us (7%)
  waiting for transfers between devices  16.4 us (6%)
  starting transfers between devices  9.06 us (3%)
    all_to_all x4, blocking collectives, on_device(): pay = lax.all_to_all(pay, OBL, 0, 0, tiled=True)  135 us
    all_to_all x4, blocking collectives, on_device(): pay = lax.all_to_all(pay, 'x', 0, 0, tiled=True)  49.8 us
    unnamed x33, local copies, waits for them, and re-layouts  19.7 us
    pallas_call x1, Pallas kernels, on_device(): call(first_losses_kernel, (n_obl // 2,), [VMEM, pl.BlockSpec((2 * rs, fdi...  17 us
    pallas_call x4, Pallas kernels, gradient_of(): call(gradient_kernel, (half // gblock,), [VMEM, VMEM], pl.BlockSpec((gblo...  10.2 us
    all_to_all x1, blocking collectives, on_device(): both = lax.all_to_all(both, SCN, 0, 0, tiled=True)  7.72 us
    pallas_call x1, Pallas kernels, on_device(): call(losses_kernel, (n_obl // 2,), [VMEM, VMEM, whole((8, mandates))], pa...  7.62 us
    all_to_all x1, waiting for transfers between devices, on_device(): lax.all_to_all(jnp.broadcast_to(tot[None], (n_obl, 8, mandates)), OBL, 0,...  7.24 us
  transfers between devices with their start and end apart: 8, of which 4 were waited for; matrix products, arithmetic and copies ran while one was open for 0% of the time, Pallas kernels for 2%

profile of v2, /device:TPU:0, one launch (start us, length us, event | category | flops | bytes accessed | tf_op | source)
XLA Modules:
  0.0 296.6 jit_solution(10697890693182171756)
XLA Ops:
  2.2 1.6 copy-done.4
  6.9 3.3 %setup.1 = (f32[2048,256]{1,0:T(8,128)S(1)}, f32[2048,256]{1,0:T(8,128)S(1)}, bf16[2048,256]{1,0:T(8,128)(2,1)S(1)}, bf16[256,2048]{1,0:T(8,128)(2,1)S(1)}, f32[8,256]{1,0:T(8,128)S(1)}) custom-call(f32[2048,256]{1,0:T(8,128)S(1)} %copy-done.4, f32[1,2048]{1,0:T(1,128)S(1)} %bitcast.40, s32[1,2048]{1,0:T(1,128)S(1)} %bitcast.41, s32[1,2048]{1,0:T(1,128)S(1)} %bitcast.42, ...), custom_call_target="tpu_custom_call" | custom-call | bytes 6291456 | tf_op jit(solution)/shard_map/setup/pallas_call | solution.py:299
  10.3 1.3 copy-done.2
  11.6 1.3 copy-done.5
  12.9 17.0 %first_losses.1 = (bf16[2048,4096]{1,0:T(8,128)(2,1)S(1)}, bf16[16,272,256]{2,1,0:T(8,128)(2,1)S(1)}) custom-call(bf16[2048,256]{1,0:T(8,128)(2,1)S(1)} %get-tuple-element.22.load_ref, bf16[4096,128]{1,0:T(8,128)(2,1)S(1)} %copy-done.11, bf16[1,128]{1,0:T(2,128)(2,1)S(1)} %pad_bitcast_fusion.bar_ref, bf16[2048,4096]{1,0:T(8,128)(2,1)} %idio_ref.1, ...), custom_call_target="tpu_custom_call" | custom-call | flops 8589934592 | bytes 33554432 | tf_op jit(solution)/shard_map/first_losses/pallas_call | solution.py:323
  30.0 5.7 %copy-done = bf16[2048,4096]{1,0:T(8,128)(2,1)} copy-done((bf16[2048,4096]{1,0:T(8,128)(2,1)}, bf16[2048,4096]{1,0:T(8,128)(2,1)S(1)}, u32[]{:S(2)}) %copy-start) | copy-done | bytes 16777240
  35.7 37.8 %all_to_all.55.pay_ref = bf16[16,272,256]{2,1,0:T(8,128)(2,1)S(1)} all-to-all(bf16[16,272,256]{2,1,0:T(8,128)(2,1)S(1)} %get-tuple-element.26), channel_id=1, replica_groups=mesh['y'=4,'z'=4,'x'=4,'c'=2] {'y','z'}, dimensions={0} | all-to-all | bytes 4456448 | tf_op jit(solution)/shard_map/all_to_all | solution.py:352
  74.7 31.9 %all_to_all.56.pay_ref = bf16[16,272,256]{2,1,0:T(8,128)(2,1)S(1)} all-to-all(bf16[16,272,256]{2,1,0:T(8,128)(2,1)S(1)} %chunk.2), channel_id=1, replica_groups=mesh['y'=4,'z'=4,'x'=4,'c'=2] {'y','z'}, dimensions={0} | all-to-all | bytes 4456448 | tf_op jit(solution)/shard_map/all_to_all | solution.py:364
  107.4 4.3 %all-to-all-start.2 = ((f32[8,2,256]{2,1,0:T(2,128)}), f32[8,2,256]{2,1,0:T(2,128)S(1)}, u32[]{:S(2)}, u32[]{:S(2)}) async-start(f32[8,2,256]{2,1,0:T(2,128)} %broadcast_in_dim.18), calls=%async_computation.2 | async-start | bytes 32768 | tf_op jit(solution)/shard_map/all_to_all | solution.py:372
  111.8 5.3 %all-to-all-done.2 = f32[8,2,256]{2,1,0:T(2,128)S(1)} async-done(((f32[8,2,256]{2,1,0:T(2,128)}), f32[8,2,256]{2,1,0:T(2,128)S(1)}, u32[]{:S(2)}, u32[]{:S(2)}) %all-to-all-start.2) | async-done | bytes 16416 | tf_op jit(solution)/shard_map/all_to_all | solution.py:372
  117.2 3.5 %tail.2 = (bf16[4096,256]{1,0:T(8,128)(2,1)S(1)}, f32[8,256]{1,0:T(8,128)S(1)}) custom-call(bf16[16,272,256]{2,1,0:T(8,128)(2,1)S(1)} %all_to_all.56.pay_ref, f32[8,256]{1,0:T(8,128)S(1)} %maximum_maximum_fusion.stat_ref), custom_call_target="tpu_custom_call" | custom-call | bytes 4194304 | tf_op jit(solution)/shard_map/tail/pallas_call | solution.py:381
  120.7 5.8 %copy-done.1 = bf16[2048,4096]{1,0:T(8,128)(2,1)S(1)} copy-done((bf16[2048,4096]{1,0:T(8,128)(2,1)S(1)}, bf16[2048,4096]{1,0:T(8,128)(2,1)}, u32[]{:S(2)}) %copy-start.1) | copy-done | bytes 16777240
  126.5 2.6 gradient.5
  129.6 2.6 gradient.4.own_ref
  132.8 13.3 %all_to_all.57.pay_ref = bf16[4,272,256]{2,1,0:T(8,128)(2,1)S(1)} all-to-all(bf16[4,272,256]{2,1,0:T(8,128)(2,1)S(1)} %pair.2), channel_id=1, replica_groups=mesh['y'=4,'z'=4,'x'=4,'c'=2] {'x'}, dimensions={0} | all-to-all | bytes 1114112 | tf_op jit(solution)/shard_map/all_to_all | solution.py:421
  146.5 11.9 %all_to_all.58.own_ref = bf16[4,272,256]{2,1,0:T(8,128)(2,1)S(1)} all-to-all(bf16[4,272,256]{2,1,0:T(8,128)(2,1)S(1)} %get-tuple-element.29), channel_id=1, replica_groups=mesh['y'=4,'z'=4,'x'=4,'c'=2] {'x'}, dimensions={0} | all-to-all | bytes 1114112 | tf_op jit(solution)/shard_map/all_to_all | solution.py:432
  158.3 2.0 collective-permute-done.2.other_ref
  160.3 1.9 update.2
  162.3 7.6 %losses.1 = bf16[16,272,256]{2,1,0:T(8,128)(2,1)S(1)} custom-call(bf16[2048,4096]{1,0:T(8,128)(2,1)S(1)} %bitcast.39, bf16[256,2048]{1,0:T(8,128)(2,1)S(1)} %get-tuple-element.32.expot_ref, f32[8,256]{1,0:T(8,128)S(1)} %get-tuple-element.33.tot_ref), custom_call_target="tpu_custom_call" | custom-call | flops 4294967296 | bytes 16777216 | tf_op jit(solution)/shard_map/losses/pallas_call | solution.py:342
  169.9 33.3 %all_to_all.59.pay_ref = bf16[16,272,256]{2,1,0:T(8,128)(2,1)S(1)} all-to-all(bf16[16,272,256]{2,1,0:T(8,128)(2,1)S(1)} %losses.1), channel_id=1, replica_groups=mesh['y'=4,'z'=4,'x'=4,'c'=2] {'y','z'}, dimensions={0} | all-to-all | bytes 4456448 | tf_op jit(solution)/shard_map/all_to_all | solution.py:352
  204.4 32.2 %all_to_all.60.pay_ref = bf16[16,272,256]{2,1,0:T(8,128)(2,1)S(1)} all-to-all(bf16[16,272,256]{2,1,0:T(8,128)(2,1)S(1)} %chunk.3), channel_id=1, replica_groups=mesh['y'=4,'z'=4,'x'=4,'c'=2] {'y','z'}, dimensions={0} | all-to-all | bytes 4456448 | tf_op jit(solution)/shard_map/all_to_all | solution.py:364
  236.8 7.7 %all_to_all.61 = f32[8,2,256]{2,1,0:T(2,128)S(1)} all-to-all(f32[8,2,256]{2,1,0:T(2,128)S(1)} %broadcast_in_dim.19), channel_id=1, replica_groups=mesh['y'=4,'z'=4,'x'=4,'c'=2] {'x','c'}, dimensions={0} | all-to-all | bytes 32768 | tf_op jit(solution)/shard_map/all_to_all | solution.py:372
  244.7 3.5 %tail.3 = (bf16[4096,256]{1,0:T(8,128)(2,1)S(1)}, f32[8,256]{1,0:T(8,128)S(1)}) custom-call(bf16[16,272,256]{2,1,0:T(8,128)(2,1)S(1)} %all_to_all.60.pay_ref, f32[8,256]{1,0:T(8,128)S(1)} %maximum_maximum_fusion.1.stat_ref), custom_call_target="tpu_custom_call" | custom-call | bytes 4194304 | tf_op jit(solution)/shard_map/tail/pallas_call | solution.py:381
  248.2 2.5 gradient.7
  251.3 2.5 gradient.6.own_ref
  254.4 12.7 %all_to_all.62.pay_ref = bf16[4,272,256]{2,1,0:T(8,128)(2,1)S(1)} all-to-all(bf16[4,272,256]{2,1,0:T(8,128)(2,1)S(1)} %pair.3), channel_id=1, replica_groups=mesh['y'=4,'z'=4,'x'=4,'c'=2] {'x'}, dimensions={0} | all-to-all | bytes 1114112 | tf_op jit(solution)/shard_map/all_to_all | solution.py:421
  267.5 11.9 %all_to_all.63.own_ref = bf16[4,272,256]{2,1,0:T(8,128)(2,1)S(1)} all-to-all(bf16[4,272,256]{2,1,0:T(8,128)(2,1)S(1)} %get-tuple-element.36), channel_id=1, replica_groups=mesh['y'=4,'z'=4,'x'=4,'c'=2] {'x'}, dimensions={0} | all-to-all | bytes 1114112 | tf_op jit(solution)/shard_map/all_to_all | solution.py:432
  279.4 1.9 collective-permute-done.5.other_ref
  281.3 1.3 update.3
  283.3 3.6 %all-to-all-start.10 = ((f32[16,8,256]{2,1,0:T(8,128)}), f32[16,8,256]{2,1,0:T(8,128)S(1)}, u32[]{:S(2)}, u32[]{:S(2)}) async-start(f32[16,8,256]{2,1,0:T(8,128)} %broadcast_in_dim.40), calls=%async_computation.10 | async-start | bytes 262144 | tf_op jit(solution)/shard_map/all_to_all | solution.py:450
  287.5 7.2 %all-to-all-done.10 = f32[16,8,256]{2,1,0:T(8,128)S(1)} async-done(((f32[16,8,256]{2,1,0:T(8,128)}), f32[16,8,256]{2,1,0:T(8,128)S(1)}, u32[]{:S(2)}, u32[]{:S(2)}) %all-to-all-start.10) | async-done | bytes 131104 | tf_op jit(solution)/shard_map/all_to_all | solution.py:450
  294.7 1.9 scale.1
  (82 shorter events, 12.7 us)
Async XLA Ops:
  2.2 1.6 copy-start.4
  3.8 1.0 copy-start.7
  4.8 0.7 copy-start.8
  5.5 0.7 copy-start.9
  6.2 0.7 copy-start.10
  6.9 6.0 %copy-start.11 = (bf16[4096,128]{1,0:T(8,128)(2,1)S(1)}, bf16[4096,128]{1,0:T(8,128)(2,1)}, u32[]{:S(2)}) copy-start(bf16[4096,128]{1,0:T(8,128)(2,1)} %fac_ref.1) | copy-start | bytes 3145732
  10.3 1.4 copy-start.2
  11.6 1.3 copy-start.5
  29.9 5.7 %copy-start = (bf16[2048,4096]{1,0:T(8,128)(2,1)}, bf16[2048,4096]{1,0:T(8,128)(2,1)S(1)}, u32[]{:S(2)}) copy-start(bf16[2048,4096]{1,0:T(8,128)(2,1)S(1)} %get-tuple-element.25.p_ref) | copy-start | bytes 50331652
  107.4 9.7 %all-to-all-start.2 = ((f32[8,2,256]{2,1,0:T(2,128)}), f32[8,2,256]{2,1,0:T(2,128)S(1)}, u32[]{:S(2)}, u32[]{:S(2)}) async-start(f32[8,2,256]{2,1,0:T(2,128)} %broadcast_in_dim.18), calls=%async_computation.2 | async-start | bytes 32768 | tf_op jit(solution)/shard_map/all_to_all | solution.py:372
  120.7 5.8 %copy-start.1 = (bf16[2048,4096]{1,0:T(8,128)(2,1)S(1)}, bf16[2048,4096]{1,0:T(8,128)(2,1)}, u32[]{:S(2)}) copy-start(bf16[2048,4096]{1,0:T(8,128)(2,1)} %copy-done) | copy-start | bytes 50331652
  129.1 3.2 %collective-permute-start = (f32[1024,256]{1,0:T(8,128)S(1)}, f32[1024,256]{1,0:T(8,128)S(1)}, u32[]{:S(2)}, u32[]{:S(2)}) collective-permute-start(f32[1024,256]{1,0:T(8,128)S(1)} %gradient.5), channel_id=1, source_target_pairs={{0,1},{1,0},{2,3},{3,2},{4,5},{5,4},{6,7},{7,6},{8,9},{9,8},{10,11... | collective-permute-start | bytes 3145736 | tf_op jit(solution)/shard_map/ppermute | solution.py:407
  129.1 3.1 %collective-permute-start.1 = (f32[8,256]{1,0:T(8,128)S(1)}, f32[8,256]{1,0:T(8,128)S(1)}, u32[]{:S(2)}, u32[]{:S(2)}) collective-permute-start(f32[8,256]{1,0:T(8,128)S(1)} %get-tuple-element.28.soft_ref), channel_id=1, source_target_pairs={{0,1},{1,0},{2,3},{3,2},{4,5},{5,4},{6,7},{7,6},{8,9},{9,8},{10,11... | collective-permute-start | bytes 24584 | tf_op jit(solution)/shard_map/ppermute | solution.py:408
  129.6 32.6 %slice-start = ((s8[16777216]{0:T(1024)(128)(4,1)}), s8[4194304]{0:T(1024)(128)(4,1)S(1)}, s32[]{:S(2)}) async-start(s8[16777216]{0:T(1024)(128)(4,1)} %bitcast.38), calls=%async_computation.11 | async-start | bytes 8388608
  129.6 32.6 %slice-start.1 = ((s8[16777216]{0:T(1024)(128)(4,1)}), s8[4194304]{0:T(1024)(128)(4,1)S(1)}, s32[]{:S(2)}) async-start(s8[16777216]{0:T(1024)(128)(4,1)} %bitcast.38), calls=%async_computation.12 | async-start | bytes 8388608
  129.6 32.6 %slice-start.2 = ((s8[16777216]{0:T(1024)(128)(4,1)}), s8[4194304]{0:T(1024)(128)(4,1)S(1)}, s32[]{:S(2)}) async-start(s8[16777216]{0:T(1024)(128)(4,1)} %bitcast.38), calls=%async_computation.13 | async-start | bytes 8388608
  132.2 28.1 %copy-start.3 = (f32[2048,256]{1,0:T(8,128)S(1)}, f32[2048,256]{1,0:T(8,128)}, u32[]{:S(2)}) copy-start(f32[2048,256]{1,0:T(8,128)} %copy-done.2) | copy-start | bytes 6291460
  132.3 28.0 %copy-start.6 = (f32[2048,256]{1,0:T(8,128)S(1)}, f32[2048,256]{1,0:T(8,128)}, u32[]{:S(2)}) copy-start(f32[2048,256]{1,0:T(8,128)} %copy-done.5) | copy-start | bytes 6291460
  132.8 29.4 %slice-start.3 = ((s8[16777216]{0:T(1024)(128)(4,1)}), s8[4194304]{0:T(1024)(128)(4,1)S(1)}, s32[]{:S(2)}) async-start(s8[16777216]{0:T(1024)(128)(4,1)} %bitcast.38), calls=%async_computation.14 | async-start | bytes 8388608
  158.3 2.0 collective-permute-start.2
  250.7 3.1 %collective-permute-start.3 = (f32[1024,256]{1,0:T(8,128)S(1)}, f32[1024,256]{1,0:T(8,128)S(1)}, u32[]{:S(2)}, u32[]{:S(2)}) collective-permute-start(f32[1024,256]{1,0:T(8,128)S(1)} %gradient.7), channel_id=1, source_target_pairs={{0,1},{1,0},{2,3},{3,2},{4,5},{5,4},{6,7},{7,6},{8,9},{9,8},{10,11... | collective-permute-start | bytes 3145736 | tf_op jit(solution)/shard_map/ppermute | solution.py:407
  250.8 3.0 %collective-permute-start.4 = (f32[8,256]{1,0:T(8,128)S(1)}, f32[8,256]{1,0:T(8,128)S(1)}, u32[]{:S(2)}, u32[]{:S(2)}) collective-permute-start(f32[8,256]{1,0:T(8,128)S(1)} %get-tuple-element.35.soft_ref), channel_id=1, source_target_pairs={{0,1},{1,0},{2,3},{3,2},{4,5},{5,4},{6,7},{7,6},{8,9},{9,8},{10,11... | collective-permute-start | bytes 24584 | tf_op jit(solution)/shard_map/ppermute | solution.py:408
  279.4 2.0 collective-permute-start.5
  283.3 11.4 %all-to-all-start.10 = ((f32[16,8,256]{2,1,0:T(8,128)}), f32[16,8,256]{2,1,0:T(8,128)S(1)}, u32[]{:S(2)}, u32[]{:S(2)}) async-start(f32[16,8,256]{2,1,0:T(8,128)} %broadcast_in_dim.40), calls=%async_computation.10 | async-start | bytes 262144 | tf_op jit(solution)/shard_map/all_to_all | solution.py:450

commit v3 on v2

--- a/solution.py
+++ b/solution.py
@@ -17,7 +17,7 @@
 SMOOTH = 0.5
 EPSILON = 1e-06
 STEP_RATE = 8.0
-HEAD = 16
+HEAD = 8
 SPAN = 127.0
 INTERPRET = False
 
@@ -62,7 +62,8 @@
     rows = [base, span]
     for row in extra:
         rows += split3(row)
-    rows.append(jnp.zeros((HEAD - len(rows), values.shape[1]), f32))
+    if len(rows) < HEAD:
+        rows.append(jnp.zeros((HEAD - len(rows), values.shape[1]), f32))
     return code, jnp.concatenate(rows, axis=0).astype(bf16)
 
 
@@ -73,15 +74,15 @@
 
 def setup_kernel(hold_ref, lgd_ref, sector_ref, rating_ref, allowed_ref, load_ref, weighted_ref, lge_ref, aug_ref, expot_ref, tot_ref):
     rows = sector_ref.shape[1]
-    sectors = allowed_ref.shape[1]
+    sectors = allowed_ref.shape[0]
     here = pl.ds(pl.multiple_of(pl.program_id(0) * rows, rows), rows)
     allowed = allowed_ref[...].astype(f32)
     hot = (lax.broadcasted_iota(jnp.int32, (sectors, rows), 0) == sector_ref[...]).astype(f32)
     lgd = lgd_ref[...]
     parts = jnp.concatenate([hot * part for part in split3(lgd)], axis=0)
-    dims = (((0,), (1,)), ((), ()))
+    dims = (((0,), (0,)), ((), ()))
     elig = lax.dot_general(hot.astype(bf16), allowed.astype(bf16), dims, preferred_element_type=f32)
-    thrice = jnp.concatenate([allowed] * 3, axis=1)
+    thrice = jnp.concatenate([allowed] * 3, axis=0)
     lge = lax.dot_general(parts.astype(bf16), thrice.astype(bf16), dims, preferred_element_type=f32)
     hold = hold_ref[...]
     weighted = elig * hold
@@ -156,18 +157,41 @@
             out_ref[k, rows : rows + HEAD] = head
 
 
-def tail_kernel(tail_scale, pay_ref, stat_ref, weight_ref, soft_ref):
+def stats_kernel(rows, head_ref, out_ref):
+    count = head_ref.shape[0]
+    heads = [head_ref[k].astype(f32) for k in range(count)]
+    means = [join3(head, 2) for head in heads]
+    mean = sum(means) * (1.0 / count)
+    second = sum(join3(head, 5) for head in heads)
+    second += rows * sum(jnp.square(each - mean) for each in means)
+    both = jnp.concatenate([mean, second], axis=0)
+    for k in range(out_ref.shape[0]):
+        out_ref[k] = both
+
+
+def tail_kernel(tail_scale, scenarios, pay_ref, both_ref, weight_ref, soft_ref, stat_ref):
     count, rows = pay_ref.shape[0], pay_ref.shape[1] - HEAD
     step = pl.program_id(0)
+    groups = both_ref.shape[0]
+    means = [both_ref[k, 0:1] for k in range(groups)]
+    center = sum(means) * (1.0 / groups)
+    spread = sum(both_ref[k, 1:2] for k in range(groups)) * (1.0 / scenarios)
+    spread += sum(jnp.square(each - center) for each in means) * (1.0 / groups)
+    deviation = jnp.sqrt(spread + EPSILON)
+    thresh = center + QUANTILE * deviation
+    width = SMOOTH * deviation
+    narrow = 1.0 / width
 
     @pl.when(step == 0)
     def _():
         soft_ref[...] = jnp.zeros_like(soft_ref)
+        stat_ref[0:1] = thresh
+        stat_ref[1:2] = width
 
     for k in range(count):
         head = pay_ref[k, rows : rows + HEAD].astype(f32)
         losses = decode(pay_ref[k, 0:rows], head)
-        scaled = (losses - stat_ref[0:1]) * stat_ref[1:2]
+        scaled = (losses - thresh) * narrow
         small = jnp.exp(-jnp.abs(scaled))
         grown = 1.0 + small
         sigmoid = jnp.where(scaled >= 0.0, tail_scale, tail_scale * small) / grown
@@ -181,76 +205,67 @@
         soft_ref[...] += up + jnp.log(tile).sum(axis=0)
 
 
-def gradient_kernel(half_ref, p_ref, weight_ref, out_ref):
+def gradient_kernel(own, p_ref, weight_ref, out_ref):
     rows = out_ref.shape[0]
-    at = (half_ref[0] * pl.num_programs(0) + pl.program_id(0)) * rows
+    core = lax.axis_index("c")
+    half = core if own else 1 - core
+    at = (half * pl.num_programs(0) + pl.program_id(0)) * rows
     out_ref[...] = jnp.dot(
         p_ref[pl.ds(pl.multiple_of(at, rows), rows)], weight_ref[...], preferred_element_type=f32
     )
 
 
-def pair_kernel(own_ref, other_ref, soft_ref, soft_other_ref, pay_ref):
-    rows = own_ref.shape[0]
-    code, head = encode(own_ref[...] + other_ref[...], [jnp.sum(soft_ref[...] + soft_other_ref[...], axis=0, keepdims=True)])
-    pay_ref[0, 0:rows] = code
-    pay_ref[0, rows : rows + HEAD] = head
-
-
-def whole_kernel(pay_ref, out_ref, soft_ref):
-    rows = pay_ref.shape[1] - HEAD
-    total = jnp.zeros((rows, pay_ref.shape[2]), f32)
-    soft = jnp.zeros((1, pay_ref.shape[2]), f32)
-    for k in range(pay_ref.shape[0]):
-        head = pay_ref[k, rows : rows + HEAD].astype(f32)
-        total += decode(pay_ref[k, 0:rows], head)
+def pair_kernel(own_ref, other_ref, soft_ref, soft_other_ref, *pay_refs):
+    count = len(pay_refs)
+    rows = pay_refs[0].shape[0] - HEAD
+    soft = jnp.sum(soft_ref[...] + soft_other_ref[...], axis=0, keepdims=True)
+    for k, pay_ref in enumerate(pay_refs):
+        at = pl.multiple_of(lax.rem(lax.axis_index("x") + k, count) * rows, rows)
+        code, head = encode(own_ref[pl.ds(at, rows)] + other_ref[pl.ds(at, rows)], [soft])
+        pay_ref[0:rows] = code
+        pay_ref[rows : rows + HEAD] = head
+
+
+def whole_kernel(tail_scale, stat_ref, *refs):
+    pay_refs, out_ref, short_ref = refs[:-2], refs[-2], refs[-1]
+    rows = out_ref.shape[0] - HEAD
+    total = jnp.zeros((rows, out_ref.shape[1]), f32)
+    soft = jnp.zeros((1, out_ref.shape[1]), f32)
+    for pay_ref in pay_refs:
+        head = pay_ref[rows : rows + HEAD].astype(f32)
+        total += decode(pay_ref[0:rows], head)
         soft += join3(head, 2)
-    soft_ref[...] = jnp.broadcast_to(soft, soft_ref.shape)
     code, head = encode(total, [])
-    for k in range(out_ref.shape[0]):
-        out_ref[k, 0:rows] = code
-        out_ref[k, rows : rows + HEAD] = head
-
-
-def update_kernel(core_ref, own_ref, other_ref, prev_ref, lge_ref, unnorm_ref, expot_ref, tot_ref):
-    rows = own_ref.shape[1] - HEAD
-    step = pl.program_id(0)
-    here = pl.ds(pl.multiple_of(step * rows, rows), rows)
-    mine = (step // (pl.num_programs(0) // 2)) == core_ref[0]
-    pay = jnp.where(mine, own_ref[0], other_ref[0])
-    gradient = decode(pay[0:rows], pay[rows : rows + HEAD].astype(f32))
-    lge = lge_ref[here]
-    unnorm = prev_ref[here] * jnp.exp(lge * (-STEP_RATE * gradient))
-    unnorm_ref[here] = unnorm
-    expot_ref[:, here] = jnp.transpose(unnorm * lge).astype(bf16)
-
-    @pl.when(step == 0)
-    def _():
-        tot_ref[...] = jnp.zeros_like(tot_ref)
-
-    tot_ref[0:1] += jnp.sum(unnorm, axis=0, keepdims=True)
-
-
-def last_update_kernel(core_ref, own_ref, other_ref, prev_ref, lge_ref, unnorm_ref, tot_ref):
-    rows = own_ref.shape[1] - HEAD
-    step = pl.program_id(0)
-    here = pl.ds(pl.multiple_of(step * rows, rows), rows)
-    mine = (step // (pl.num_programs(0) // 2)) == core_ref[0]
-    pay = jnp.where(mine, own_ref[0], other_ref[0])
-    gradient = decode(pay[0:rows], pay[rows : rows + HEAD].astype(f32))
-    unnorm = prev_ref[here] * jnp.exp(lge_ref[here] * (-STEP_RATE * gradient))
-    unnorm_ref[here] = unnorm
-
-    @pl.when(step == 0)
-    def _():
-        tot_ref[...] = jnp.zeros_like(tot_ref)
-
-    tot_ref[0:1] += jnp.sum(unnorm, axis=0, keepdims=True)
-
-
-def scale_kernel(unnorm_ref, tot_ref, out_ref):
+    out_ref[0:rows] = code
+    out_ref[rows : rows + HEAD] = head
+    short_ref[...] = jnp.broadcast_to(stat_ref[0:1] + stat_ref[1:2] * (soft * tail_scale), short_ref.shape)
+
+
+def update_kernel(count, last, *refs):
+    own_refs, other_refs = refs[:count], refs[count : 2 * count]
+    prev_ref, lge_ref, unnorm_ref = refs[2 * count : 2 * count + 3]
+    rows = own_refs[0].shape[0] - HEAD
+    core = lax.axis_index("c")
+    total = jnp.zeros((1, prev_ref.shape[1]), f32)
+    for half, pay_refs in ((core, own_refs), (1 - core, other_refs)):
+        for k, pay_ref in enumerate(pay_refs):
+            at = (half * count + lax.rem(lax.axis_index("x") + (count - k), count)) * rows
+            here = pl.ds(pl.multiple_of(at, rows), rows)
+            gradient = decode(pay_ref[0:rows], pay_ref[rows : rows + HEAD].astype(f32))
+            lge = lge_ref[here]
+            unnorm = prev_ref[here] * jnp.exp(lge * (-STEP_RATE * gradient))
+            unnorm_ref[here] = unnorm
+            total += jnp.sum(unnorm, axis=0, keepdims=True)
+            if not last:
+                refs[-2][:, here] = jnp.transpose(unnorm * lge).astype(bf16)
+    refs[-1][...] = jnp.broadcast_to(total, refs[-1].shape)
+
+
+def scale_kernel(obligors, unnorm_ref, totals_ref, out_ref):
     rows = out_ref.shape[0]
     here = pl.ds(pl.multiple_of(pl.program_id(0) * rows, rows), rows)
-    out_ref[...] = unnorm_ref[here] * tot_ref[0:1]
+    total = sum(totals_ref[k, 0:1] for k in range(totals_ref.shape[0]))
+    out_ref[...] = unnorm_ref[here] * (obligors / total)
 
 
 VMEM = pl.BlockSpec(memory_space=pltpu.VMEM)
@@ -258,6 +273,10 @@
 
 def near(array):
     return array if INTERPRET else pltpu.with_memory_space_constraint(array, pltpu.VMEM)
+
+
+def far(array):
+    return array if INTERPRET else pltpu.with_memory_space_constraint(array, pltpu.HBM)
 
 
 def near_shape(shape, dtype):
@@ -283,7 +302,6 @@
     rs, ro = scn_dev // n_obl, obl_dev // (n_x * n_c)
     ps, po = rs + HEAD, ro + HEAD
     half = obl_dev // n_c
-    core = lax.axis_index("c").astype(jnp.int32).reshape(1)
     row8 = sds((8, mandates), f32)
     ratings = barrier.shape[0]
     bar_a = rounded(barrier)
@@ -299,7 +317,7 @@
     prev, lge, aug, expot, tot = call(
         setup_kernel,
         (n_ro,),
-        [blk, line, line, line, whole(allowed.shape), pl.BlockSpec((ro, fdim), lambda i: (i, 0))],
+        [blk, line, line, line, whole(allowed.shape[::-1]), pl.BlockSpec((ro, fdim), lambda i: (i, 0))],
         [VMEM, VMEM, VMEM, VMEM, whole((8, mandates))],
         [
             near_shape((obl_dev, mandates), f32),
@@ -310,7 +328,7 @@
         ],
         nbytes=obl_dev * mandates * 12,
         name="setup",
-    )(holdings, loss_given[None, :], sector[None, :], rating[None, :], allowed, loadings)
+    )(far(holdings), loss_given[None, :], sector[None, :], rating[None, :], allowed.T, far(loadings))
     lge = near(lge)
 
     results = []
@@ -363,101 +381,100 @@
         )(pay)
         pay = lax.all_to_all(pay, OBL, 0, 0, tiled=True)
 
-        heads = pay[:, rs : rs + 8].astype(f32)
-        means = heads[:, 2] + heads[:, 3] + heads[:, 4]
-        seconds = heads[:, 5] + heads[:, 6] + heads[:, 7]
-        mean = jnp.sum(means, 0) / n_obl
-        second = jnp.sum(seconds, 0) + rs * jnp.sum(jnp.square(means - mean), 0)
-        both = jnp.broadcast_to(jnp.stack([mean, second])[None], (n_x * n_c, 2, mandates))
+        n_scn = n_x * n_c
+        both = call(
+            functools.partial(stats_kernel, rs),
+            (1,),
+            [pl.BlockSpec((n_obl, HEAD, mandates), lambda i: (0, rs // HEAD, 0))],
+            whole((n_scn, 2, mandates)),
+            sds((n_scn, 2, mandates), f32),
+            name="stats",
+        )(pay)
         both = lax.all_to_all(both, SCN, 0, 0, tiled=True)
-        means, seconds = both[:, 0], both[:, 1]
-        center = jnp.sum(means, 0) / (n_x * n_c)
-        spread = (jnp.sum(seconds, 0) + scn_dev * jnp.sum(jnp.square(means - center), 0)) / scenarios
-        deviation = jnp.sqrt(spread + EPSILON)
-        thresh = center + QUANTILE * deviation
-        width = SMOOTH * deviation
-        stat = jnp.concatenate([jnp.stack([thresh, 1.0 / width]), jnp.zeros((6, mandates), f32)])
-
-        weight, soft = call(
-            functools.partial(tail_kernel, tail_scale),
+        weight, soft, stat = call(
+            functools.partial(tail_kernel, tail_scale, scenarios),
             (n_obl // 4,),
-            [pl.BlockSpec((4, ps, mandates), lambda i: (i, 0, 0)), whole((8, mandates))],
-            [VMEM, whole((8, mandates))],
-            [near_shape((scn_dev, mandates), bf16), row8],
+            [pl.BlockSpec((4, ps, mandates), lambda i: (i, 0, 0)), whole((n_scn, 2, mandates))],
+            [VMEM, whole((8, mandates)), whole((8, mandates))],
+            [near_shape((scn_dev, mandates), bf16), row8, row8],
             nbytes=scn_dev * mandates * 4,
             name="tail",
-        )(pay, stat)
+        )(pay, both)
         weight = near(weight)
         gblock = min(512, half)
 
-        def gradient_of(which):
+        def gradient_of(own):
             return call(
-                gradient_kernel,
+                functools.partial(gradient_kernel, own),
                 (half // gblock,),
                 [VMEM, VMEM],
-                pl.BlockSpec((gblock, mandates), lambda i, h: (i, 0)),
+                pl.BlockSpec((gblock, mandates), lambda i: (i, 0)),
                 sds((half, mandates), f32),
-                prefetch=1,
                 flops=2 * half * scn_dev * mandates,
                 nbytes=half * scn_dev * 2,
                 name="gradient",
-            )(which, prob, weight)
+            )(prob, weight)
 
         swap = [(0, 1), (1, 0)]
-        sent = lax.ppermute(gradient_of(1 - core), "c", swap)
+        sent = lax.ppermute(gradient_of(False), "c", swap)
         soft_other = lax.ppermute(soft, "c", swap)
-        kept = gradient_of(core)
-        gpay_shape = sds((n_x, po, mandates), bf16)
-        gpay_spec = pl.BlockSpec((1, po, mandates), lambda i, *_: (i, 0, 0))
-        pay = call(
+        kept = gradient_of(True)
+        gshape = sds((po, mandates), bf16)
+        hops = {k: [(i, (i + k) % n_x) for i in range(n_x)] for k in range(1, n_x)}
+        order = sorted(hops, key=lambda k: -min(k, n_x - k))
+        slots = call(
             pair_kernel,
-            (n_x,),
-            [blk, blk, whole((8, mandates)), whole((8, mandates))],
-            gpay_spec,
-            gpay_shape,
+            (1,),
+            [VMEM, VMEM, whole((8, mandates)), whole((8, mandates))],
+            [VMEM] * n_x,
+            [gshape] * n_x,
             nbytes=half * mandates * 10,
             name="pair",
         )(kept, sent, soft, soft_other)
-        pay = lax.all_to_all(pay, "x", 0, 0, tiled=True)
-        pay, soft = call(
-            whole_kernel,
+        slots = list(slots)
+        for k in order:
+            slots[k] = lax.ppermute(slots[k], "x", hops[k])
+        pay, short = call(
+            functools.partial(whole_kernel, tail_scale),
             (1,),
-            [whole((n_x, po, mandates))],
-            [whole((n_x, po, mandates)), whole((8, mandates))],
-            [gpay_shape, row8],
+            [whole((8, mandates))] + [VMEM] * n_x,
+            [VMEM, whole((8, mandates))],
+            [gshape, row8],
             nbytes=half * mandates * 4,
             name="whole",
-        )(pay)
-        results.append(thresh + width * (soft[0] * tail_scale))
-        pay = lax.all_to_all(pay, "x", 0, 0, tiled=True)
-        other = lax.ppermute(pay, "c", swap)
-        gspec = pl.BlockSpec((1, po, mandates), lambda i, *_: (i % n_x, 0, 0))
+        )(stat, *slots)
+        results.append(short[0])
+        slots = [pay] * n_x
+        for k in order:
+            slots[k] = lax.ppermute(pay, "x", hops[k])
+        others = [lax.ppermute(slot, "c", swap) for slot in slots]
         last = iteration == STEPS - 1
+        tot_shape = (n_obl if last else 1, 8, mandates)
         outs = call(
-            last_update_kernel if last else update_kernel,
-            (n_ro,),
-            [gspec, gspec, VMEM, VMEM],
-            [VMEM] + [VMEM] * (not last) + [whole((8, mandates))],
+            functools.partial(update_kernel, n_x, last),
+            (1,),
+            [VMEM] * (2 * n_x + 2),
+            [VMEM] + [VMEM] * (not last) + [VMEM],
             [near_shape((obl_dev, mandates), f32)]
             + [near_shape((mandates, obl_dev), bf16)] * (not last)
-            + [row8],
-            prefetch=1,
+            + [sds(tot_shape, f32)],
             nbytes=obl_dev * mandates * 14,
             name="update",
-        )(core, pay, other, near(prev), lge)
+        )(*slots, *others, near(prev), lge)
         prev, expot, tot = outs[0], outs[-2], outs[-1]
-
-    totals = lax.all_to_all(jnp.broadcast_to(tot[None], (n_obl, 8, mandates)), OBL, 0, 0, tiled=True)
-    factor = obligors / jnp.sum(totals, axis=0)
+        if not last:
+            tot = tot[0]
+
+    totals = lax.all_to_all(tot, OBL, 0, 0, tiled=True)
     positions = call(
-        scale_kernel,
+        functools.partial(scale_kernel, obligors),
         (max(1, obl_dev // 512),),
-        [VMEM, whole((8, mandates))],
+        [VMEM, whole((n_obl, 8, mandates))],
         pl.BlockSpec((min(512, obl_dev), mandates), lambda i: (i, 0)),
         sds((obl_dev, mandates), f32),
         nbytes=obl_dev * mandates * 8,
         name="scale",
-    )(near(prev), factor)
+    )(near(prev), totals)
     return (positions, jnp.stack(results))
 
 

time: 297 us -> 271 us (0.912)
  blocking collectives: 193 us -> 150 us
  waiting for transfers between devices: 16.4 us -> 39.7 us
  local copies, waits for them, and re-layouts: 21.1 us -> 2.82 us
  starting transfers between devices: 9.06 us -> 19.5 us
    all_to_all x4 -> x0, blocking collectives: 49.8 us -> none  [on_device(): pay = lax.all_to_all(pay, 'x', 0, 0, tiled=True)]
    ppermute x4 -> x22, waiting for transfers between devices: 3.91 us -> 32.4 us  [the longest x6 16.6 us: on_device(): slots[k] = lax.ppermute(pay, 'x', hops[k])]
    unnamed x33 -> x10, local copies, waits for them, and re-layouts: 19.7 us -> 2.81 us
    ppermute x4 -> x22, starting transfers between devices: 0.18 us -> 15 us  [the longest x6 7.66 us: on_device(): slots[k] = lax.ppermute(slots[k], 'x', hops[k])]
    all_to_all x1 -> x2, blocking collectives: 7.72 us -> 17.1 us  [on_device(): both = lax.all_to_all(both, SCN, 0, 0, tiled=True)]
    all_to_all x2 -> x1, waiting for transfers between devices: 12.5 us -> 7.23 us  [on_device(): totals = lax.all_to_all(tot, OBL, 0, 0, tiled=True)]
    all_to_all x2 -> x1, starting transfers between devices: 7.89 us -> 3.51 us  [on_device(): totals = lax.all_to_all(tot, OBL, 0, 0, tiled=True)]
    pallas_call x14 -> x16, Pallas kernels: 27.4 us -> 29.6 us  [the longest x4 10.3 us: gradient_of(): call(functools.partial(gradient_kernel, own), (half // gblock,), [VMEM, V...]
  transfers between devices with their start and end apart: 8 -> 25, of which waited for: 4 -> 13; matrix products, arithmetic and copies ran while one was open for 0% -> 0% of each run, Pallas kernels for 2% -> 2%
where the time goes in v3:
time: 271 us
  blocking collectives  150 us (55%)
  Pallas kernels  56.8 us (21%)
  waiting for transfers between devices  39.7 us (15%)
  starting transfers between devices  19.5 us (7%)
  local copies, waits for them, and re-layouts  2.82 us (1%)
    all_to_all x4, blocking collectives, on_device(): pay = lax.all_to_all(pay, OBL, 0, 0, tiled=True)  133 us
    pallas_call x1, Pallas kernels, on_device(): call(first_losses_kernel, (n_obl // 2,), [VMEM, pl.BlockSpec((2 * rs, fdi...  17.2 us
    all_to_all x2, blocking collectives, on_device(): both = lax.all_to_all(both, SCN, 0, 0, tiled=True)  17.1 us
    ppermute x6, waiting for transfers between devices, on_device(): slots[k] = lax.ppermute(pay, 'x', hops[k])  16.6 us
    ppermute x6, waiting for transfers between devices, on_device(): slots[k] = lax.ppermute(slots[k], 'x', hops[k])  13.1 us
    pallas_call x4, Pallas kernels, gradient_of(): call(functools.partial(gradient_kernel, own), (half // gblock,), [VMEM, V...  10.3 us
    ppermute x6, starting transfers between devices, on_device(): slots[k] = lax.ppermute(slots[k], 'x', hops[k])  7.66 us
    pallas_call x1, Pallas kernels, on_device(): call(losses_kernel, (n_obl // 2,), [VMEM, VMEM, whole((8, mandates))], pa...  7.65 us
  transfers between devices with their start and end apart: 25, of which 13 were waited for; matrix products, arithmetic and copies ran while one was open for 0% of the time, Pallas kernels for 2%

profile of v3, /device:TPU:0, one launch (start us, length us, event | category | flops | bytes accessed | tf_op | source)
XLA Modules:
  0.0 270.8 jit_solution(8340276181474441906)
XLA Ops:
  4.2 5.9 %setup.1 = (f32[2048,256]{1,0:T(8,128)S(1)}, f32[2048,256]{1,0:T(8,128)S(1)}, bf16[2048,256]{1,0:T(8,128)(2,1)S(1)}, bf16[256,2048]{1,0:T(8,128)(2,1)S(1)}, f32[8,256]{1,0:T(8,128)S(1)}) custom-call(f32[2048,256]{1,0:T(8,128)} %hold_ref.1, f32[1,2048]{1,0:T(1,128)S(1)} %bitcast.8, s32[1,2048]{1,0:T(1,128)S(1)} %bitcast.9, s32[1,2048]{1,0:T(1,128)S(1)} %bitcast.10, ...), custom_call_target="tpu_custom_call" | custom-call | bytes 6291456 | tf_op jit(solution)/shard_map/setup/pallas_call | solution.py:317
  10.1 17.2 %first_losses.1 = (bf16[2048,4096]{1,0:T(8,128)(2,1)S(1)}, bf16[16,264,256]{2,1,0:T(8,128)(2,1)S(1)}) custom-call(bf16[2048,256]{1,0:T(8,128)(2,1)S(1)} %get-tuple-element.32.load_ref, bf16[4096,128]{1,0:T(8,128)(2,1)S(1)} %copy-done.4, bf16[1,128]{1,0:T(2,128)(2,1)S(1)} %pad_bitcast_fusion.bar_ref, bf16[2048,4096]{1,0:T(8,128)(2,1)} %idio_ref.1, ...), custom_call_target="tpu_custom_call" | custom-call | flops 8589934592 | bytes 33554432 | tf_op jit(solution)/shard_map/first_losses/pallas_call | solution.py:341
  27.3 37.3 %all_to_all.35.pay_ref = bf16[16,264,256]{2,1,0:T(8,128)(2,1)S(1)} all-to-all(bf16[16,264,256]{2,1,0:T(8,128)(2,1)S(1)} %get-tuple-element.36), channel_id=1, replica_groups=mesh['y'=4,'z'=4,'x'=4,'c'=2] {'y','z'}, dimensions={0} | all-to-all | bytes 4325376 | tf_op jit(solution)/shard_map/all_to_all | solution.py:370
  65.8 31.2 %all_to_all.36.head_ref.pay_ref = bf16[16,264,256]{2,1,0:T(8,128)(2,1)S(1)} all-to-all(bf16[16,264,256]{2,1,0:T(8,128)(2,1)S(1)} %chunk.2), channel_id=1, replica_groups=mesh['y'=4,'z'=4,'x'=4,'c'=2] {'y','z'}, dimensions={0} | all-to-all | bytes 4325376 | tf_op jit(solution)/shard_map/all_to_all | solution.py:382
  97.1 9.4 %all_to_all.37.both_ref = f32[8,2,256]{2,1,0:T(2,128)S(1)} all-to-all(f32[8,2,256]{2,1,0:T(2,128)S(1)} %stats.2), channel_id=1, replica_groups=mesh['y'=4,'z'=4,'x'=4,'c'=2] {'x','c'}, dimensions={0} | all-to-all | bytes 32768 | tf_op jit(solution)/shard_map/all_to_all | solution.py:393
  106.5 3.6 %tail.2 = (bf16[4096,256]{1,0:T(8,128)(2,1)S(1)}, f32[8,256]{1,0:T(8,128)S(1)}, f32[8,256]{1,0:T(8,128)S(1)}) custom-call(bf16[16,264,256]{2,1,0:T(8,128)(2,1)S(1)} %all_to_all.36.head_ref.pay_ref, f32[8,2,256]{2,1,0:T(2,128)S(1)} %all_to_all.37.both_ref), custom_call_target="tpu_custom_call" | custom-call | bytes 4194304 | tf_op jit(solution)/shard_map/tail/pallas_call | solution.py:394
  110.1 2.6 gradient.5
  113.3 2.6 gradient.4.own_ref
  117.0 2.1 collective-permute-start.3
  120.2 5.9 %collective-permute-done.2.refs_1_ = bf16[264,256]{1,0:T(8,128)(2,1)S(1)} collective-permute-done((bf16[264,256]{1,0:T(8,128)(2,1)S(1)}, bf16[264,256]{1,0:T(8,128)(2,1)S(1)}, u32[]{:S(2)}, u32[]{:S(2)}) %collective-permute-start.2) | collective-permute-done | bytes 135200 | tf_op jit(solution)/shard_map/ppermute | solution.py:436
  127.1 2.6 collective-permute-start.7
  130.7 4.9 %collective-permute-done.7.refs_3_ = bf16[264,256]{1,0:T(8,128)(2,1)S(1)} collective-permute-done((bf16[264,256]{1,0:T(8,128)(2,1)S(1)}, bf16[264,256]{1,0:T(8,128)(2,1)S(1)}, u32[]{:S(2)}, u32[]{:S(2)}) %collective-permute-start.7) | collective-permute-done | bytes 135200 | tf_op jit(solution)/shard_map/ppermute | solution.py:449
  135.6 2.1 collective-permute-done.6.refs_2_
  139.0 1.3 collective-permute-done.9.refs_5_
  141.4 7.7 %losses.1 = bf16[16,264,256]{2,1,0:T(8,128)(2,1)S(1)} custom-call(bf16[2048,4096]{1,0:T(8,128)(2,1)S(1)} %get-tuple-element.35.p_ref, bf16[256,2048]{1,0:T(8,128)(2,1)S(1)} %get-tuple-element.47.expot_ref, f32[8,256]{1,0:T(8,128)S(1)} %bitcast.11), custom_call_target="tpu_custom_call" | custom-call | flops 4294967296 | bytes 16777216 | tf_op jit(solution)/shard_map/losses/pallas_call | solution.py:360
  149.1 32.6 %all_to_all.38.pay_ref = bf16[16,264,256]{2,1,0:T(8,128)(2,1)S(1)} all-to-all(bf16[16,264,256]{2,1,0:T(8,128)(2,1)S(1)} %losses.1), channel_id=1, replica_groups=mesh['y'=4,'z'=4,'x'=4,'c'=2] {'y','z'}, dimensions={0} | all-to-all | bytes 4325376 | tf_op jit(solution)/shard_map/all_to_all | solution.py:370
  182.9 31.5 %all_to_all.39.head_ref.pay_ref = bf16[16,264,256]{2,1,0:T(8,128)(2,1)S(1)} all-to-all(bf16[16,264,256]{2,1,0:T(8,128)(2,1)S(1)} %chunk.3), channel_id=1, replica_groups=mesh['y'=4,'z'=4,'x'=4,'c'=2] {'y','z'}, dimensions={0} | all-to-all | bytes 4325376 | tf_op jit(solution)/shard_map/all_to_all | solution.py:382
  214.5 7.7 %all_to_all.40.both_ref = f32[8,2,256]{2,1,0:T(2,128)S(1)} all-to-all(f32[8,2,256]{2,1,0:T(2,128)S(1)} %stats.3), channel_id=1, replica_groups=mesh['y'=4,'z'=4,'x'=4,'c'=2] {'x','c'}, dimensions={0} | all-to-all | bytes 32768 | tf_op jit(solution)/shard_map/all_to_all | solution.py:393
  222.2 3.6 %tail.3 = (bf16[4096,256]{1,0:T(8,128)(2,1)S(1)}, f32[8,256]{1,0:T(8,128)S(1)}, f32[8,256]{1,0:T(8,128)S(1)}) custom-call(bf16[16,264,256]{2,1,0:T(8,128)(2,1)S(1)} %all_to_all.39.head_ref.pay_ref, f32[8,2,256]{2,1,0:T(2,128)S(1)} %all_to_all.40.both_ref), custom_call_target="tpu_custom_call" | custom-call | bytes 4194304 | tf_op jit(solution)/shard_map/tail/pallas_call | solution.py:394
  225.8 2.6 gradient.7
  229.0 2.6 gradient.6.own_ref
  232.6 2.1 collective-permute-start.15
  235.8 5.9 %collective-permute-done.14.refs_1_ = bf16[264,256]{1,0:T(8,128)(2,1)S(1)} collective-permute-done((bf16[264,256]{1,0:T(8,128)(2,1)S(1)}, bf16[264,256]{1,0:T(8,128)(2,1)S(1)}, u32[]{:S(2)}, u32[]{:S(2)}) %collective-permute-start.14) | collective-permute-done | bytes 135200 | tf_op jit(solution)/shard_map/ppermute | solution.py:436
  242.7 2.6 collective-permute-start.19
  246.3 4.9 %collective-permute-done.19.refs_3_ = bf16[264,256]{1,0:T(8,128)(2,1)S(1)} collective-permute-done((bf16[264,256]{1,0:T(8,128)(2,1)S(1)}, bf16[264,256]{1,0:T(8,128)(2,1)S(1)}, u32[]{:S(2)}, u32[]{:S(2)}) %collective-permute-start.19) | collective-permute-done | bytes 135200 | tf_op jit(solution)/shard_map/ppermute | solution.py:449
  251.2 2.1 collective-permute-done.18.refs_2_
  253.3 1.3 collective-permute-done.17.refs_1_
  254.7 1.3 collective-permute-done.21.refs_5_
  256.0 1.6 update.3
  257.6 3.5 %all-to-all-start.6 = ((f32[16,8,256]{2,1,0:T(8,128)}), f32[16,8,256]{2,1,0:T(8,128)S(1)}, u32[]{:S(2)}, u32[]{:S(2)}) async-start(f32[16,8,256]{2,1,0:T(8,128)} %get-tuple-element.59), calls=%async_computation.6 | async-start | bytes 262144 | tf_op jit(solution)/shard_map/all_to_all | solution.py:468
  261.7 7.2 %all-to-all-done.6.totals_ref = f32[16,8,256]{2,1,0:T(8,128)S(1)} async-done(((f32[16,8,256]{2,1,0:T(8,128)}), f32[16,8,256]{2,1,0:T(8,128)S(1)}, u32[]{:S(2)}, u32[]{:S(2)}) %all-to-all-start.6) | async-done | bytes 131104 | tf_op jit(solution)/shard_map/all_to_all | solution.py:468
  268.9 1.9 scale.1
  (60 shorter events, 18.6 us)
Async XLA Ops:
  1.4 0.7 copy-start
  2.1 0.7 copy-start.1
  2.8 0.7 copy-start.2
  3.5 0.7 copy-start.3
  4.2 5.9 %copy-start.4 = (bf16[4096,128]{1,0:T(8,128)(2,1)S(1)}, bf16[4096,128]{1,0:T(8,128)(2,1)}, u32[]{:S(2)}) copy-start(bf16[4096,128]{1,0:T(8,128)(2,1)} %fac_ref.1) | copy-start | bytes 3145732
  112.7 3.2 %collective-permute-start = (f32[1024,256]{1,0:T(8,128)S(1)}, f32[1024,256]{1,0:T(8,128)S(1)}, u32[]{:S(2)}, u32[]{:S(2)}) collective-permute-start(f32[1024,256]{1,0:T(8,128)S(1)} %gradient.5), channel_id=1, source_target_pairs={{0,1},{1,0},{2,3},{3,2},{4,5},{5,4},{6,7},{7,6},{8,9},{9,8},{10,11... | collective-permute-start | bytes 3145736 | tf_op jit(solution)/shard_map/ppermute | solution.py:419
  112.8 3.1 %collective-permute-start.1 = (f32[8,256]{1,0:T(8,128)S(1)}, f32[8,256]{1,0:T(8,128)S(1)}, u32[]{:S(2)}, u32[]{:S(2)}) collective-permute-start(f32[8,256]{1,0:T(8,128)S(1)} %get-tuple-element.39.soft_ref), channel_id=1, source_target_pairs={{0,1},{1,0},{2,3},{3,2},{4,5},{5,4},{6,7},{7,6},{8,9},{9,8},{10,11... | collective-permute-start | bytes 24584 | tf_op jit(solution)/shard_map/ppermute | solution.py:420
  116.3 9.8 %collective-permute-start.2 = (bf16[264,256]{1,0:T(8,128)(2,1)S(1)}, bf16[264,256]{1,0:T(8,128)(2,1)S(1)}, u32[]{:S(2)}, u32[]{:S(2)}) collective-permute-start(bf16[264,256]{1,0:T(8,128)(2,1)S(1)} %get-tuple-element.41), channel_id=1, source_target_pairs={{0,2},{2,4},{4,6},{6,0},{1,3},{3,5},{5,7},{7,1},{8,10},{10,12},{12... | collective-permute-start | bytes 405512 | tf_op jit(solution)/shard_map/ppermute | solution.py:436
  117.0 9.1 %collective-permute-start.3 = (bf16[264,256]{1,0:T(8,128)(2,1)S(1)}, bf16[264,256]{1,0:T(8,128)(2,1)S(1)}, u32[]{:S(2)}, u32[]{:S(2)}) collective-permute-start(bf16[264,256]{1,0:T(8,128)(2,1)S(1)} %get-tuple-element.42), channel_id=1, source_target_pairs={{0,4},{2,6},{4,0},{6,2},{1,5},{3,7},{5,1},{7,3},{8,12},{10,14},{12... | collective-permute-start | bytes 405512 | tf_op jit(solution)/shard_map/ppermute | solution.py:436
  119.0 7.7 %collective-permute-start.4 = (bf16[264,256]{1,0:T(8,128)(2,1)S(1)}, bf16[264,256]{1,0:T(8,128)(2,1)S(1)}, u32[]{:S(2)}, u32[]{:S(2)}) collective-permute-start(bf16[264,256]{1,0:T(8,128)(2,1)S(1)} %get-tuple-element.43), channel_id=1, source_target_pairs={{0,6},{2,0},{4,2},{6,4},{1,7},{3,1},{5,3},{7,5},{8,14},{10,8},{12,... | collective-permute-start | bytes 405512 | tf_op jit(solution)/shard_map/ppermute | solution.py:436
  127.1 8.5 %collective-permute-start.7 = (bf16[264,256]{1,0:T(8,128)(2,1)S(1)}, bf16[264,256]{1,0:T(8,128)(2,1)S(1)}, u32[]{:S(2)}, u32[]{:S(2)}) collective-permute-start(bf16[264,256]{1,0:T(8,128)(2,1)S(1)} %get-tuple-element.44.refs_0_), channel_id=1, source_target_pairs={{0,6},{2,0},{4,2},{6,4},{1,7},{3,1},{5,3},{7,5},{8,14},{10,8},{12,... | collective-permute-start | bytes 405512 | tf_op jit(solution)/shard_map/ppermute | solution.py:449
  129.7 8.0 %collective-permute-start.6 = (bf16[264,256]{1,0:T(8,128)(2,1)S(1)}, bf16[264,256]{1,0:T(8,128)(2,1)S(1)}, u32[]{:S(2)}, u32[]{:S(2)}) collective-permute-start(bf16[264,256]{1,0:T(8,128)(2,1)S(1)} %get-tuple-element.44.refs_0_), channel_id=1, source_target_pairs={{0,4},{2,6},{4,0},{6,2},{1,5},{3,7},{5,1},{7,3},{8,12},{10,14},{12... | collective-permute-start | bytes 405512 | tf_op jit(solution)/shard_map/ppermute | solution.py:449
  129.7 9.3 %collective-permute-start.5 = (bf16[264,256]{1,0:T(8,128)(2,1)S(1)}, bf16[264,256]{1,0:T(8,128)(2,1)S(1)}, u32[]{:S(2)}, u32[]{:S(2)}) collective-permute-start(bf16[264,256]{1,0:T(8,128)(2,1)S(1)} %get-tuple-element.44.refs_0_), channel_id=1, source_target_pairs={{0,2},{2,4},{4,6},{6,0},{1,3},{3,5},{5,7},{7,1},{8,10},{10,12},{12... | collective-permute-start | bytes 405512 | tf_op jit(solution)/shard_map/ppermute | solution.py:449
  130.7 8.3 %collective-permute-start.8 = (bf16[264,256]{1,0:T(8,128)(2,1)S(1)}, bf16[264,256]{1,0:T(8,128)(2,1)S(1)}, u32[]{:S(2)}, u32[]{:S(2)}) collective-permute-start(bf16[264,256]{1,0:T(8,128)(2,1)S(1)} %get-tuple-element.44.refs_0_), channel_id=1, source_target_pairs={{0,1},{1,0},{2,3},{3,2},{4,5},{5,4},{6,7},{7,6},{8,9},{9,8},{10,11... | collective-permute-start | bytes 405512 | tf_op jit(solution)/shard_map/ppermute | solution.py:450
  135.6 3.4 %collective-permute-start.11 = (bf16[264,256]{1,0:T(8,128)(2,1)S(1)}, bf16[264,256]{1,0:T(8,128)(2,1)S(1)}, u32[]{:S(2)}, u32[]{:S(2)}) collective-permute-start(bf16[264,256]{1,0:T(8,128)(2,1)S(1)} %collective-permute-done.7.refs_3_), channel_id=1, source_target_pairs={{0,1},{1,0},{2,3},{3,2},{4,5},{5,4},{6,7},{7,6},{8,9},{9,8},{10,11... | collective-permute-start | bytes 405512 | tf_op jit(solution)/shard_map/ppermute | solution.py:450
  137.7 1.4 collective-permute-start.10
  139.0 1.4 collective-permute-start.9
  228.4 3.2 %collective-permute-start.12 = (f32[1024,256]{1,0:T(8,128)S(1)}, f32[1024,256]{1,0:T(8,128)S(1)}, u32[]{:S(2)}, u32[]{:S(2)}) collective-permute-start(f32[1024,256]{1,0:T(8,128)S(1)} %gradient.7), channel_id=1, source_target_pairs={{0,1},{1,0},{2,3},{3,2},{4,5},{5,4},{6,7},{7,6},{8,9},{9,8},{10,11... | collective-permute-start | bytes 3145736 | tf_op jit(solution)/shard_map/ppermute | solution.py:419
  228.5 3.1 %collective-permute-start.13 = (f32[8,256]{1,0:T(8,128)S(1)}, f32[8,256]{1,0:T(8,128)S(1)}, u32[]{:S(2)}, u32[]{:S(2)}) collective-permute-start(f32[8,256]{1,0:T(8,128)S(1)} %get-tuple-element.51.soft_ref), channel_id=1, source_target_pairs={{0,1},{1,0},{2,3},{3,2},{4,5},{5,4},{6,7},{7,6},{8,9},{9,8},{10,11... | collective-permute-start | bytes 24584 | tf_op jit(solution)/shard_map/ppermute | solution.py:420
  232.0 9.8 %collective-permute-start.14 = (bf16[264,256]{1,0:T(8,128)(2,1)S(1)}, bf16[264,256]{1,0:T(8,128)(2,1)S(1)}, u32[]{:S(2)}, u32[]{:S(2)}) collective-permute-start(bf16[264,256]{1,0:T(8,128)(2,1)S(1)} %get-tuple-element.53), channel_id=1, source_target_pairs={{0,2},{2,4},{4,6},{6,0},{1,3},{3,5},{5,7},{7,1},{8,10},{10,12},{12... | collective-permute-start | bytes 405512 | tf_op jit(solution)/shard_map/ppermute | solution.py:436
  232.6 9.1 %collective-permute-start.15 = (bf16[264,256]{1,0:T(8,128)(2,1)S(1)}, bf16[264,256]{1,0:T(8,128)(2,1)S(1)}, u32[]{:S(2)}, u32[]{:S(2)}) collective-permute-start(bf16[264,256]{1,0:T(8,128)(2,1)S(1)} %get-tuple-element.54), channel_id=1, source_target_pairs={{0,4},{2,6},{4,0},{6,2},{1,5},{3,7},{5,1},{7,3},{8,12},{10,14},{12... | collective-permute-start | bytes 405512 | tf_op jit(solution)/shard_map/ppermute | solution.py:436
  234.7 7.7 %collective-permute-start.16 = (bf16[264,256]{1,0:T(8,128)(2,1)S(1)}, bf16[264,256]{1,0:T(8,128)(2,1)S(1)}, u32[]{:S(2)}, u32[]{:S(2)}) collective-permute-start(bf16[264,256]{1,0:T(8,128)(2,1)S(1)} %get-tuple-element.55), channel_id=1, source_target_pairs={{0,6},{2,0},{4,2},{6,4},{1,7},{3,1},{5,3},{7,5},{8,14},{10,8},{12,... | collective-permute-start | bytes 405512 | tf_op jit(solution)/shard_map/ppermute | solution.py:436
  242.7 8.5 %collective-permute-start.19 = (bf16[264,256]{1,0:T(8,128)(2,1)S(1)}, bf16[264,256]{1,0:T(8,128)(2,1)S(1)}, u32[]{:S(2)}, u32[]{:S(2)}) collective-permute-start(bf16[264,256]{1,0:T(8,128)(2,1)S(1)} %get-tuple-element.56.refs_0_), channel_id=1, source_target_pairs={{0,6},{2,0},{4,2},{6,4},{1,7},{3,1},{5,3},{7,5},{8,14},{10,8},{12,... | collective-permute-start | bytes 405512 | tf_op jit(solution)/shard_map/ppermute | solution.py:449
  245.4 8.0 %collective-permute-start.18 = (bf16[264,256]{1,0:T(8,128)(2,1)S(1)}, bf16[264,256]{1,0:T(8,128)(2,1)S(1)}, u32[]{:S(2)}, u32[]{:S(2)}) collective-permute-start(bf16[264,256]{1,0:T(8,128)(2,1)S(1)} %get-tuple-element.56.refs_0_), channel_id=1, source_target_pairs={{0,4},{2,6},{4,0},{6,2},{1,5},{3,7},{5,1},{7,3},{8,12},{10,14},{12... | collective-permute-start | bytes 405512 | tf_op jit(solution)/shard_map/ppermute | solution.py:449
  245.4 9.3 %collective-permute-start.17 = (bf16[264,256]{1,0:T(8,128)(2,1)S(1)}, bf16[264,256]{1,0:T(8,128)(2,1)S(1)}, u32[]{:S(2)}, u32[]{:S(2)}) collective-permute-start(bf16[264,256]{1,0:T(8,128)(2,1)S(1)} %get-tuple-element.56.refs_0_), channel_id=1, source_target_pairs={{0,2},{2,4},{4,6},{6,0},{1,3},{3,5},{5,7},{7,1},{8,10},{10,12},{12... | collective-permute-start | bytes 405512 | tf_op jit(solution)/shard_map/ppermute | solution.py:449
  246.3 8.3 %collective-permute-start.20 = (bf16[264,256]{1,0:T(8,128)(2,1)S(1)}, bf16[264,256]{1,0:T(8,128)(2,1)S(1)}, u32[]{:S(2)}, u32[]{:S(2)}) collective-permute-start(bf16[264,256]{1,0:T(8,128)(2,1)S(1)} %get-tuple-element.56.refs_0_), channel_id=1, source_target_pairs={{0,1},{1,0},{2,3},{3,2},{4,5},{5,4},{6,7},{7,6},{8,9},{9,8},{10,11... | collective-permute-start | bytes 405512 | tf_op jit(solution)/shard_map/ppermute | solution.py:450
  251.2 3.4 %collective-permute-start.23 = (bf16[264,256]{1,0:T(8,128)(2,1)S(1)}, bf16[264,256]{1,0:T(8,128)(2,1)S(1)}, u32[]{:S(2)}, u32[]{:S(2)}) collective-permute-start(bf16[264,256]{1,0:T(8,128)(2,1)S(1)} %collective-permute-done.19.refs_3_), channel_id=1, source_target_pairs={{0,1},{1,0},{2,3},{3,2},{4,5},{5,4},{6,7},{7,6},{8,9},{9,8},{10,11... | collective-permute-start | bytes 405512 | tf_op jit(solution)/shard_map/ppermute | solution.py:450
  253.3 1.4 collective-permute-start.22
  254.7 1.4 collective-permute-start.21
  257.6 11.4 %all-to-all-start.6 = ((f32[16,8,256]{2,1,0:T(8,128)}), f32[16,8,256]{2,1,0:T(8,128)S(1)}, u32[]{:S(2)}, u32[]{:S(2)}) async-start(f32[16,8,256]{2,1,0:T(8,128)} %get-tuple-element.59), calls=%async_computation.6 | async-start | bytes 262144 | tf_op jit(solution)/shard_map/all_to_all | solution.py:468

commit v4 on v3

v4 whole, which is shorter than its diff:
```python
import functools

import jax
import jax.numpy as jnp
from jax import lax
from jax.experimental import pallas as pl
from jax.experimental.pallas import tpu as pltpu
from jax.sharding import Mesh
from jax.sharding import PartitionSpec as P

STEPS = 2
OBL = ("y", "z")
SCN = ("x", "c")
IDIO_SCALE = 0.8
LEVEL = 0.99
QUANTILE = 2.326
SMOOTH = 0.5
EPSILON = 1e-06
STEP_RATE = 8.0
HEAD = 8
SPAN = 127.0
INTERPRET = False

f32 = jnp.float32
bf16 = jnp.bfloat16


def call(kernel, grid, in_specs, out_specs, out_shape, scratch=(), prefetch=0, flops=0, nbytes=0, name=None):
    spec = pltpu.PrefetchScalarGridSpec(
        num_scalar_prefetch=prefetch, grid=grid, in_specs=in_specs, out_specs=out_specs, scratch_shapes=list(scratch)
    )
    return pl.pallas_call(
        kernel,
        grid_spec=spec,
        out_shape=out_shape,
        compiler_params=pltpu.CompilerParams(vmem_limit_bytes=24 * 1024 * 1024),
        cost_estimate=pl.CostEstimate(flops=int(flops), bytes_accessed=int(nbytes), transcendentals=0),
        interpret=INTERPRET,
        name=name,
    )


def split3(value):
    a = value.astype(bf16)
    rest = value - a.astype(f32)
    b = rest.astype(bf16)
    c = (rest - b.astype(f32)).astype(bf16)
    return [a.astype(f32), b.astype(f32), c.astype(f32)]


def join3(head, at):
    return head[at : at + 1] + head[at + 1 : at + 2] + head[at + 2 : at + 3]


def encode(values, extra):
    low = jnp.min(values, axis=0, keepdims=True)
    high = jnp.max(values, axis=0, keepdims=True)
    span = jnp.maximum(jnp.maximum(high - low, jnp.abs(low) * (1.0 / 64.0)), 1e-30)
    base = low.astype(bf16).astype(f32)
    span = (span * 1.02).astype(bf16).astype(f32)
    code = jnp.exp((values - base) * (SPAN / span) - 0.5 * SPAN).astype(bf16)
    rows = [base, span]
    for row in extra:
        rows += split3(row)
    if len(rows) < HEAD:
        rows.append(jnp.zeros((HEAD - len(rows), values.shape[1]), f32))
    return code, jnp.concatenate(rows, axis=0).astype(bf16)


def decode(code, head):
    base, span = head[0:1], head[1:2]
    return (base + 0.5 * span) + jnp.log(code.astype(f32)) * (span * (1.0 / SPAN))


def edge_of(total, reach):
    span = jnp.maximum(2.02 * reach, 1e-30).astype(bf16).astype(f32)
    rows = [span] + split3(total)
    rows.append(jnp.zeros((128 - len(rows), total.shape[1]), f32))
    return jnp.transpose(jnp.concatenate(rows, axis=0)).astype(bf16)


def put_codes(doubled, edge_ref, pay_ref, at):
    parts, rows = pay_ref.shape[:2]
    span = edge_ref[:, 0:1].astype(f32)
    code = jnp.exp(doubled * (SPAN / span) - 0.5 * SPAN).astype(bf16)
    pay_ref[:, :, at] = code.reshape(parts, rows, -1)

    @pl.when(pl.program_id(0) == 0)
    def _():
        pay_ref[:, :, pay_ref.shape[2] - 128 :] = edge_ref[...].reshape(parts, rows, 128)


def setup_kernel(hold_ref, lgd_ref, sector_ref, rating_ref, allowed_ref, load_ref, weighted_ref, lge_ref, aug_ref, expot_ref, edge_ref, sums_ref):
    rows = sector_ref.shape[1]
    sectors = allowed_ref.shape[0]
    here = pl.ds(pl.multiple_of(pl.program_id(0) * rows, rows), rows)
    allowed = allowed_ref[...].astype(f32)
    hot = (lax.broadcasted_iota(jnp.int32, (sectors, rows), 0) == sector_ref[...]).astype(f32)
    lgd = lgd_ref[...]
    parts = jnp.concatenate([hot * part for part in split3(lgd)], axis=0)
    dims = (((0,), (0,)), ((), ()))
    elig = lax.dot_general(hot.astype(bf16), allowed.astype(bf16), dims, preferred_element_type=f32)
    thrice = jnp.concatenate([allowed] * 3, axis=0)
    lge = lax.dot_general(parts.astype(bf16), thrice.astype(bf16), dims, preferred_element_type=f32)
    hold = hold_ref[...]
    weighted = elig * hold
    weighted_ref[here] = weighted
    lge_ref[here] = lge
    expo = (lge * hold).astype(bf16).astype(f32)
    expot_ref[:, here] = jnp.transpose(expo).astype(bf16)
    lane = lax.broadcasted_iota(jnp.int32, (128, rows), 0)
    rated = ((lane % 16 == rating_ref[...]) & (lane < 48)).astype(f32)
    aug_ref[here] = jnp.concatenate([load_ref[...], jnp.transpose(rated).astype(bf16)], axis=1)

    @pl.when(pl.program_id(0) == 0)
    def _():
        sums_ref[...] = jnp.zeros_like(sums_ref)

    sums_ref[0:1] += jnp.sum(weighted, axis=0, keepdims=True)
    sums_ref[1:2] += jnp.sum(expo, axis=0, keepdims=True)

    @pl.when(pl.program_id(0) == pl.num_programs(0) - 1)
    def _():
        edge_ref[...] = edge_of(sums_ref[0:1], sums_ref[1:2])


def first_losses_kernel(load_ref, fac_ref, bar_ref, idio_ref, expot_ref, edge_ref, p_ref, pay_ref):
    wide = fac_ref.shape[0]
    cols = pl.ds(pl.multiple_of(pl.program_id(0) * wide, wide), wide)
    block = min(256, load_ref.shape[0])
    fac = jnp.concatenate([fac_ref[...], jnp.broadcast_to(bar_ref[...], (wide, 128))], axis=1)
    for i in range(load_ref.shape[0] // block):
        sl = slice(i * block, (i + 1) * block)
        latent = lax.dot_general(load_ref[sl], fac, (((1,), (1,)), ((), ())), preferred_element_type=f32)
        p_ref[sl, cols] = (jnp.tanh(latent + IDIO_SCALE * idio_ref[sl].astype(f32)) + 1.0).astype(bf16)
    put_codes(jnp.dot(expot_ref[...], p_ref[:, cols], preferred_element_type=f32), edge_ref, pay_ref, cols)


def losses_kernel(wide, p_ref, expot_ref, edge_ref, pay_ref):
    cols = pl.ds(pl.multiple_of(pl.program_id(0) * wide, wide), wide)
    put_codes(jnp.dot(expot_ref[...], p_ref[:, cols], preferred_element_type=f32), edge_ref, pay_ref, cols)


def sum_kernel(pay_ref, losses_ref, both_ref):
    count = pay_ref.shape[0]
    wide = losses_ref.shape[1]
    edges = [pay_ref[k, :, wide:].astype(f32) for k in range(count)]
    spans = [edge[:, 0:1] for edge in edges]
    offset = 0.5 * sum(spans)
    scale = 0.5 / sum(edge[:, 1:2] + edge[:, 2:3] + edge[:, 3:4] for edge in edges)
    factors = [span * (1.0 / SPAN) for span in spans]
    piece = min(1024, wide)
    total = 0.0
    for at in range(0, wide, piece):
        part = sum(jnp.log(pay_ref[k, :, at : at + piece].astype(f32)) * factors[k] for k in range(count))
        part = (part + offset) * scale
        losses_ref[:, at : at + piece] = part
        total += jnp.sum(part, axis=1, keepdims=True)
    mean = total * (1.0 / wide)
    second = jnp.sum(jnp.square(losses_ref[...] - mean), axis=1, keepdims=True)
    lane = lax.broadcasted_iota(jnp.int32, both_ref.shape[1:], 1)
    both = jnp.where(lane == 0, mean, jnp.where(lane == 1, second, 0.0))
    for k in range(both_ref.shape[0]):
        both_ref[k] = both


def tail_kernel(tail_scale, scenarios, losses_ref, both_ref, pay_ref):
    groups = both_ref.shape[0]
    wide = losses_ref.shape[1]
    means = [both_ref[k, :, 0:1] for k in range(groups)]
    center = sum(means) * (1.0 / groups)
    spread = sum(both_ref[k, :, 1:2] for k in range(groups)) * (1.0 / scenarios)
    spread += sum(jnp.square(each - center) for each in means) * (1.0 / groups)
    deviation = jnp.sqrt(spread + EPSILON)
    thresh = center + QUANTILE * deviation
    width = SMOOTH * deviation
    narrow = 1.0 / width
    piece = min(1024, wide)
    soft = 0.0
    for at in range(0, wide, piece):
        scaled = (losses_ref[:, at : at + piece] - thresh) * narrow
        small = jnp.exp(-jnp.abs(scaled))
        grown = 1.0 + small
        half = 0.5 * tail_scale
        weight = (jnp.where(scaled >= 0.0, half, half * small) / grown).astype(bf16)
        soft += jnp.sum(jnp.maximum(scaled, 0.0) + jnp.log(grown), axis=1, keepdims=True)
        for k in range(pay_ref.shape[0]):
            pay_ref[k, :, at : at + piece] = weight
    lane = lax.broadcasted_iota(jnp.int32, (pay_ref.shape[1], 128), 1)
    edge = jnp.zeros(lane.shape, f32)
    for at, part in enumerate(split3(soft) + split3(thresh) + split3(width)):
        edge = jnp.where(lane == at, part, edge)
    for k in range(pay_ref.shape[0]):
        pay_ref[k, :, wide:] = edge.astype(bf16)


def heads_kernel(edge_ref, soft_ref, stat_ref):
    rows = jnp.transpose(edge_ref[...].reshape(-1, 128).astype(f32))
    soft_ref[...] = jnp.broadcast_to(join3(rows, 0), soft_ref.shape)
    stat_ref[...] = jnp.zeros_like(stat_ref)
    stat_ref[0:1] = join3(rows, 3)
    stat_ref[1:2] = join3(rows, 6)


def gradient_kernel(own, p_ref, weight_ref, out_ref):
    rows = out_ref.shape[0]
    core = lax.axis_index("c")
    half = core if own else 1 - core
    at = (half * pl.num_programs(0) + pl.program_id(0)) * rows
    weight = weight_ref[:, :, 0 : p_ref.shape[1]].reshape(out_ref.shape[1], -1)
    out_ref[...] = lax.dot_general(
        p_ref[pl.ds(pl.multiple_of(at, rows), rows)],
        weight,
        (((1,), (1,)), ((), ())),
        preferred_element_type=f32,
    )


def pair_kernel(own_ref, other_ref, soft_ref, soft_other_ref, *pay_refs):
    count = len(pay_refs)
    rows = pay_refs[0].shape[0] - HEAD
    soft = soft_ref[0:1] + soft_other_ref[0:1]
    for k, pay_ref in enumerate(pay_refs):
        at = pl.multiple_of(lax.rem(lax.axis_index("x") + k, count) * rows, rows)
        code, head = encode(own_ref[pl.ds(at, rows)] + other_ref[pl.ds(at, rows)], [soft])
        pay_ref[0:rows] = code
        pay_ref[rows : rows + HEAD] = head


def whole_kernel(tail_scale, stat_ref, *refs):
    pay_refs, out_ref, short_ref = refs[:-2], refs[-2], refs[-1]
    rows = out_ref.shape[0] - HEAD
    total = jnp.zeros((rows, out_ref.shape[1]), f32)
    soft = jnp.zeros((1, out_ref.shape[1]), f32)
    for pay_ref in pay_refs:
        head = pay_ref[rows : rows + HEAD].astype(f32)
        total += decode(pay_ref[0:rows], head)
        soft += join3(head, 2)
    code, head = encode(total, [])
    out_ref[0:rows] = code
    out_ref[rows : rows + HEAD] = head
    short_ref[...] = jnp.broadcast_to(stat_ref[0:1] + stat_ref[1:2] * (soft * tail_scale), short_ref.shape)


def update_kernel(count, last, *refs):
    own_refs, other_refs = refs[:count], refs[count : 2 * count]
    prev_ref, lge_ref, unnorm_ref = refs[2 * count : 2 * count + 3]
    rows = own_refs[0].shape[0] - HEAD
    core = lax.axis_index("c")
    total = jnp.zeros((1, prev_ref.shape[1]), f32)
    reach = jnp.zeros((1, prev_ref.shape[1]), f32)
    for half, pay_refs in ((core, own_refs), (1 - core, other_refs)):
        for k, pay_ref in enumerate(pay_refs):
            at = (half * count + lax.rem(lax.axis_index("x") + (count - k), count)) * rows
            here = pl.ds(pl.multiple_of(at, rows), rows)
            gradient = decode(pay_ref[0:rows], pay_ref[rows : rows + HEAD].astype(f32))
            lge = lge_ref[here]
            unnorm = prev_ref[here] * jnp.exp(lge * (-STEP_RATE * gradient))
            unnorm_ref[here] = unnorm
            total += jnp.sum(unnorm, axis=0, keepdims=True)
            if not last:
                expo = (unnorm * lge).astype(bf16).astype(f32)
                refs[-2][:, here] = jnp.transpose(expo).astype(bf16)
                reach += jnp.sum(expo, axis=0, keepdims=True)
    if last:
        refs[-1][...] = jnp.broadcast_to(total[None], refs[-1].shape)
    else:
        refs[-1][...] = edge_of(total, reach)


def scale_kernel(obligors, unnorm_ref, totals_ref, out_ref):
    rows = out_ref.shape[0]
    here = pl.ds(pl.multiple_of(pl.program_id(0) * rows, rows), rows)
    total = sum(totals_ref[k] for k in range(totals_ref.shape[0]))
    out_ref[...] = unnorm_ref[here] * (obligors / total)


VMEM = pl.BlockSpec(memory_space=pltpu.VMEM)


def near(array):
    return array if INTERPRET else pltpu.with_memory_space_constraint(array, pltpu.VMEM)


def far(array):
    return array if INTERPRET else pltpu.with_memory_space_constraint(array, pltpu.HBM)


def near_shape(shape, dtype):
    return jax.ShapeDtypeStruct(shape, dtype) if INTERPRET else pltpu.VMEM(shape, dtype)


def whole(shape):
    return pl.BlockSpec(shape, lambda *_: (0,) * len(shape))


def rounded(value):
    return lax.reduce_precision(value, 8, 7)


def on_device(factors, idiosyncratic, loadings, rating, barrier, loss_given, sector, allowed, holdings):
    sds = jax.ShapeDtypeStruct
    n_obl, n_x, n_c = lax.axis_size(OBL), lax.axis_size("x"), lax.axis_size("c")
    obl_dev, scn_dev = idiosyncratic.shape
    mandates = holdings.shape[1]
    obligors = obl_dev * n_obl
    scenarios = scn_dev * n_x * n_c
    tail_scale = 1.0 / ((1.0 - LEVEL) * scenarios)
    ro = obl_dev // (n_x * n_c)
    po = ro + HEAD
    mr = mandates // n_obl
    half = obl_dev // n_c
    row8 = sds((8, mandates), f32)
    ratings = barrier.shape[0]
    bar_a = rounded(barrier)
    bar_b = rounded(barrier - bar_a)
    bar_c = barrier - bar_a - bar_b
    bars = -jnp.concatenate([bar_a, bar_b, bar_c])
    bars = jnp.pad(bars, (0, 128 - 3 * ratings)).astype(bf16)[None, :]
    fdim = factors.shape[1]

    sb = min(512, obl_dev)
    line = pl.BlockSpec((1, sb), lambda i: (0, i))
    prev, lge, aug, expot, edge = call(
        setup_kernel,
        (obl_dev // sb,),
        [
            pl.BlockSpec((sb, mandates), lambda i: (i, 0)),
            line,
            line,
            line,
            whole(allowed.shape[::-1]),
            pl.BlockSpec((sb, fdim), lambda i: (i, 0)),
        ],
        [VMEM] * 5,
        [
            near_shape((obl_dev, mandates), f32),
            near_shape((obl_dev, mandates), f32),
            near_shape((obl_dev, fdim + 128), bf16),
            near_shape((mandates, obl_dev), bf16),
            near_shape((mandates, 128), bf16),
        ],
        scratch=[pltpu.VMEM((8, mandates), f32)],
        nbytes=obl_dev * mandates * 12,
        name="setup",
    )(far(holdings), far(loss_given[None, :]), far(sector[None, :]), far(rating[None, :]), allowed.T, far(loadings))
    lge = near(lge)

    results = []
    prob = None
    for iteration in range(STEPS):
        pay_shape = sds((n_obl, mr, scn_dev + 128), bf16)
        wide = min(512, scn_dev)
        if iteration == 0:
            prob, pay = call(
                first_losses_kernel,
                (scn_dev // wide,),
                [
                    VMEM,
                    pl.BlockSpec((wide, fdim), lambda i: (i, 0)),
                    whole((1, 128)),
                    pl.BlockSpec((obl_dev, wide), lambda i: (0, i)),
                    VMEM,
                    VMEM,
                ],
                [VMEM, VMEM],
                [near_shape((obl_dev, scn_dev), bf16), pay_shape],
                flops=4 * obl_dev * scn_dev * mandates,
                nbytes=obl_dev * scn_dev * 4,
                name="first_losses",
            )(near(aug), factors, bars, idiosyncratic, near(expot), near(edge))
            prob = near(prob)
        else:
            pay = call(
                functools.partial(losses_kernel, wide),
                (scn_dev // wide,),
                [VMEM, VMEM, VMEM],
                VMEM,
                pay_shape,
                flops=2 * obl_dev * scn_dev * mandates,
                nbytes=obl_dev * scn_dev * 2,
                name="losses",
            )(prob, near(expot), near(edge))
        pay = lax.all_to_all(pay, OBL, 0, 0, tiled=True)
        n_scn = n_x * n_c
        losses, both = call(
            sum_kernel,
            (1,),
            [VMEM],
            [VMEM, VMEM],
            [near_shape((mr, scn_dev), f32), sds((n_scn, mr, 128), f32)],
            nbytes=mandates * scn_dev * 2,
            name="sum",
        )(pay)
        both = lax.all_to_all(both, SCN, 0, 0, tiled=True)
        weight = call(
            functools.partial(tail_kernel, tail_scale, scenarios),
            (1,),
            [VMEM, VMEM],
            VMEM,
            pay_shape,
            nbytes=mandates * scn_dev * 2,
            name="tail",
        )(near(losses), both)
        weight = lax.all_to_all(weight, OBL, 0, 0, tiled=True)
        soft, stat = call(
            heads_kernel,
            (1,),
            [pl.BlockSpec((n_obl, mr, 128), lambda i: (0, 0, scn_dev // 128))],
            [whole((8, mandates)), whole((8, mandates))],
            [row8, row8],
            name="heads",
        )(weight)
        gblock = min(512, half)

        def gradient_of(own):
            return call(
                functools.partial(gradient_kernel, own),
                (half // gblock,),
                [VMEM, VMEM],
                pl.BlockSpec((gblock, mandates), lambda i: (i, 0)),
                sds((half, mandates), f32),
                flops=2 * half * scn_dev * mandates,
                nbytes=half * scn_dev * 2,
                name="gradient",
            )(prob, weight)

        swap = [(0, 1), (1, 0)]
        sent = lax.ppermute(gradient_of(False), "c", swap)
        soft_other = lax.ppermute(soft, "c", swap)
        kept = gradient_of(True)
        gshape = sds((po, mandates), bf16)
        hops = {k: [(i, (i + k) % n_x) for i in range(n_x)] for k in range(1, n_x)}
        order = sorted(hops, key=lambda k: -min(k, n_x - k))
        slots = call(
            pair_kernel,
            (1,),
            [VMEM, VMEM, whole((8, mandates)), whole((8, mandates))],
            [VMEM] * n_x,
            [gshape] * n_x,
            nbytes=half * mandates * 10,
            name="pair",
        )(kept, sent, soft, soft_other)
        slots = list(slots)
        for k in order:
            slots[k] = lax.ppermute(slots[k], "x", hops[k])
        pay, short = call(
            functools.partial(whole_kernel, tail_scale),
            (1,),
            [whole((8, mandates))] + [VMEM] * n_x,
            [VMEM, whole((8, mandates))],
            [gshape, row8],
            nbytes=half * mandates * 4,
            name="whole",
        )(stat, *slots)
        results.append(short[0])
        slots = [pay] * n_x
        for k in order:
            slots[k] = lax.ppermute(pay, "x", hops[k])
        others = [lax.ppermute(slot, "c", swap) for slot in slots]
        last = iteration == STEPS - 1
        outs = call(
            functools.partial(update_kernel, n_x, last),
            (1,),
            [VMEM] * (2 * n_x + 2),
            [VMEM] + [VMEM] * (not last) + [VMEM],
            [near_shape((obl_dev, mandates), f32)]
            + [near_shape((mandates, obl_dev), bf16)] * (not last)
            + [sds((n_obl, 1, mandates), f32) if last else near_shape((mandates, 128), bf16)],
            nbytes=obl_dev * mandates * 14,
            name="update",
        )(*slots, *others, near(prev), lge)
        prev, expot, edge = outs[0], outs[-2], outs[-1]

    totals = lax.all_to_all(edge, OBL, 0, 0, tiled=True)
    positions = call(
        functools.partial(scale_kernel, obligors),
        (max(1, obl_dev // 512),),
        [VMEM, whole((n_obl, 1, mandates))],
        pl.BlockSpec((min(512, obl_dev), mandates), lambda i: (i, 0)),
        sds((obl_dev, mandates), f32),
        nbytes=obl_dev * mandates * 8,
        name="scale",
    )(near(prev), totals)
    return (positions, jnp.stack(results))


def solution(mesh):
    n_obl, n_scn = mesh.shape["obl"], mesh.shape["scn"]
    side = 1
    while side * side < n_obl:
        side *= 2
    fine = Mesh(mesh.devices.reshape(side, n_obl // side, n_scn // 2, 2), ("y", "z", "x", "c"))
    in_specs = (P(SCN, None), P(OBL, SCN), P(OBL, None), P(OBL), P(), P(OBL), P(OBL), P(), P(OBL, None))
    return jax.shard_map(on_device, mesh=fine, in_specs=in_specs, out_specs=(P(OBL, None), P()), check_vma=False)
```

time: 271 us -> 259 us (0.956)
  Pallas kernels: 56.8 us -> 44.3 us
  blocking collectives: 150 us -> 153 us
    all_to_all x0 -> x2, blocking collectives: none -> 65 us  [on_device(): weight = lax.all_to_all(weight, OBL, 0, 0, tiled=True)]
    all_to_all x4 -> x2, blocking collectives: 133 us -> 69.9 us  [on_device(): pay = lax.all_to_all(pay, OBL, 0, 0, tiled=True)]
    pallas_call x9, Pallas kernels: 40.5 us -> 27.5 us  [the longest x1 14.3 us: on_device(): call(first_losses_kernel, (scn_dev // wide,), [VMEM, pl.BlockSpec((wide,...]
  transfers between devices with their start and end apart: 25 -> 25, of which waited for: 13 -> 15; matrix products, arithmetic and copies ran while one was open for 0% -> 0% of each run, Pallas kernels for 2% -> 2%
where the time goes in v4:
time: 259 us; the launch traced here: 258 us
  blocking collectives  153 us (59%)
  Pallas kernels  44.3 us (17%)
  waiting for transfers between devices  39.3 us (15%)
  starting transfers between devices  19.2 us (7%)
    all_to_all x2, blocking collectives, on_device(): pay = lax.all_to_all(pay, OBL, 0, 0, tiled=True)  69.9 us
    all_to_all x2, blocking collectives, on_device(): weight = lax.all_to_all(weight, OBL, 0, 0, tiled=True)  65 us
    all_to_all x2, blocking collectives, on_device(): both = lax.all_to_all(both, SCN, 0, 0, tiled=True)  17.7 us
    ppermute x6, waiting for transfers between devices, on_device(): slots[k] = lax.ppermute(pay, 'x', hops[k])  16.4 us
    pallas_call x1, Pallas kernels, on_device(): call(first_losses_kernel, (scn_dev // wide,), [VMEM, pl.BlockSpec((wide,...  14.3 us
    ppermute x6, waiting for transfers between devices, on_device(): slots[k] = lax.ppermute(slots[k], 'x', hops[k])  13.2 us
    pallas_call x4, Pallas kernels, gradient_of(): call(functools.partial(gradient_kernel, own), (half // gblock,), [VMEM, V...  10.5 us
    ppermute x6, starting transfers between devices, on_device(): slots[k] = lax.ppermute(slots[k], 'x', hops[k])  7.39 us
  transfers between devices with their start and end apart: 25, of which 15 were waited for; matrix products, arithmetic and copies ran while one was open for 0% of the time, Pallas kernels for 2%

profile of v4, /device:TPU:0, one launch (start us, length us, event | category | flops | bytes accessed | tf_op | source)
XLA Modules:
  0.0 258.3 jit_solution(1550086891253267700)
XLA Ops:
  2.1 4.1 %setup.1 = (f32[2048,256]{1,0:T(8,128)S(1)}, f32[2048,256]{1,0:T(8,128)S(1)}, bf16[2048,256]{1,0:T(8,128)(2,1)S(1)}, bf16[256,2048]{1,0:T(8,128)(2,1)S(1)}, bf16[256,128]{1,0:T(8,128)(2,1)S(1)}) custom-call(f32[2048,256]{1,0:T(8,128)} %hold_ref.1, f32[1,2048]{1,0:T(1,128)} %bitcast.7, s32[1,2048]{1,0:T(1,128)} %bitcast.8, s32[1,2048]{1,0:T(1,128)} %bitcast.9, ...), custom_call_target="tpu_custom_call" | custom-call | bytes 6291456 | tf_op jit(solution)/shard_map/setup/pallas_call | solution.py:324
  6.3 14.3 %first_losses.1 = (bf16[2048,4096]{1,0:T(8,128)(2,1)S(1)}, bf16[16,16,4224]{2,1,0:T(8,128)(2,1)S(1)}) custom-call(bf16[2048,256]{1,0:T(8,128)(2,1)S(1)} %get-tuple-element.34.load_ref, bf16[4096,128]{1,0:T(8,128)(2,1)S(1)} %copy-done.1, bf16[1,128]{1,0:T(2,128)(2,1)S(1)} %pad_bitcast_fusion.bar_ref, bf16[2048,4096]{1,0:T(8,128)(2,1)} %idio_ref.1, ...), custom_call_target="tpu_custom_call" | custom-call | flops 8589934592 | bytes 33554432 | tf_op jit(solution)/shard_map/first_losses/pallas_call | solution.py:355
  20.5 37.3 %all_to_all.35.pay_ref = bf16[16,16,4224]{2,1,0:T(8,128)(2,1)S(1)} all-to-all(bf16[16,16,4224]{2,1,0:T(8,128)(2,1)S(1)} %get-tuple-element.38), channel_id=1, replica_groups=mesh['y'=4,'z'=4,'x'=4,'c'=2] {'y','z'}, dimensions={0} | all-to-all | bytes 4325376 | tf_op jit(solution)/shard_map/all_to_all | solution.py:384
  58.8 9.7 %all_to_all.36.both_ref = f32[8,16,128]{2,1,0:T(8,128)S(1)} all-to-all(f32[8,16,128]{2,1,0:T(8,128)S(1)} %get-tuple-element.40), channel_id=1, replica_groups=mesh['y'=4,'z'=4,'x'=4,'c'=2] {'x','c'}, dimensions={0} | all-to-all | bytes 131072 | tf_op jit(solution)/shard_map/all_to_all | solution.py:395
  69.0 32.5 %all_to_all.37.edge_ref.weight_ref = bf16[16,16,4224]{2,1,0:T(8,128)(2,1)S(1)} all-to-all(bf16[16,16,4224]{2,1,0:T(8,128)(2,1)S(1)} %tail.2), channel_id=1, replica_groups=mesh['y'=4,'z'=4,'x'=4,'c'=2] {'y','z'}, dimensions={0} | all-to-all | bytes 4325376 | tf_op jit(solution)/shard_map/all_to_all | solution.py:405
  101.5 2.6 %gradient.5 = f32[1024,256]{1,0:T(8,128)S(1)} custom-call(bf16[2048,4096]{1,0:T(8,128)(2,1)S(1)} %get-tuple-element.37.p_ref, bf16[16,16,4224]{2,1,0:T(8,128)(2,1)S(1)} %all_to_all.37.edge_ref.weight_ref), custom_call_target="tpu_custom_call" | custom-call | flops 2147483648 | bytes 8388608 | tf_op jit(solution)/shard_map/gradient/pallas_call | solution.py:417
  104.9 2.6 %gradient.4.own_ref = f32[1024,256]{1,0:T(8,128)S(1)} custom-call(bf16[2048,4096]{1,0:T(8,128)(2,1)S(1)} %get-tuple-element.37.p_ref, bf16[16,16,4224]{2,1,0:T(8,128)(2,1)S(1)} %all_to_all.37.edge_ref.weight_ref), custom_call_target="tpu_custom_call" | custom-call | flops 2147483648 | bytes 8388608 | tf_op jit(solution)/shard_map/gradient/pallas_call | solution.py:417
  108.7 2.1 collective-permute-start.3
  111.7 6.0 %collective-permute-done.2.refs_1_ = bf16[264,256]{1,0:T(8,128)(2,1)S(1)} collective-permute-done((bf16[264,256]{1,0:T(8,128)(2,1)S(1)}, bf16[264,256]{1,0:T(8,128)(2,1)S(1)}, u32[]{:S(2)}, u32[]{:S(2)}) %collective-permute-start.2) | collective-permute-done | bytes 135200 | tf_op jit(solution)/shard_map/ppermute | solution.py:446
  118.7 2.5 collective-permute-start.7
  122.2 4.8 %collective-permute-done.7.refs_3_ = bf16[264,256]{1,0:T(8,128)(2,1)S(1)} collective-permute-done((bf16[264,256]{1,0:T(8,128)(2,1)S(1)}, bf16[264,256]{1,0:T(8,128)(2,1)S(1)}, u32[]{:S(2)}, u32[]{:S(2)}) %collective-permute-start.7) | collective-permute-done | bytes 135200 | tf_op jit(solution)/shard_map/ppermute | solution.py:459
  127.0 2.2 collective-permute-done.6.refs_2_
  129.2 1.2 collective-permute-done.5.refs_1_
  130.5 1.2 collective-permute-done.9.refs_5_
  131.7 1.3 update.2
  133.1 6.0 %losses.1 = bf16[16,16,4224]{2,1,0:T(8,128)(2,1)S(1)} custom-call(bf16[2048,4096]{1,0:T(8,128)(2,1)S(1)} %get-tuple-element.37.p_ref, bf16[256,2048]{1,0:T(8,128)(2,1)S(1)} %get-tuple-element.50.expot_ref, bf16[256,128]{1,0:T(8,128)(2,1)S(1)} %get-tuple-element.51.edge_ref), custom_call_target="tpu_custom_call" | custom-call | flops 4294967296 | bytes 16777216 | tf_op jit(solution)/shard_map/losses/pallas_call | solution.py:374
  139.1 32.6 %all_to_all.38.pay_ref = bf16[16,16,4224]{2,1,0:T(8,128)(2,1)S(1)} all-to-all(bf16[16,16,4224]{2,1,0:T(8,128)(2,1)S(1)} %losses.1), channel_id=1, replica_groups=mesh['y'=4,'z'=4,'x'=4,'c'=2] {'y','z'}, dimensions={0} | all-to-all | bytes 4325376 | tf_op jit(solution)/shard_map/all_to_all | solution.py:384
  172.7 8.0 %all_to_all.39.both_ref = f32[8,16,128]{2,1,0:T(8,128)S(1)} all-to-all(f32[8,16,128]{2,1,0:T(8,128)S(1)} %get-tuple-element.53), channel_id=1, replica_groups=mesh['y'=4,'z'=4,'x'=4,'c'=2] {'x','c'}, dimensions={0} | all-to-all | bytes 131072 | tf_op jit(solution)/shard_map/all_to_all | solution.py:395
  181.2 32.5 %all_to_all.40.edge_ref.weight_ref = bf16[16,16,4224]{2,1,0:T(8,128)(2,1)S(1)} all-to-all(bf16[16,16,4224]{2,1,0:T(8,128)(2,1)S(1)} %tail.3), channel_id=1, replica_groups=mesh['y'=4,'z'=4,'x'=4,'c'=2] {'y','z'}, dimensions={0} | all-to-all | bytes 4325376 | tf_op jit(solution)/shard_map/all_to_all | solution.py:405
  213.7 2.6 %gradient.7 = f32[1024,256]{1,0:T(8,128)S(1)} custom-call(bf16[2048,4096]{1,0:T(8,128)(2,1)S(1)} %get-tuple-element.37.p_ref, bf16[16,16,4224]{2,1,0:T(8,128)(2,1)S(1)} %all_to_all.40.edge_ref.weight_ref), custom_call_target="tpu_custom_call" | custom-call | flops 2147483648 | bytes 8388608 | tf_op jit(solution)/shard_map/gradient/pallas_call | solution.py:417
  217.0 2.6 %gradient.6.own_ref = f32[1024,256]{1,0:T(8,128)S(1)} custom-call(bf16[2048,4096]{1,0:T(8,128)(2,1)S(1)} %get-tuple-element.37.p_ref, bf16[16,16,4224]{2,1,0:T(8,128)(2,1)S(1)} %all_to_all.40.edge_ref.weight_ref), custom_call_target="tpu_custom_call" | custom-call | flops 2147483648 | bytes 8388608 | tf_op jit(solution)/shard_map/gradient/pallas_call | solution.py:417
  220.8 2.0 collective-permute-start.15
  223.8 6.0 %collective-permute-done.14.refs_1_ = bf16[264,256]{1,0:T(8,128)(2,1)S(1)} collective-permute-done((bf16[264,256]{1,0:T(8,128)(2,1)S(1)}, bf16[264,256]{1,0:T(8,128)(2,1)S(1)}, u32[]{:S(2)}, u32[]{:S(2)}) %collective-permute-start.14) | collective-permute-done | bytes 135200 | tf_op jit(solution)/shard_map/ppermute | solution.py:446
  230.8 2.5 collective-permute-start.19
  234.3 4.8 %collective-permute-done.19.refs_3_ = bf16[264,256]{1,0:T(8,128)(2,1)S(1)} collective-permute-done((bf16[264,256]{1,0:T(8,128)(2,1)S(1)}, bf16[264,256]{1,0:T(8,128)(2,1)S(1)}, u32[]{:S(2)}, u32[]{:S(2)}) %collective-permute-start.19) | collective-permute-done | bytes 135200 | tf_op jit(solution)/shard_map/ppermute | solution.py:459
  239.1 2.2 collective-permute-done.18.refs_2_
  241.3 1.2 collective-permute-done.17.refs_1_
  242.6 1.2 collective-permute-done.21.refs_5_
  243.8 1.5 update.3
  245.3 3.5 %all-to-all-start.6 = ((f32[16,1,256]{2,1,0:T(1,128)}), f32[16,1,256]{2,1,0:T(1,128)S(1)}, u32[]{:S(2)}, u32[]{:S(2)}) async-start(f32[16,1,256]{2,1,0:T(1,128)} %get-tuple-element.63), calls=%async_computation.6 | async-start | bytes 32768 | tf_op jit(solution)/shard_map/all_to_all | solution.py:475
  249.4 7.0 %all-to-all-done.6.totals_ref = f32[16,1,256]{2,1,0:T(1,128)S(1)} async-done(((f32[16,1,256]{2,1,0:T(1,128)}), f32[16,1,256]{2,1,0:T(1,128)S(1)}, u32[]{:S(2)}, u32[]{:S(2)}) %all-to-all-start.6) | async-done | bytes 16416 | tf_op jit(solution)/shard_map/all_to_all | solution.py:475
  256.4 1.9 scale.1
  (54 shorter events, 14.8 us)
Async XLA Ops:
  1.4 0.7 copy-start
  2.1 4.1 %copy-start.1 = (bf16[4096,128]{1,0:T(8,128)(2,1)S(1)}, bf16[4096,128]{1,0:T(8,128)(2,1)}, u32[]{:S(2)}) copy-start(bf16[4096,128]{1,0:T(8,128)(2,1)} %fac_ref.1) | copy-start | bytes 3145732
  104.2 3.4 %collective-permute-start = (f32[1024,256]{1,0:T(8,128)S(1)}, f32[1024,256]{1,0:T(8,128)S(1)}, u32[]{:S(2)}, u32[]{:S(2)}) collective-permute-start(f32[1024,256]{1,0:T(8,128)S(1)} %gradient.5), channel_id=1, source_target_pairs={{0,1},{1,0},{2,3},{3,2},{4,5},{5,4},{6,7},{7,6},{8,9},{9,8},{10,11... | collective-permute-start | bytes 3145736 | tf_op jit(solution)/shard_map/ppermute | solution.py:429
  104.4 3.2 %collective-permute-start.1 = (f32[8,256]{1,0:T(8,128)S(1)}, f32[8,256]{1,0:T(8,128)S(1)}, u32[]{:S(2)}, u32[]{:S(2)}) collective-permute-start(f32[8,256]{1,0:T(8,128)S(1)} %get-tuple-element.42.soft_ref), channel_id=1, source_target_pairs={{0,1},{1,0},{2,3},{3,2},{4,5},{5,4},{6,7},{7,6},{8,9},{9,8},{10,11... | collective-permute-start | bytes 24584 | tf_op jit(solution)/shard_map/ppermute | solution.py:430
  108.0 9.7 %collective-permute-start.2 = (bf16[264,256]{1,0:T(8,128)(2,1)S(1)}, bf16[264,256]{1,0:T(8,128)(2,1)S(1)}, u32[]{:S(2)}, u32[]{:S(2)}) collective-permute-start(bf16[264,256]{1,0:T(8,128)(2,1)S(1)} %get-tuple-element.44), channel_id=1, source_target_pairs={{0,2},{2,4},{4,6},{6,0},{1,3},{3,5},{5,7},{7,1},{8,10},{10,12},{12... | collective-permute-start | bytes 405512 | tf_op jit(solution)/shard_map/ppermute | solution.py:446
  108.7 9.1 %collective-permute-start.3 = (bf16[264,256]{1,0:T(8,128)(2,1)S(1)}, bf16[264,256]{1,0:T(8,128)(2,1)S(1)}, u32[]{:S(2)}, u32[]{:S(2)}) collective-permute-start(bf16[264,256]{1,0:T(8,128)(2,1)S(1)} %get-tuple-element.45), channel_id=1, source_target_pairs={{0,4},{2,6},{4,0},{6,2},{1,5},{3,7},{5,1},{7,3},{8,12},{10,14},{12... | collective-permute-start | bytes 405512 | tf_op jit(solution)/shard_map/ppermute | solution.py:446
  110.7 7.6 %collective-permute-start.4 = (bf16[264,256]{1,0:T(8,128)(2,1)S(1)}, bf16[264,256]{1,0:T(8,128)(2,1)S(1)}, u32[]{:S(2)}, u32[]{:S(2)}) collective-permute-start(bf16[264,256]{1,0:T(8,128)(2,1)S(1)} %get-tuple-element.46), channel_id=1, source_target_pairs={{0,6},{2,0},{4,2},{6,4},{1,7},{3,1},{5,3},{7,5},{8,14},{10,8},{12,... | collective-permute-start | bytes 405512 | tf_op jit(solution)/shard_map/ppermute | solution.py:446
  118.7 8.3 %collective-permute-start.7 = (bf16[264,256]{1,0:T(8,128)(2,1)S(1)}, bf16[264,256]{1,0:T(8,128)(2,1)S(1)}, u32[]{:S(2)}, u32[]{:S(2)}) collective-permute-start(bf16[264,256]{1,0:T(8,128)(2,1)S(1)} %get-tuple-element.47.refs_0_), channel_id=1, source_target_pairs={{0,6},{2,0},{4,2},{6,4},{1,7},{3,1},{5,3},{7,5},{8,14},{10,8},{12,... | collective-permute-start | bytes 405512 | tf_op jit(solution)/shard_map/ppermute | solution.py:459
  121.2 8.0 %collective-permute-start.6 = (bf16[264,256]{1,0:T(8,128)(2,1)S(1)}, bf16[264,256]{1,0:T(8,128)(2,1)S(1)}, u32[]{:S(2)}, u32[]{:S(2)}) collective-permute-start(bf16[264,256]{1,0:T(8,128)(2,1)S(1)} %get-tuple-element.47.refs_0_), channel_id=1, source_target_pairs={{0,4},{2,6},{4,0},{6,2},{1,5},{3,7},{5,1},{7,3},{8,12},{10,14},{12... | collective-permute-start | bytes 405512 | tf_op jit(solution)/shard_map/ppermute | solution.py:459
  121.2 9.2 %collective-permute-start.5 = (bf16[264,256]{1,0:T(8,128)(2,1)S(1)}, bf16[264,256]{1,0:T(8,128)(2,1)S(1)}, u32[]{:S(2)}, u32[]{:S(2)}) collective-permute-start(bf16[264,256]{1,0:T(8,128)(2,1)S(1)} %get-tuple-element.47.refs_0_), channel_id=1, source_target_pairs={{0,2},{2,4},{4,6},{6,0},{1,3},{3,5},{5,7},{7,1},{8,10},{10,12},{12... | collective-permute-start | bytes 405512 | tf_op jit(solution)/shard_map/ppermute | solution.py:459
  122.2 8.2 %collective-permute-start.8 = (bf16[264,256]{1,0:T(8,128)(2,1)S(1)}, bf16[264,256]{1,0:T(8,128)(2,1)S(1)}, u32[]{:S(2)}, u32[]{:S(2)}) collective-permute-start(bf16[264,256]{1,0:T(8,128)(2,1)S(1)} %get-tuple-element.47.refs_0_), channel_id=1, source_target_pairs={{0,1},{1,0},{2,3},{3,2},{4,5},{5,4},{6,7},{7,6},{8,9},{9,8},{10,11... | collective-permute-start | bytes 405512 | tf_op jit(solution)/shard_map/ppermute | solution.py:460
  127.0 3.4 %collective-permute-start.11 = (bf16[264,256]{1,0:T(8,128)(2,1)S(1)}, bf16[264,256]{1,0:T(8,128)(2,1)S(1)}, u32[]{:S(2)}, u32[]{:S(2)}) collective-permute-start(bf16[264,256]{1,0:T(8,128)(2,1)S(1)} %collective-permute-done.7.refs_3_), channel_id=1, source_target_pairs={{0,1},{1,0},{2,3},{3,2},{4,5},{5,4},{6,7},{7,6},{8,9},{9,8},{10,11... | collective-permute-start | bytes 405512 | tf_op jit(solution)/shard_map/ppermute | solution.py:460
  129.2 1.4 collective-permute-start.10
  130.4 1.4 collective-permute-start.9
  216.3 3.4 %collective-permute-start.12 = (f32[1024,256]{1,0:T(8,128)S(1)}, f32[1024,256]{1,0:T(8,128)S(1)}, u32[]{:S(2)}, u32[]{:S(2)}) collective-permute-start(f32[1024,256]{1,0:T(8,128)S(1)} %gradient.7), channel_id=1, source_target_pairs={{0,1},{1,0},{2,3},{3,2},{4,5},{5,4},{6,7},{7,6},{8,9},{9,8},{10,11... | collective-permute-start | bytes 3145736 | tf_op jit(solution)/shard_map/ppermute | solution.py:429
  216.5 3.2 %collective-permute-start.13 = (f32[8,256]{1,0:T(8,128)S(1)}, f32[8,256]{1,0:T(8,128)S(1)}, u32[]{:S(2)}, u32[]{:S(2)}) collective-permute-start(f32[8,256]{1,0:T(8,128)S(1)} %get-tuple-element.55.soft_ref), channel_id=1, source_target_pairs={{0,1},{1,0},{2,3},{3,2},{4,5},{5,4},{6,7},{7,6},{8,9},{9,8},{10,11... | collective-permute-start | bytes 24584 | tf_op jit(solution)/shard_map/ppermute | solution.py:430
  220.1 9.7 %collective-permute-start.14 = (bf16[264,256]{1,0:T(8,128)(2,1)S(1)}, bf16[264,256]{1,0:T(8,128)(2,1)S(1)}, u32[]{:S(2)}, u32[]{:S(2)}) collective-permute-start(bf16[264,256]{1,0:T(8,128)(2,1)S(1)} %get-tuple-element.57), channel_id=1, source_target_pairs={{0,2},{2,4},{4,6},{6,0},{1,3},{3,5},{5,7},{7,1},{8,10},{10,12},{12... | collective-permute-start | bytes 405512 | tf_op jit(solution)/shard_map/ppermute | solution.py:446
  220.8 9.1 %collective-permute-start.15 = (bf16[264,256]{1,0:T(8,128)(2,1)S(1)}, bf16[264,256]{1,0:T(8,128)(2,1)S(1)}, u32[]{:S(2)}, u32[]{:S(2)}) collective-permute-start(bf16[264,256]{1,0:T(8,128)(2,1)S(1)} %get-tuple-element.58), channel_id=1, source_target_pairs={{0,4},{2,6},{4,0},{6,2},{1,5},{3,7},{5,1},{7,3},{8,12},{10,14},{12... | collective-permute-start | bytes 405512 | tf_op jit(solution)/shard_map/ppermute | solution.py:446
  222.8 7.6 %collective-permute-start.16 = (bf16[264,256]{1,0:T(8,128)(2,1)S(1)}, bf16[264,256]{1,0:T(8,128)(2,1)S(1)}, u32[]{:S(2)}, u32[]{:S(2)}) collective-permute-start(bf16[264,256]{1,0:T(8,128)(2,1)S(1)} %get-tuple-element.59), channel_id=1, source_target_pairs={{0,6},{2,0},{4,2},{6,4},{1,7},{3,1},{5,3},{7,5},{8,14},{10,8},{12,... | collective-permute-start | bytes 405512 | tf_op jit(solution)/shard_map/ppermute | solution.py:446
  230.8 8.3 %collective-permute-start.19 = (bf16[264,256]{1,0:T(8,128)(2,1)S(1)}, bf16[264,256]{1,0:T(8,128)(2,1)S(1)}, u32[]{:S(2)}, u32[]{:S(2)}) collective-permute-start(bf16[264,256]{1,0:T(8,128)(2,1)S(1)} %get-tuple-element.60.refs_0_), channel_id=1, source_target_pairs={{0,6},{2,0},{4,2},{6,4},{1,7},{3,1},{5,3},{7,5},{8,14},{10,8},{12,... | collective-permute-start | bytes 405512 | tf_op jit(solution)/shard_map/ppermute | solution.py:459
  233.3 8.0 %collective-permute-start.18 = (bf16[264,256]{1,0:T(8,128)(2,1)S(1)}, bf16[264,256]{1,0:T(8,128)(2,1)S(1)}, u32[]{:S(2)}, u32[]{:S(2)}) collective-permute-start(bf16[264,256]{1,0:T(8,128)(2,1)S(1)} %get-tuple-element.60.refs_0_), channel_id=1, source_target_pairs={{0,4},{2,6},{4,0},{6,2},{1,5},{3,7},{5,1},{7,3},{8,12},{10,14},{12... | collective-permute-start | bytes 405512 | tf_op jit(solution)/shard_map/ppermute | solution.py:459
  233.3 9.1 %collective-permute-start.17 = (bf16[264,256]{1,0:T(8,128)(2,1)S(1)}, bf16[264,256]{1,0:T(8,128)(2,1)S(1)}, u32[]{:S(2)}, u32[]{:S(2)}) collective-permute-start(bf16[264,256]{1,0:T(8,128)(2,1)S(1)} %get-tuple-element.60.refs_0_), channel_id=1, source_target_pairs={{0,2},{2,4},{4,6},{6,0},{1,3},{3,5},{5,7},{7,1},{8,10},{10,12},{12... | collective-permute-start | bytes 405512 | tf_op jit(solution)/shard_map/ppermute | solution.py:459
  234.3 8.2 %collective-permute-start.20 = (bf16[264,256]{1,0:T(8,128)(2,1)S(1)}, bf16[264,256]{1,0:T(8,128)(2,1)S(1)}, u32[]{:S(2)}, u32[]{:S(2)}) collective-permute-start(bf16[264,256]{1,0:T(8,128)(2,1)S(1)} %get-tuple-element.60.refs_0_), channel_id=1, source_target_pairs={{0,1},{1,0},{2,3},{3,2},{4,5},{5,4},{6,7},{7,6},{8,9},{9,8},{10,11... | collective-permute-start | bytes 405512 | tf_op jit(solution)/shard_map/ppermute | solution.py:460
  239.1 3.4 %collective-permute-start.23 = (bf16[264,256]{1,0:T(8,128)(2,1)S(1)}, bf16[264,256]{1,0:T(8,128)(2,1)S(1)}, u32[]{:S(2)}, u32[]{:S(2)}) collective-permute-start(bf16[264,256]{1,0:T(8,128)(2,1)S(1)} %collective-permute-done.19.refs_3_), channel_id=1, source_target_pairs={{0,1},{1,0},{2,3},{3,2},{4,5},{5,4},{6,7},{7,6},{8,9},{9,8},{10,11... | collective-permute-start | bytes 405512 | tf_op jit(solution)/shard_map/ppermute | solution.py:460
  241.3 1.4 collective-permute-start.22
  242.5 1.4 collective-permute-start.21
  245.3 11.1 %all-to-all-start.6 = ((f32[16,1,256]{2,1,0:T(1,128)}), f32[16,1,256]{2,1,0:T(1,128)S(1)}, u32[]{:S(2)}, u32[]{:S(2)}) async-start(f32[16,1,256]{2,1,0:T(1,128)} %get-tuple-element.63), calls=%async_computation.6 | async-start | bytes 32768 | tf_op jit(solution)/shard_map/all_to_all | solution.py:475

commit v5 on v4

--- a/solution.py
+++ b/solution.py
@@ -11,6 +11,7 @@
 STEPS = 2
 OBL = ("y", "z")
 SCN = ("x", "c")
+PLANE = ("y", "z", "c")
 IDIO_SCALE = 0.8
 LEVEL = 0.99
 QUANTILE = 2.326
@@ -141,13 +142,44 @@
     put_codes(jnp.dot(expot_ref[...], p_ref[:, cols], preferred_element_type=f32), edge_ref, pay_ref, cols)
 
 
+def mid_kernel(pay_ref, out_ref, part_ref):
+    fewer = out_ref.shape[0]
+    count = pay_ref.shape[0] // fewer
+    wide = part_ref.shape[2]
+    piece = min(1024, wide)
+    lane = lax.broadcasted_iota(jnp.int32, (pay_ref.shape[1], 128), 1)
+    for q in range(fewer):
+        edges = [pay_ref[k * fewer + q, :, wide:].astype(f32) for k in range(count)]
+        spans = [edge[:, 0:1] for edge in edges]
+        offset = 0.5 * sum(spans)
+        factors = [span * (1.0 / SPAN) for span in spans]
+        low, high = jnp.inf, -jnp.inf
+        for at in range(0, wide, piece):
+            codes = [pay_ref[k * fewer + q, :, at : at + piece].astype(f32) for k in range(count)]
+            part = sum(jnp.log(code) * factor for code, factor in zip(codes, factors)) + offset
+            part_ref[q, :, at : at + piece] = part
+            low = jnp.minimum(low, jnp.min(part, axis=1, keepdims=True))
+            high = jnp.maximum(high, jnp.max(part, axis=1, keepdims=True))
+        span = jnp.maximum(jnp.maximum(high - low, jnp.abs(low) * (1.0 / 64.0)), 1e-30)
+        base = low.astype(bf16).astype(f32)
+        span = (span * 1.02).astype(bf16).astype(f32)
+        for at in range(0, wide, piece):
+            part = part_ref[q, :, at : at + piece]
+            out_ref[q, :, at : at + piece] = jnp.exp((part - base) * (SPAN / span) - 0.5 * SPAN).astype(bf16)
+        total = sum(edge[:, 1:2] + edge[:, 2:3] + edge[:, 3:4] for edge in edges)
+        edge = jnp.zeros(lane.shape, f32)
+        for at, value in enumerate([base, span] + split3(total)):
+            edge = jnp.where(lane == at, value, edge)
+        out_ref[q, :, wide:] = edge.astype(bf16)
+
+
 def sum_kernel(pay_ref, losses_ref, both_ref):
     count = pay_ref.shape[0]
     wide = losses_ref.shape[1]
     edges = [pay_ref[k, :, wide:].astype(f32) for k in range(count)]
-    spans = [edge[:, 0:1] for edge in edges]
-    offset = 0.5 * sum(spans)
-    scale = 0.5 / sum(edge[:, 1:2] + edge[:, 2:3] + edge[:, 3:4] for edge in edges)
+    spans = [edge[:, 1:2] for edge in edges]
+    offset = sum(edge[:, 0:1] for edge in edges) + 0.5 * sum(spans)
+    scale = 0.5 / sum(edge[:, 2:3] + edge[:, 3:4] + edge[:, 4:5] for edge in edges)
     factors = [span * (1.0 / SPAN) for span in spans]
     piece = min(1024, wide)
     total = 0.0
@@ -294,6 +326,18 @@
     return pl.BlockSpec(shape, lambda *_: (0,) * len(shape))
 
 
+def groups_of(side, n_x):
+    span = range(side)
+    plane = lambda y, z, c: (y * side + z) * 2 + c
+    along_y = lambda c: [[plane(y, z, c) for y in span] for z in span]
+    along_z = lambda c: [[plane(y, z, c) for z in span] for y in span]
+    place = lambda y, z, x, c: ((y * side + z) * n_x + x) * 2 + c
+    same = [
+        [place(a, b, x, 0) for x in range(n_x)] + [place(b, a, x, 1) for x in range(n_x)] for a in span for b in span
+    ]
+    return along_y(0) + along_z(1), along_z(0) + along_y(1), same
+
+
 def rounded(value):
     return lax.reduce_precision(value, 8, 7)
 
@@ -301,6 +345,8 @@
 def on_device(factors, idiosyncratic, loadings, rating, barrier, loss_given, sector, allowed, holdings):
     sds = jax.ShapeDtypeStruct
     n_obl, n_x, n_c = lax.axis_size(OBL), lax.axis_size("x"), lax.axis_size("c")
+    side = lax.axis_size("y")
+    first, second, same = groups_of(side, n_x)
     obl_dev, scn_dev = idiosyncratic.shape
     mandates = holdings.shape[1]
     obligors = obl_dev * n_obl
@@ -381,7 +427,19 @@
                 nbytes=obl_dev * scn_dev * 2,
                 name="losses",
             )(prob, near(expot), near(edge))
-        pay = lax.all_to_all(pay, OBL, 0, 0, tiled=True)
+        pay = lax.all_to_all(pay, PLANE, 0, 0, axis_index_groups=first, tiled=True)
+        few = sds((side, mr, scn_dev + 128), bf16)
+        pay = call(
+            mid_kernel,
+            (1,),
+            [VMEM],
+            VMEM,
+            few,
+            scratch=[pltpu.VMEM((side, mr, scn_dev), f32)],
+            nbytes=mandates * scn_dev * 2,
+            name="mid",
+        )(pay)
+        pay = lax.all_to_all(pay, PLANE, 0, 0, axis_index_groups=second, tiled=True)
         n_scn = n_x * n_c
         losses, both = call(
             sum_kernel,
@@ -392,17 +450,19 @@
             nbytes=mandates * scn_dev * 2,
             name="sum",
         )(pay)
-        both = lax.all_to_all(both, SCN, 0, 0, tiled=True)
+        both = lax.all_to_all(both, OBL + SCN, 0, 0, axis_index_groups=same, tiled=True)
         weight = call(
             functools.partial(tail_kernel, tail_scale, scenarios),
             (1,),
             [VMEM, VMEM],
             VMEM,
-            pay_shape,
+            few,
             nbytes=mandates * scn_dev * 2,
             name="tail",
         )(near(losses), both)
-        weight = lax.all_to_all(weight, OBL, 0, 0, tiled=True)
+        weight = lax.all_to_all(weight, PLANE, 0, 0, axis_index_groups=second, tiled=True)
+        weight = jnp.broadcast_to(weight[None], (side, *weight.shape)).reshape(pay_shape.shape)
+        weight = lax.all_to_all(weight, PLANE, 0, 0, axis_index_groups=first, tiled=True)
         soft, stat = call(
             heads_kernel,
             (1,),

time: 259 us -> 258 us (level)
  blocking collectives: 153 us -> 150 us
    all_to_all x6 -> x10, blocking collectives: 153 us -> 150 us  [the longest x2 40.6 us: on_device(): pay = lax.all_to_all(pay, PLANE, 0, 0, axis_index_groups=first, tiled=True)]
  transfers between devices with their start and end apart: 25 -> 25, of which waited for: 15 -> 13; matrix products, arithmetic and copies ran while one was open for 0% -> 0% of each run, Pallas kernels for 2% -> 2%
where the time goes in v5:
time: 258 us
  blocking collectives  150 us (58%)
  Pallas kernels  45.7 us (18%)
  waiting for transfers between devices  39.3 us (15%)
  starting transfers between devices  19.8 us (8%)
    all_to_all x2, blocking collectives, on_device(): pay = lax.all_to_all(pay, PLANE, 0, 0, axis_index_groups=first, tiled=True)  40.6 us
    all_to_all x2, blocking collectives, on_device(): lax.all_to_all(weight, PLANE, 0, 0, axis_index_groups=first, tiled=True)  38.6 us
    all_to_all x2, blocking collectives, on_device(): lax.all_to_all(weight, PLANE, 0, 0, axis_index_groups=second, tiled=True)  29.4 us
    all_to_all x2, blocking collectives, on_device(): pay = lax.all_to_all(pay, PLANE, 0, 0, axis_index_groups=second, tiled=True)  23.8 us
    all_to_all x2, blocking collectives, on_device(): lax.all_to_all(both, OBL + SCN, 0, 0, axis_index_groups=same, tiled=True)  17.2 us
    ppermute x6, waiting for transfers between devices, on_device(): slots[k] = lax.ppermute(pay, 'x', hops[k])  16.7 us
    pallas_call x1, Pallas kernels, on_device(): call(first_losses_kernel, (scn_dev // wide,), [VMEM, pl.BlockSpec((wide,...  14.3 us
    ppermute x6, waiting for transfers between devices, on_device(): slots[k] = lax.ppermute(slots[k], 'x', hops[k])  12.9 us
  transfers between devices with their start and end apart: 25, of which 13 were waited for; matrix products, arithmetic and copies ran while one was open for 0% of the time, Pallas kernels for 2%

profile of v5, /device:TPU:0, one launch (start us, length us, event | category | flops | bytes accessed | tf_op | source)
XLA Modules:
  0.0 257.6 jit_solution(15886570109507064770)
XLA Ops:
  2.1 4.1 %setup.1 = (f32[2048,256]{1,0:T(8,128)S(1)}, f32[2048,256]{1,0:T(8,128)S(1)}, bf16[2048,256]{1,0:T(8,128)(2,1)S(1)}, bf16[256,2048]{1,0:T(8,128)(2,1)S(1)}, bf16[256,128]{1,0:T(8,128)(2,1)S(1)}) custom-call(f32[2048,256]{1,0:T(8,128)} %hold_ref.1, f32[1,2048]{1,0:T(1,128)} %bitcast.11, s32[1,2048]{1,0:T(1,128)} %bitcast.12, s32[1,2048]{1,0:T(1,128)} %bitcast.13, ...), custom_call_target="tpu_custom_call" | custom-call | bytes 6291456 | tf_op jit(solution)/shard_map/setup/pallas_call | solution.py:370
  6.3 14.3 %first_losses.1 = (bf16[2048,4096]{1,0:T(8,128)(2,1)S(1)}, bf16[16,16,4224]{2,1,0:T(8,128)(2,1)S(1)}) custom-call(bf16[2048,256]{1,0:T(8,128)(2,1)S(1)} %get-tuple-element.34.load_ref, bf16[4096,128]{1,0:T(8,128)(2,1)S(1)} %copy-done.1, bf16[1,128]{1,0:T(2,128)(2,1)S(1)} %pad_bitcast_fusion.bar_ref, bf16[2048,4096]{1,0:T(8,128)(2,1)} %idio_ref.1, ...), custom_call_target="tpu_custom_call" | custom-call | flops 8589934592 | bytes 33554432 | tf_op jit(solution)/shard_map/first_losses/pallas_call | solution.py:401
  20.5 21.2 %all_to_all.55.pay_ref = bf16[16,16,4224]{2,1,0:T(8,128)(2,1)S(1)} all-to-all(bf16[16,16,4224]{2,1,0:T(8,128)(2,1)S(1)} %get-tuple-element.38), channel_id=1, replica_groups={{0,32,64,96},{8,40,72,104},{16,48,80,112},{24,56,88,120},{1,9,17,25},{3..., dimensions={0} | all-to-all | bytes 4325376 | tf_op jit(solution)/shard_map/all_to_all | solution.py:430
  43.0 13.3 %all_to_all.56.pay_ref = bf16[4,16,4224]{2,1,0:T(8,128)(2,1)S(1)} all-to-all(bf16[4,16,4224]{2,1,0:T(8,128)(2,1)S(1)} %mid.2), channel_id=1, replica_groups={{0,8,16,24},{32,40,48,56},{64,72,80,88},{96,104,112,120},{1,33,65,97},{..., dimensions={0} | all-to-all | bytes 1081344 | tf_op jit(solution)/shard_map/all_to_all | solution.py:442
  56.8 9.4 %all_to_all.57.both_ref = f32[8,16,128]{2,1,0:T(8,128)S(1)} all-to-all(f32[8,16,128]{2,1,0:T(8,128)S(1)} %get-tuple-element.40), channel_id=1, replica_groups={{0,2,4,6,1,3,5,7},{8,10,12,14,33,35,37,39},{16,18,20,22,65,67,69,71},{2..., dimensions={0} | all-to-all | bytes 131072 | tf_op jit(solution)/shard_map/all_to_all | solution.py:453
  66.7 14.7 %all_to_all.58 = bf16[4,16,4224]{2,1,0:T(8,128)(2,1)S(1)} all-to-all(bf16[4,16,4224]{2,1,0:T(8,128)(2,1)S(1)} %tail.2), channel_id=1, replica_groups={{0,8,16,24},{32,40,48,56},{64,72,80,88},{96,104,112,120},{1,33,65,97},{..., dimensions={0} | all-to-all | bytes 1081344 | tf_op jit(solution)/shard_map/all_to_all | solution.py:463
  81.5 19.3 %all_to_all.59.edge_ref.weight_ref = bf16[16,16,4224]{2,1,0:T(8,128)(2,1)S(1)} all-to-all(bf16[16,16,4224]{2,1,0:T(8,128)(2,1)S(1)} %bitcast.9), channel_id=1, replica_groups={{0,32,64,96},{8,40,72,104},{16,48,80,112},{24,56,88,120},{1,9,17,25},{3..., dimensions={0} | all-to-all | bytes 4325376 | tf_op jit(solution)/shard_map/all_to_all | solution.py:465
  100.9 2.6 %gradient.5 = f32[1024,256]{1,0:T(8,128)S(1)} custom-call(bf16[2048,4096]{1,0:T(8,128)(2,1)S(1)} %get-tuple-element.37.p_ref, bf16[16,16,4224]{2,1,0:T(8,128)(2,1)S(1)} %all_to_all.59.edge_ref.weight_ref), custom_call_target="tpu_custom_call" | custom-call | flops 2147483648 | bytes 8388608 | tf_op jit(solution)/shard_map/gradient/pallas_call | solution.py:477
  104.3 2.6 %gradient.4.own_ref = f32[1024,256]{1,0:T(8,128)S(1)} custom-call(bf16[2048,4096]{1,0:T(8,128)(2,1)S(1)} %get-tuple-element.37.p_ref, bf16[16,16,4224]{2,1,0:T(8,128)(2,1)S(1)} %all_to_all.59.edge_ref.weight_ref), custom_call_target="tpu_custom_call" | custom-call | flops 2147483648 | bytes 8388608 | tf_op jit(solution)/shard_map/gradient/pallas_call | solution.py:477
  108.1 2.0 collective-permute-start.3
  111.2 5.8 %collective-permute-done.2.refs_1_ = bf16[264,256]{1,0:T(8,128)(2,1)S(1)} collective-permute-done((bf16[264,256]{1,0:T(8,128)(2,1)S(1)}, bf16[264,256]{1,0:T(8,128)(2,1)S(1)}, u32[]{:S(2)}, u32[]{:S(2)}) %collective-permute-start.2) | collective-permute-done | bytes 135200 | tf_op jit(solution)/shard_map/ppermute | solution.py:506
  118.0 2.7 %collective-permute-start.7 = (bf16[264,256]{1,0:T(8,128)(2,1)S(1)}, bf16[264,256]{1,0:T(8,128)(2,1)S(1)}, u32[]{:S(2)}, u32[]{:S(2)}) collective-permute-start(bf16[264,256]{1,0:T(8,128)(2,1)S(1)} %get-tuple-element.47.refs_0_), channel_id=1, source_target_pairs={{0,6},{2,0},{4,2},{6,4},{1,7},{3,1},{5,3},{7,5},{8,14},{10,8},{12,... | collective-permute-start | bytes 405512 | tf_op jit(solution)/shard_map/ppermute | solution.py:519
  121.7 5.0 %collective-permute-done.7.refs_3_ = bf16[264,256]{1,0:T(8,128)(2,1)S(1)} collective-permute-done((bf16[264,256]{1,0:T(8,128)(2,1)S(1)}, bf16[264,256]{1,0:T(8,128)(2,1)S(1)}, u32[]{:S(2)}, u32[]{:S(2)}) %collective-permute-start.7) | collective-permute-done | bytes 135200 | tf_op jit(solution)/shard_map/ppermute | solution.py:519
  126.6 2.0 collective-permute-done.6.refs_2_
  128.7 1.4 collective-permute-done.5.refs_1_
  132.7 6.0 %losses.1 = bf16[16,16,4224]{2,1,0:T(8,128)(2,1)S(1)} custom-call(bf16[2048,4096]{1,0:T(8,128)(2,1)S(1)} %get-tuple-element.37.p_ref, bf16[256,2048]{1,0:T(8,128)(2,1)S(1)} %get-tuple-element.50.expot_ref, bf16[256,128]{1,0:T(8,128)(2,1)S(1)} %get-tuple-element.51.edge_ref), custom_call_target="tpu_custom_call" | custom-call | flops 4294967296 | bytes 16777216 | tf_op jit(solution)/shard_map/losses/pallas_call | solution.py:420
  138.7 19.3 %all_to_all.60.pay_ref = bf16[16,16,4224]{2,1,0:T(8,128)(2,1)S(1)} all-to-all(bf16[16,16,4224]{2,1,0:T(8,128)(2,1)S(1)} %losses.1), channel_id=1, replica_groups={{0,32,64,96},{8,40,72,104},{16,48,80,112},{24,56,88,120},{1,9,17,25},{3..., dimensions={0} | all-to-all | bytes 4325376 | tf_op jit(solution)/shard_map/all_to_all | solution.py:430
  159.3 10.5 %all_to_all.61.pay_ref = bf16[4,16,4224]{2,1,0:T(8,128)(2,1)S(1)} all-to-all(bf16[4,16,4224]{2,1,0:T(8,128)(2,1)S(1)} %mid.3), channel_id=1, replica_groups={{0,8,16,24},{32,40,48,56},{64,72,80,88},{96,104,112,120},{1,33,65,97},{..., dimensions={0} | all-to-all | bytes 1081344 | tf_op jit(solution)/shard_map/all_to_all | solution.py:442
  170.3 7.7 %all_to_all.62.both_ref = f32[8,16,128]{2,1,0:T(8,128)S(1)} all-to-all(f32[8,16,128]{2,1,0:T(8,128)S(1)} %get-tuple-element.53), channel_id=1, replica_groups={{0,2,4,6,1,3,5,7},{8,10,12,14,33,35,37,39},{16,18,20,22,65,67,69,71},{2..., dimensions={0} | all-to-all | bytes 131072 | tf_op jit(solution)/shard_map/all_to_all | solution.py:453
  178.5 14.7 %all_to_all.63 = bf16[4,16,4224]{2,1,0:T(8,128)(2,1)S(1)} all-to-all(bf16[4,16,4224]{2,1,0:T(8,128)(2,1)S(1)} %tail.3), channel_id=1, replica_groups={{0,8,16,24},{32,40,48,56},{64,72,80,88},{96,104,112,120},{1,33,65,97},{..., dimensions={0} | all-to-all | bytes 1081344 | tf_op jit(solution)/shard_map/all_to_all | solution.py:463
  193.4 19.3 %all_to_all.64.edge_ref.weight_ref = bf16[16,16,4224]{2,1,0:T(8,128)(2,1)S(1)} all-to-all(bf16[16,16,4224]{2,1,0:T(8,128)(2,1)S(1)} %bitcast.10), channel_id=1, replica_groups={{0,32,64,96},{8,40,72,104},{16,48,80,112},{24,56,88,120},{1,9,17,25},{3..., dimensions={0} | all-to-all | bytes 4325376 | tf_op jit(solution)/shard_map/all_to_all | solution.py:465
  212.7 2.6 %gradient.7 = f32[1024,256]{1,0:T(8,128)S(1)} custom-call(bf16[2048,4096]{1,0:T(8,128)(2,1)S(1)} %get-tuple-element.37.p_ref, bf16[16,16,4224]{2,1,0:T(8,128)(2,1)S(1)} %all_to_all.64.edge_ref.weight_ref), custom_call_target="tpu_custom_call" | custom-call | flops 2147483648 | bytes 8388608 | tf_op jit(solution)/shard_map/gradient/pallas_call | solution.py:477
  216.1 2.6 %gradient.6.own_ref = f32[1024,256]{1,0:T(8,128)S(1)} custom-call(bf16[2048,4096]{1,0:T(8,128)(2,1)S(1)} %get-tuple-element.37.p_ref, bf16[16,16,4224]{2,1,0:T(8,128)(2,1)S(1)} %all_to_all.64.edge_ref.weight_ref), custom_call_target="tpu_custom_call" | custom-call | flops 2147483648 | bytes 8388608 | tf_op jit(solution)/shard_map/gradient/pallas_call | solution.py:477
  220.0 2.0 collective-permute-start.15
  223.0 5.8 %collective-permute-done.14.refs_1_ = bf16[264,256]{1,0:T(8,128)(2,1)S(1)} collective-permute-done((bf16[264,256]{1,0:T(8,128)(2,1)S(1)}, bf16[264,256]{1,0:T(8,128)(2,1)S(1)}, u32[]{:S(2)}, u32[]{:S(2)}) %collective-permute-start.14) | collective-permute-done | bytes 135200 | tf_op jit(solution)/shard_map/ppermute | solution.py:506
  229.8 2.7 %collective-permute-start.19 = (bf16[264,256]{1,0:T(8,128)(2,1)S(1)}, bf16[264,256]{1,0:T(8,128)(2,1)S(1)}, u32[]{:S(2)}, u32[]{:S(2)}) collective-permute-start(bf16[264,256]{1,0:T(8,128)(2,1)S(1)} %get-tuple-element.60.refs_0_), channel_id=1, source_target_pairs={{0,6},{2,0},{4,2},{6,4},{1,7},{3,1},{5,3},{7,5},{8,14},{10,8},{12,... | collective-permute-start | bytes 405512 | tf_op jit(solution)/shard_map/ppermute | solution.py:519
  233.5 5.0 %collective-permute-done.19.refs_3_ = bf16[264,256]{1,0:T(8,128)(2,1)S(1)} collective-permute-done((bf16[264,256]{1,0:T(8,128)(2,1)S(1)}, bf16[264,256]{1,0:T(8,128)(2,1)S(1)}, u32[]{:S(2)}, u32[]{:S(2)}) %collective-permute-start.19) | collective-permute-done | bytes 135200 | tf_op jit(solution)/shard_map/ppermute | solution.py:519
  238.4 2.1 collective-permute-done.18.refs_2_
  243.2 1.5 update.3
  244.7 3.5 %all-to-all-start.10 = ((f32[16,1,256]{2,1,0:T(1,128)}), f32[16,1,256]{2,1,0:T(1,128)S(1)}, u32[]{:S(2)}, u32[]{:S(2)}) async-start(f32[16,1,256]{2,1,0:T(1,128)} %get-tuple-element.63), calls=%async_computation.10 | async-start | bytes 32768 | tf_op jit(solution)/shard_map/all_to_all | solution.py:535
  248.8 7.0 %all-to-all-done.10.totals_ref = f32[16,1,256]{2,1,0:T(1,128)S(1)} async-done(((f32[16,1,256]{2,1,0:T(1,128)}), f32[16,1,256]{2,1,0:T(1,128)S(1)}, u32[]{:S(2)}, u32[]{:S(2)}) %all-to-all-start.10) | async-done | bytes 16416 | tf_op jit(solution)/shard_map/all_to_all | solution.py:535
  255.7 1.9 scale.1
  (62 shorter events, 22.1 us)
Async XLA Ops:
  1.4 0.7 copy-start
  2.1 4.1 %copy-start.1 = (bf16[4096,128]{1,0:T(8,128)(2,1)S(1)}, bf16[4096,128]{1,0:T(8,128)(2,1)}, u32[]{:S(2)}) copy-start(bf16[4096,128]{1,0:T(8,128)(2,1)} %fac_ref.1) | copy-start | bytes 3145732
  103.5 3.4 %collective-permute-start = (f32[1024,256]{1,0:T(8,128)S(1)}, f32[1024,256]{1,0:T(8,128)S(1)}, u32[]{:S(2)}, u32[]{:S(2)}) collective-permute-start(f32[1024,256]{1,0:T(8,128)S(1)} %gradient.5), channel_id=1, source_target_pairs={{0,1},{1,0},{2,3},{3,2},{4,5},{5,4},{6,7},{7,6},{8,9},{9,8},{10,11... | collective-permute-start | bytes 3145736 | tf_op jit(solution)/shard_map/ppermute | solution.py:489
  103.7 3.2 %collective-permute-start.1 = (f32[8,256]{1,0:T(8,128)S(1)}, f32[8,256]{1,0:T(8,128)S(1)}, u32[]{:S(2)}, u32[]{:S(2)}) collective-permute-start(f32[8,256]{1,0:T(8,128)S(1)} %get-tuple-element.42.soft_ref), channel_id=1, source_target_pairs={{0,1},{1,0},{2,3},{3,2},{4,5},{5,4},{6,7},{7,6},{8,9},{9,8},{10,11... | collective-permute-start | bytes 24584 | tf_op jit(solution)/shard_map/ppermute | solution.py:490
  107.3 9.7 %collective-permute-start.2 = (bf16[264,256]{1,0:T(8,128)(2,1)S(1)}, bf16[264,256]{1,0:T(8,128)(2,1)S(1)}, u32[]{:S(2)}, u32[]{:S(2)}) collective-permute-start(bf16[264,256]{1,0:T(8,128)(2,1)S(1)} %get-tuple-element.44), channel_id=1, source_target_pairs={{0,2},{2,4},{4,6},{6,0},{1,3},{3,5},{5,7},{7,1},{8,10},{10,12},{12... | collective-permute-start | bytes 405512 | tf_op jit(solution)/shard_map/ppermute | solution.py:506
  108.1 8.9 %collective-permute-start.3 = (bf16[264,256]{1,0:T(8,128)(2,1)S(1)}, bf16[264,256]{1,0:T(8,128)(2,1)S(1)}, u32[]{:S(2)}, u32[]{:S(2)}) collective-permute-start(bf16[264,256]{1,0:T(8,128)(2,1)S(1)} %get-tuple-element.45), channel_id=1, source_target_pairs={{0,4},{2,6},{4,0},{6,2},{1,5},{3,7},{5,1},{7,3},{8,12},{10,14},{12... | collective-permute-start | bytes 405512 | tf_op jit(solution)/shard_map/ppermute | solution.py:506
  110.1 7.5 %collective-permute-start.4 = (bf16[264,256]{1,0:T(8,128)(2,1)S(1)}, bf16[264,256]{1,0:T(8,128)(2,1)S(1)}, u32[]{:S(2)}, u32[]{:S(2)}) collective-permute-start(bf16[264,256]{1,0:T(8,128)(2,1)S(1)} %get-tuple-element.46), channel_id=1, source_target_pairs={{0,6},{2,0},{4,2},{6,4},{1,7},{3,1},{5,3},{7,5},{8,14},{10,8},{12,... | collective-permute-start | bytes 405512 | tf_op jit(solution)/shard_map/ppermute | solution.py:506
  118.0 8.6 %collective-permute-start.7 = (bf16[264,256]{1,0:T(8,128)(2,1)S(1)}, bf16[264,256]{1,0:T(8,128)(2,1)S(1)}, u32[]{:S(2)}, u32[]{:S(2)}) collective-permute-start(bf16[264,256]{1,0:T(8,128)(2,1)S(1)} %get-tuple-element.47.refs_0_), channel_id=1, source_target_pairs={{0,6},{2,0},{4,2},{6,4},{1,7},{3,1},{5,3},{7,5},{8,14},{10,8},{12,... | collective-permute-start | bytes 405512 | tf_op jit(solution)/shard_map/ppermute | solution.py:519
  120.7 8.0 %collective-permute-start.6 = (bf16[264,256]{1,0:T(8,128)(2,1)S(1)}, bf16[264,256]{1,0:T(8,128)(2,1)S(1)}, u32[]{:S(2)}, u32[]{:S(2)}) collective-permute-start(bf16[264,256]{1,0:T(8,128)(2,1)S(1)} %get-tuple-element.47.refs_0_), channel_id=1, source_target_pairs={{0,4},{2,6},{4,0},{6,2},{1,5},{3,7},{5,1},{7,3},{8,12},{10,14},{12... | collective-permute-start | bytes 405512 | tf_op jit(solution)/shard_map/ppermute | solution.py:519
  120.7 9.3 %collective-permute-start.5 = (bf16[264,256]{1,0:T(8,128)(2,1)S(1)}, bf16[264,256]{1,0:T(8,128)(2,1)S(1)}, u32[]{:S(2)}, u32[]{:S(2)}) collective-permute-start(bf16[264,256]{1,0:T(8,128)(2,1)S(1)} %get-tuple-element.47.refs_0_), channel_id=1, source_target_pairs={{0,2},{2,4},{4,6},{6,0},{1,3},{3,5},{5,7},{7,1},{8,10},{10,12},{12... | collective-permute-start | bytes 405512 | tf_op jit(solution)/shard_map/ppermute | solution.py:519
  121.7 8.4 %collective-permute-start.8 = (bf16[264,256]{1,0:T(8,128)(2,1)S(1)}, bf16[264,256]{1,0:T(8,128)(2,1)S(1)}, u32[]{:S(2)}, u32[]{:S(2)}) collective-permute-start(bf16[264,256]{1,0:T(8,128)(2,1)S(1)} %get-tuple-element.47.refs_0_), channel_id=1, source_target_pairs={{0,1},{1,0},{2,3},{3,2},{4,5},{5,4},{6,7},{7,6},{8,9},{9,8},{10,11... | collective-permute-start | bytes 405512 | tf_op jit(solution)/shard_map/ppermute | solution.py:520
  126.6 3.4 %collective-permute-start.11 = (bf16[264,256]{1,0:T(8,128)(2,1)S(1)}, bf16[264,256]{1,0:T(8,128)(2,1)S(1)}, u32[]{:S(2)}, u32[]{:S(2)}) collective-permute-start(bf16[264,256]{1,0:T(8,128)(2,1)S(1)} %collective-permute-done.7.refs_3_), channel_id=1, source_target_pairs={{0,1},{1,0},{2,3},{3,2},{4,5},{5,4},{6,7},{7,6},{8,9},{9,8},{10,11... | collective-permute-start | bytes 405512 | tf_op jit(solution)/shard_map/ppermute | solution.py:520
  128.7 1.4 collective-permute-start.10
  130.0 1.4 collective-permute-start.9
  215.3 3.4 %collective-permute-start.12 = (f32[1024,256]{1,0:T(8,128)S(1)}, f32[1024,256]{1,0:T(8,128)S(1)}, u32[]{:S(2)}, u32[]{:S(2)}) collective-permute-start(f32[1024,256]{1,0:T(8,128)S(1)} %gradient.7), channel_id=1, source_target_pairs={{0,1},{1,0},{2,3},{3,2},{4,5},{5,4},{6,7},{7,6},{8,9},{9,8},{10,11... | collective-permute-start | bytes 3145736 | tf_op jit(solution)/shard_map/ppermute | solution.py:489
  215.5 3.2 %collective-permute-start.13 = (f32[8,256]{1,0:T(8,128)S(1)}, f32[8,256]{1,0:T(8,128)S(1)}, u32[]{:S(2)}, u32[]{:S(2)}) collective-permute-start(f32[8,256]{1,0:T(8,128)S(1)} %get-tuple-element.55.soft_ref), channel_id=1, source_target_pairs={{0,1},{1,0},{2,3},{3,2},{4,5},{5,4},{6,7},{7,6},{8,9},{9,8},{10,11... | collective-permute-start | bytes 24584 | tf_op jit(solution)/shard_map/ppermute | solution.py:490
  219.2 9.7 %collective-permute-start.14 = (bf16[264,256]{1,0:T(8,128)(2,1)S(1)}, bf16[264,256]{1,0:T(8,128)(2,1)S(1)}, u32[]{:S(2)}, u32[]{:S(2)}) collective-permute-start(bf16[264,256]{1,0:T(8,128)(2,1)S(1)} %get-tuple-element.57), channel_id=1, source_target_pairs={{0,2},{2,4},{4,6},{6,0},{1,3},{3,5},{5,7},{7,1},{8,10},{10,12},{12... | collective-permute-start | bytes 405512 | tf_op jit(solution)/shard_map/ppermute | solution.py:506
  220.0 8.9 %collective-permute-start.15 = (bf16[264,256]{1,0:T(8,128)(2,1)S(1)}, bf16[264,256]{1,0:T(8,128)(2,1)S(1)}, u32[]{:S(2)}, u32[]{:S(2)}) collective-permute-start(bf16[264,256]{1,0:T(8,128)(2,1)S(1)} %get-tuple-element.58), channel_id=1, source_target_pairs={{0,4},{2,6},{4,0},{6,2},{1,5},{3,7},{5,1},{7,3},{8,12},{10,14},{12... | collective-permute-start | bytes 405512 | tf_op jit(solution)/shard_map/ppermute | solution.py:506
  222.0 7.5 %collective-permute-start.16 = (bf16[264,256]{1,0:T(8,128)(2,1)S(1)}, bf16[264,256]{1,0:T(8,128)(2,1)S(1)}, u32[]{:S(2)}, u32[]{:S(2)}) collective-permute-start(bf16[264,256]{1,0:T(8,128)(2,1)S(1)} %get-tuple-element.59), channel_id=1, source_target_pairs={{0,6},{2,0},{4,2},{6,4},{1,7},{3,1},{5,3},{7,5},{8,14},{10,8},{12,... | collective-permute-start | bytes 405512 | tf_op jit(solution)/shard_map/ppermute | solution.py:506
  229.8 8.6 %collective-permute-start.19 = (bf16[264,256]{1,0:T(8,128)(2,1)S(1)}, bf16[264,256]{1,0:T(8,128)(2,1)S(1)}, u32[]{:S(2)}, u32[]{:S(2)}) collective-permute-start(bf16[264,256]{1,0:T(8,128)(2,1)S(1)} %get-tuple-element.60.refs_0_), channel_id=1, source_target_pairs={{0,6},{2,0},{4,2},{6,4},{1,7},{3,1},{5,3},{7,5},{8,14},{10,8},{12,... | collective-permute-start | bytes 405512 | tf_op jit(solution)/shard_map/ppermute | solution.py:519
  232.5 8.0 %collective-permute-start.18 = (bf16[264,256]{1,0:T(8,128)(2,1)S(1)}, bf16[264,256]{1,0:T(8,128)(2,1)S(1)}, u32[]{:S(2)}, u32[]{:S(2)}) collective-permute-start(bf16[264,256]{1,0:T(8,128)(2,1)S(1)} %get-tuple-element.60.refs_0_), channel_id=1, source_target_pairs={{0,4},{2,6},{4,0},{6,2},{1,5},{3,7},{5,1},{7,3},{8,12},{10,14},{12... | collective-permute-start | bytes 405512 | tf_op jit(solution)/shard_map/ppermute | solution.py:519
  232.5 9.3 %collective-permute-start.17 = (bf16[264,256]{1,0:T(8,128)(2,1)S(1)}, bf16[264,256]{1,0:T(8,128)(2,1)S(1)}, u32[]{:S(2)}, u32[]{:S(2)}) collective-permute-start(bf16[264,256]{1,0:T(8,128)(2,1)S(1)} %get-tuple-element.60.refs_0_), channel_id=1, source_target_pairs={{0,2},{2,4},{4,6},{6,0},{1,3},{3,5},{5,7},{7,1},{8,10},{10,12},{12... | collective-permute-start | bytes 405512 | tf_op jit(solution)/shard_map/ppermute | solution.py:519
  233.5 8.4 %collective-permute-start.20 = (bf16[264,256]{1,0:T(8,128)(2,1)S(1)}, bf16[264,256]{1,0:T(8,128)(2,1)S(1)}, u32[]{:S(2)}, u32[]{:S(2)}) collective-permute-start(bf16[264,256]{1,0:T(8,128)(2,1)S(1)} %get-tuple-element.60.refs_0_), channel_id=1, source_target_pairs={{0,1},{1,0},{2,3},{3,2},{4,5},{5,4},{6,7},{7,6},{8,9},{9,8},{10,11... | collective-permute-start | bytes 405512 | tf_op jit(solution)/shard_map/ppermute | solution.py:520
  238.4 3.4 %collective-permute-start.23 = (bf16[264,256]{1,0:T(8,128)(2,1)S(1)}, bf16[264,256]{1,0:T(8,128)(2,1)S(1)}, u32[]{:S(2)}, u32[]{:S(2)}) collective-permute-start(bf16[264,256]{1,0:T(8,128)(2,1)S(1)} %collective-permute-done.19.refs_3_), channel_id=1, source_target_pairs={{0,1},{1,0},{2,3},{3,2},{4,5},{5,4},{6,7},{7,6},{8,9},{9,8},{10,11... | collective-permute-start | bytes 405512 | tf_op jit(solution)/shard_map/ppermute | solution.py:520
  240.5 1.4 collective-permute-start.22
  241.8 1.4 collective-permute-start.21
  244.7 11.0 %all-to-all-start.10 = ((f32[16,1,256]{2,1,0:T(1,128)}), f32[16,1,256]{2,1,0:T(1,128)S(1)}, u32[]{:S(2)}, u32[]{:S(2)}) async-start(f32[16,1,256]{2,1,0:T(1,128)} %get-tuple-element.63), calls=%async_computation.10 | async-start | bytes 32768 | tf_op jit(solution)/shard_map/all_to_all | solution.py:535

commit v6 on v5

--- a/solution.py
+++ b/solution.py
@@ -80,18 +80,34 @@
     return jnp.transpose(jnp.concatenate(rows, axis=0)).astype(bf16)
 
 
-def put_codes(doubled, edge_ref, pay_ref, at):
-    parts, rows = pay_ref.shape[:2]
+def spot():
+    y, z, core = lax.axis_index("y"), lax.axis_index("z"), lax.axis_index("c")
+    return jnp.where(core == 0, y, z), jnp.where(core == 0, z, y)
+
+
+def put_rotated(ref, cols, value, side):
+    rows = value.shape[0] // side
+    for block in range(side):
+        at = pl.multiple_of(lax.rem(block + side - spot()[0], side) * rows, rows)
+        ref[pl.ds(at, rows), cols] = value[block * rows : (block + 1) * rows]
+
+
+def put_codes(doubled, edge_ref, pay_refs, at):
+    parts, rows, wide = pay_refs[0].shape
     span = edge_ref[:, 0:1].astype(f32)
     code = jnp.exp(doubled * (SPAN / span) - 0.5 * SPAN).astype(bf16)
-    pay_ref[:, :, at] = code.reshape(parts, rows, -1)
+    for k, pay_ref in enumerate(pay_refs):
+        part = slice(k * parts * rows, (k + 1) * parts * rows)
+        pay_ref[:, :, at] = code[part].reshape(parts, rows, -1)
 
     @pl.when(pl.program_id(0) == 0)
     def _():
-        pay_ref[:, :, pay_ref.shape[2] - 128 :] = edge_ref[...].reshape(parts, rows, 128)
-
-
-def setup_kernel(hold_ref, lgd_ref, sector_ref, rating_ref, allowed_ref, load_ref, weighted_ref, lge_ref, aug_ref, expot_ref, edge_ref, sums_ref):
+        for k, pay_ref in enumerate(pay_refs):
+            part = slice(k * parts * rows, (k + 1) * parts * rows)
+            pay_ref[:, :, wide - 128 :] = edge_ref[part].reshape(parts, rows, 128)
+
+
+def setup_kernel(side, hold_ref, lgd_ref, sector_ref, rating_ref, allowed_ref, load_ref, weighted_ref, lge_ref, aug_ref, expot_ref, edge_ref, sums_ref):
     rows = sector_ref.shape[1]
     sectors = allowed_ref.shape[0]
     here = pl.ds(pl.multiple_of(pl.program_id(0) * rows, rows), rows)
@@ -108,7 +124,7 @@
     weighted_ref[here] = weighted
     lge_ref[here] = lge
     expo = (lge * hold).astype(bf16).astype(f32)
-    expot_ref[:, here] = jnp.transpose(expo).astype(bf16)
+    put_rotated(expot_ref, here, jnp.transpose(expo).astype(bf16), side)
     lane = lax.broadcasted_iota(jnp.int32, (128, rows), 0)
     rated = ((lane % 16 == rating_ref[...]) & (lane < 48)).astype(f32)
     aug_ref[here] = jnp.concatenate([load_ref[...], jnp.transpose(rated).astype(bf16)], axis=1)
@@ -122,10 +138,10 @@
 
     @pl.when(pl.program_id(0) == pl.num_programs(0) - 1)
     def _():
-        edge_ref[...] = edge_of(sums_ref[0:1], sums_ref[1:2])
-
-
-def first_losses_kernel(load_ref, fac_ref, bar_ref, idio_ref, expot_ref, edge_ref, p_ref, pay_ref):
+        put_rotated(edge_ref, slice(None), edge_of(sums_ref[0:1], sums_ref[1:2]), side)
+
+
+def first_losses_kernel(load_ref, fac_ref, bar_ref, idio_ref, expot_ref, edge_ref, p_ref, *pay_refs):
     wide = fac_ref.shape[0]
     cols = pl.ds(pl.multiple_of(pl.program_id(0) * wide, wide), wide)
     block = min(256, load_ref.shape[0])
@@ -134,49 +150,51 @@
         sl = slice(i * block, (i + 1) * block)
         latent = lax.dot_general(load_ref[sl], fac, (((1,), (1,)), ((), ())), preferred_element_type=f32)
         p_ref[sl, cols] = (jnp.tanh(latent + IDIO_SCALE * idio_ref[sl].astype(f32)) + 1.0).astype(bf16)
-    put_codes(jnp.dot(expot_ref[...], p_ref[:, cols], preferred_element_type=f32), edge_ref, pay_ref, cols)
-
-
-def losses_kernel(wide, p_ref, expot_ref, edge_ref, pay_ref):
+    put_codes(jnp.dot(expot_ref[...], p_ref[:, cols], preferred_element_type=f32), edge_ref, pay_refs, cols)
+
+
+def losses_kernel(wide, p_ref, expot_ref, edge_ref, *pay_refs):
     cols = pl.ds(pl.multiple_of(pl.program_id(0) * wide, wide), wide)
-    put_codes(jnp.dot(expot_ref[...], p_ref[:, cols], preferred_element_type=f32), edge_ref, pay_ref, cols)
-
-
-def mid_kernel(pay_ref, out_ref, part_ref):
-    fewer = out_ref.shape[0]
-    count = pay_ref.shape[0] // fewer
-    wide = part_ref.shape[2]
+    put_codes(jnp.dot(expot_ref[...], p_ref[:, cols], preferred_element_type=f32), edge_ref, pay_refs, cols)
+
+
+def mid_kernel(*refs):
+    part_ref = refs[-1]
+    count = len(refs) // 2
+    pay_refs, out_refs = refs[:count], refs[count:-1]
+    wide = part_ref.shape[1]
     piece = min(1024, wide)
-    lane = lax.broadcasted_iota(jnp.int32, (pay_ref.shape[1], 128), 1)
-    for q in range(fewer):
-        edges = [pay_ref[k * fewer + q, :, wide:].astype(f32) for k in range(count)]
+    lane = lax.broadcasted_iota(jnp.int32, (part_ref.shape[0], 128), 1)
+    for k, out_ref in enumerate(out_refs):
+        row = lax.rem(spot()[1] + k, count)
+        edges = [pay_ref[row, :, wide:].astype(f32) for pay_ref in pay_refs]
         spans = [edge[:, 0:1] for edge in edges]
         offset = 0.5 * sum(spans)
         factors = [span * (1.0 / SPAN) for span in spans]
         low, high = jnp.inf, -jnp.inf
         for at in range(0, wide, piece):
-            codes = [pay_ref[k * fewer + q, :, at : at + piece].astype(f32) for k in range(count)]
+            codes = [pay_ref[row, :, at : at + piece].astype(f32) for pay_ref in pay_refs]
             part = sum(jnp.log(code) * factor for code, factor in zip(codes, factors)) + offset
-            part_ref[q, :, at : at + piece] = part
+            part_ref[:, at : at + piece] = part
             low = jnp.minimum(low, jnp.min(part, axis=1, keepdims=True))
             high = jnp.maximum(high, jnp.max(part, axis=1, keepdims=True))
         span = jnp.maximum(jnp.maximum(high - low, jnp.abs(low) * (1.0 / 64.0)), 1e-30)
         base = low.astype(bf16).astype(f32)
         span = (span * 1.02).astype(bf16).astype(f32)
         for at in range(0, wide, piece):
-            part = part_ref[q, :, at : at + piece]
-            out_ref[q, :, at : at + piece] = jnp.exp((part - base) * (SPAN / span) - 0.5 * SPAN).astype(bf16)
+            part = part_ref[:, at : at + piece]
+            out_ref[:, at : at + piece] = jnp.exp((part - base) * (SPAN / span) - 0.5 * SPAN).astype(bf16)
         total = sum(edge[:, 1:2] + edge[:, 2:3] + edge[:, 3:4] for edge in edges)
         edge = jnp.zeros(lane.shape, f32)
         for at, value in enumerate([base, span] + split3(total)):
             edge = jnp.where(lane == at, value, edge)
-        out_ref[q, :, wide:] = edge.astype(bf16)
-
-
-def sum_kernel(pay_ref, losses_ref, both_ref):
-    count = pay_ref.shape[0]
+        out_ref[:, wide:] = edge.astype(bf16)
+
+
+def sum_kernel(*refs):
+    pay_refs, losses_ref, both_ref = refs[:-2], refs[-2], refs[-1]
     wide = losses_ref.shape[1]
-    edges = [pay_ref[k, :, wide:].astype(f32) for k in range(count)]
+    edges = [pay_ref[:, wide:].astype(f32) for pay_ref in pay_refs]
     spans = [edge[:, 1:2] for edge in edges]
     offset = sum(edge[:, 0:1] for edge in edges) + 0.5 * sum(spans)
     scale = 0.5 / sum(edge[:, 2:3] + edge[:, 3:4] + edge[:, 4:5] for edge in edges)
@@ -184,7 +202,8 @@
     piece = min(1024, wide)
     total = 0.0
     for at in range(0, wide, piece):
-        part = sum(jnp.log(pay_ref[k, :, at : at + piece].astype(f32)) * factors[k] for k in range(count))
+        codes = [pay_ref[:, at : at + piece].astype(f32) for pay_ref in pay_refs]
+        part = sum(jnp.log(code) * factor for code, factor in zip(codes, factors))
         part = (part + offset) * scale
         losses_ref[:, at : at + piece] = part
         total += jnp.sum(part, axis=1, keepdims=True)
@@ -216,22 +235,34 @@
         half = 0.5 * tail_scale
         weight = (jnp.where(scaled >= 0.0, half, half * small) / grown).astype(bf16)
         soft += jnp.sum(jnp.maximum(scaled, 0.0) + jnp.log(grown), axis=1, keepdims=True)
-        for k in range(pay_ref.shape[0]):
-            pay_ref[k, :, at : at + piece] = weight
-    lane = lax.broadcasted_iota(jnp.int32, (pay_ref.shape[1], 128), 1)
+        pay_ref[:, at : at + piece] = weight
+    lane = lax.broadcasted_iota(jnp.int32, (pay_ref.shape[0], 128), 1)
     edge = jnp.zeros(lane.shape, f32)
     for at, part in enumerate(split3(soft) + split3(thresh) + split3(width)):
         edge = jnp.where(lane == at, part, edge)
-    for k in range(pay_ref.shape[0]):
-        pay_ref[k, :, wide:] = edge.astype(bf16)
-
-
-def heads_kernel(edge_ref, soft_ref, stat_ref):
-    rows = jnp.transpose(edge_ref[...].reshape(-1, 128).astype(f32))
-    soft_ref[...] = jnp.broadcast_to(join3(rows, 0), soft_ref.shape)
+    pay_ref[:, wide:] = edge.astype(bf16)
+
+
+def join_kernel(*refs):
+    count = len(refs) - 1
+    for k in range(count):
+        refs[-1][lax.rem(spot()[1] + (count - k), count)] = refs[k][...]
+
+
+def spread_kernel(*refs):
+    pay_refs, (weight_ref, soft_ref, stat_ref, head_ref) = refs[:-4], refs[-4:]
+    count = len(pay_refs)
+    wide = weight_ref.shape[1]
+    rows = weight_ref.shape[0] // count
+    for k, pay_ref in enumerate(pay_refs):
+        at = pl.multiple_of(lax.rem(spot()[0] + (count - k), count) * rows, rows)
+        weight_ref[pl.ds(at, rows)] = pay_ref[:, :, 0:wide].reshape(rows, wide)
+        head_ref[pl.ds(at, rows)] = pay_ref[:, :, wide:].reshape(rows, 128).astype(f32)
+    heads = jnp.transpose(head_ref[...])
+    soft_ref[...] = jnp.broadcast_to(join3(heads, 0), soft_ref.shape)
     stat_ref[...] = jnp.zeros_like(stat_ref)
-    stat_ref[0:1] = join3(rows, 3)
-    stat_ref[1:2] = join3(rows, 6)
+    stat_ref[0:1] = join3(heads, 3)
+    stat_ref[1:2] = join3(heads, 6)
 
 
 def gradient_kernel(own, p_ref, weight_ref, out_ref):
@@ -239,10 +270,9 @@
     core = lax.axis_index("c")
     half = core if own else 1 - core
     at = (half * pl.num_programs(0) + pl.program_id(0)) * rows
-    weight = weight_ref[:, :, 0 : p_ref.shape[1]].reshape(out_ref.shape[1], -1)
     out_ref[...] = lax.dot_general(
         p_ref[pl.ds(pl.multiple_of(at, rows), rows)],
-        weight,
+        weight_ref[...],
         (((1,), (1,)), ((), ())),
         preferred_element_type=f32,
     )
@@ -274,7 +304,7 @@
     short_ref[...] = jnp.broadcast_to(stat_ref[0:1] + stat_ref[1:2] * (soft * tail_scale), short_ref.shape)
 
 
-def update_kernel(count, last, *refs):
+def update_kernel(count, last, side, *refs):
     own_refs, other_refs = refs[:count], refs[count : 2 * count]
     prev_ref, lge_ref, unnorm_ref = refs[2 * count : 2 * count + 3]
     rows = own_refs[0].shape[0] - HEAD
@@ -292,12 +322,12 @@
             total += jnp.sum(unnorm, axis=0, keepdims=True)
             if not last:
                 expo = (unnorm * lge).astype(bf16).astype(f32)
-                refs[-2][:, here] = jnp.transpose(expo).astype(bf16)
+                put_rotated(refs[-2], here, jnp.transpose(expo).astype(bf16), side)
                 reach += jnp.sum(expo, axis=0, keepdims=True)
     if last:
         refs[-1][...] = jnp.broadcast_to(total[None], refs[-1].shape)
     else:
-        refs[-1][...] = edge_of(total, reach)
+        put_rotated(refs[-1], slice(None), edge_of(total, reach), side)
 
 
 def scale_kernel(obligors, unnorm_ref, totals_ref, out_ref):
@@ -336,6 +366,16 @@
         [place(a, b, x, 0) for x in range(n_x)] + [place(b, a, x, 1) for x in range(n_x)] for a in span for b in span
     ]
     return along_y(0) + along_z(1), along_z(0) + along_y(1), same
+
+
+def exchanged(slots, groups):
+    count = len(slots)
+    out = list(slots)
+    for k in sorted(range(1, count), key=lambda k: -min(k, count - k)):
+        out[k] = lax.ppermute(
+            slots[k], PLANE, [(group[i], group[(i + k) % count]) for group in groups for i in range(count)]
+        )
+    return out
 
 
 def rounded(value):
@@ -368,7 +408,7 @@
     sb = min(512, obl_dev)
     line = pl.BlockSpec((1, sb), lambda i: (0, i))
     prev, lge, aug, expot, edge = call(
-        setup_kernel,
+        functools.partial(setup_kernel, side),
         (obl_dev // sb,),
         [
             pl.BlockSpec((sb, mandates), lambda i: (i, 0)),
@@ -395,10 +435,11 @@
     results = []
     prob = None
     for iteration in range(STEPS):
-        pay_shape = sds((n_obl, mr, scn_dev + 128), bf16)
+        quarter = sds((side, mr, scn_dev + 128), bf16)
+        few = sds((mr, scn_dev + 128), bf16)
         wide = min(512, scn_dev)
         if iteration == 0:
-            prob, pay = call(
+            prob, *pays = call(
                 first_losses_kernel,
                 (scn_dev // wide,),
                 [
@@ -409,47 +450,46 @@
                     VMEM,
                     VMEM,
                 ],
-                [VMEM, VMEM],
-                [near_shape((obl_dev, scn_dev), bf16), pay_shape],
+                [VMEM] * (1 + side),
+                [near_shape((obl_dev, scn_dev), bf16)] + [quarter] * side,
                 flops=4 * obl_dev * scn_dev * mandates,
                 nbytes=obl_dev * scn_dev * 4,
                 name="first_losses",
             )(near(aug), factors, bars, idiosyncratic, near(expot), near(edge))
             prob = near(prob)
         else:
-            pay = call(
+            pays = call(
                 functools.partial(losses_kernel, wide),
                 (scn_dev // wide,),
                 [VMEM, VMEM, VMEM],
-                VMEM,
-                pay_shape,
+                [VMEM] * side,
+                [quarter] * side,
                 flops=2 * obl_dev * scn_dev * mandates,
                 nbytes=obl_dev * scn_dev * 2,
                 name="losses",
             )(prob, near(expot), near(edge))
-        pay = lax.all_to_all(pay, PLANE, 0, 0, axis_index_groups=first, tiled=True)
-        few = sds((side, mr, scn_dev + 128), bf16)
-        pay = call(
+        pays = exchanged(pays, first)
+        pays = call(
             mid_kernel,
             (1,),
-            [VMEM],
-            VMEM,
-            few,
-            scratch=[pltpu.VMEM((side, mr, scn_dev), f32)],
+            [VMEM] * side,
+            [VMEM] * side,
+            [few] * side,
+            scratch=[pltpu.VMEM((mr, scn_dev), f32)],
             nbytes=mandates * scn_dev * 2,
             name="mid",
-        )(pay)
-        pay = lax.all_to_all(pay, PLANE, 0, 0, axis_index_groups=second, tiled=True)
+        )(*pays)
+        pays = exchanged(pays, second)
         n_scn = n_x * n_c
         losses, both = call(
             sum_kernel,
             (1,),
-            [VMEM],
+            [VMEM] * side,
             [VMEM, VMEM],
             [near_shape((mr, scn_dev), f32), sds((n_scn, mr, 128), f32)],
             nbytes=mandates * scn_dev * 2,
             name="sum",
-        )(pay)
+        )(*pays)
         both = lax.all_to_all(both, OBL + SCN, 0, 0, axis_index_groups=same, tiled=True)
         weight = call(
             functools.partial(tail_kernel, tail_scale, scenarios),
@@ -460,17 +500,26 @@
             nbytes=mandates * scn_dev * 2,
             name="tail",
         )(near(losses), both)
-        weight = lax.all_to_all(weight, PLANE, 0, 0, axis_index_groups=second, tiled=True)
-        weight = jnp.broadcast_to(weight[None], (side, *weight.shape)).reshape(pay_shape.shape)
-        weight = lax.all_to_all(weight, PLANE, 0, 0, axis_index_groups=first, tiled=True)
-        soft, stat = call(
-            heads_kernel,
-            (1,),
-            [pl.BlockSpec((n_obl, mr, 128), lambda i: (0, 0, scn_dev // 128))],
-            [whole((8, mandates)), whole((8, mandates))],
-            [row8, row8],
-            name="heads",
-        )(weight)
+        weight = call(
+            join_kernel,
+            (1,),
+            [VMEM] * side,
+            VMEM,
+            quarter,
+            nbytes=scn_dev * mandates,
+            name="join",
+        )(*exchanged([weight] * side, second))
+        weight, soft, stat = call(
+            spread_kernel,
+            (1,),
+            [VMEM] * side,
+            [VMEM, whole((8, mandates)), whole((8, mandates))],
+            [near_shape((mandates, scn_dev), bf16), row8, row8],
+            scratch=[pltpu.VMEM((mandates, 128), f32)],
+            nbytes=scn_dev * mandates * 4,
+            name="spread",
+        )(*exchanged([weight] * side, first))
+        weight = near(weight)
         gblock = min(512, half)
 
         def gradient_of(own):
@@ -520,7 +569,7 @@
         others = [lax.ppermute(slot, "c", swap) for slot in slots]
         last = iteration == STEPS - 1
         outs = call(
-            functools.partial(update_kernel, n_x, last),
+            functools.partial(update_kernel, n_x, last, side),
             (1,),
             [VMEM] * (2 * n_x + 2),
             [VMEM] + [VMEM] * (not last) + [VMEM],

time: 258 us -> 246 us (0.953)
  blocking collectives: 150 us -> 17.2 us
  waiting for transfers between devices: 39.3 us -> 115 us
  starting transfers between devices: 19.8 us -> 63.9 us
    all_to_all x8 -> x0, blocking collectives: 132 us -> none  [the longest x2 40.6 us: on_device(): pay = lax.all_to_all(pay, PLANE, 0, 0, axis_index_groups=first, tiled=True)]
    ppermute x0 -> x24, waiting for transfers between devices: none -> 75.6 us  [exchanged(): lax.ppermute(slots[k], PLANE, [(group[i], group[(i + k) % count]) for gro...]
    ppermute x0 -> x24, starting transfers between devices: none -> 43.9 us  [exchanged(): lax.ppermute(slots[k], PLANE, [(group[i], group[(i + k) % count]) for gro...]
    pallas_call x9 -> x11, Pallas kernels: 10.5 us -> 11.1 us  [the longest x1 4.14 us: on_device(): call(functools.partial(setup_kernel, side), (obl_dev // sb,), [pl.BlockSp...]
  transfers between devices with their start and end apart: 25 -> 49, of which waited for: 13 -> 32; matrix products, arithmetic and copies ran while one was open for 0% -> 0% of each run, Pallas kernels for 2% -> 2%
where the time goes in v6:
time: 246 us; the launch traced here: 245 us
  waiting for transfers between devices  115 us (47%)
  starting transfers between devices  63.9 us (26%)
  Pallas kernels  46.3 us (19%)
  blocking collectives  17.2 us (7%)
    ppermute x24, waiting for transfers between devices, exchanged(): lax.ppermute(slots[k], PLANE, [(group[i], group[(i + k) % count]) for gro...  75.6 us
    ppermute x24, starting transfers between devices, exchanged(): lax.ppermute(slots[k], PLANE, [(group[i], group[(i + k) % count]) for gro...  43.9 us
    all_to_all x2, blocking collectives, on_device(): lax.all_to_all(both, OBL + SCN, 0, 0, axis_index_groups=same, tiled=True)  17.2 us
    ppermute x6, waiting for transfers between devices, on_device(): slots[k] = lax.ppermute(pay, 'x', hops[k])  16.7 us
    pallas_call x1, Pallas kernels, on_device(): call(first_losses_kernel, (scn_dev // wide,), [VMEM, pl.BlockSpec((wide,...  14.3 us
    ppermute x6, waiting for transfers between devices, on_device(): slots[k] = lax.ppermute(slots[k], 'x', hops[k])  13 us
    pallas_call x4, Pallas kernels, gradient_of(): call(functools.partial(gradient_kernel, own), (half // gblock,), [VMEM, V...  10.5 us
    ppermute x6, starting transfers between devices, on_device(): slots[k] = lax.ppermute(slots[k], 'x', hops[k])  7.73 us
  transfers between devices with their start and end apart: 49, of which 32 were waited for; matrix products, arithmetic and copies ran while one was open for 0% of the time, Pallas kernels for 2%

profile of v6, /device:TPU:0, one launch (start us, length us, event | category | flops | bytes accessed | tf_op | source)
XLA Modules:
  0.0 245.2 jit_solution(18015099552766702043)
XLA Ops:
  2.1 4.1 %setup.1 = (f32[2048,256]{1,0:T(8,128)S(1)}, f32[2048,256]{1,0:T(8,128)S(1)}, bf16[2048,256]{1,0:T(8,128)(2,1)S(1)}, bf16[256,2048]{1,0:T(8,128)(2,1)S(1)}, bf16[256,128]{1,0:T(8,128)(2,1)S(1)}) custom-call(f32[2048,256]{1,0:T(8,128)} %hold_ref.1, f32[1,2048]{1,0:T(1,128)} %bitcast.7, s32[1,2048]{1,0:T(1,128)} %bitcast.8, s32[1,2048]{1,0:T(1,128)} %bitcast.9, ...), custom_call_target="tpu_custom_call" | custom-call | bytes 6291456 | tf_op jit(solution)/shard_map/setup/pallas_call | solution.py:410
  6.3 14.3 %first_losses.1 = (bf16[2048,4096]{1,0:T(8,128)(2,1)S(1)}, bf16[4,16,4224]{2,1,0:T(8,128)(2,1)S(1)}, bf16[4,16,4224]{2,1,0:T(8,128)(2,1)S(1)}, bf16[4,16,4224]{2,1,0:T(8,128)(2,1)S(1)}, bf16[4,16,4224]{2,1,0:T(8,128)(2,1)S(1)}) custom-call(bf16[2048,256]{1,0:T(8,128)(2,1)S(1)} %get-tuple-element.51.load_ref, bf16[4096,128]{1,0:T(8,128)(2,1)S(1)} %copy-done.1, ...), custom_call_target="tpu_custom_call" | custom-call | flops 8589934592 | bytes 33554432 | tf_op jit(solution)/shard_map/first_losses/pallas_call | solution.py:442
  22.3 2.9 %collective-permute-start.1 = (bf16[4,16,4224]{2,1,0:T(8,128)(2,1)S(1)}, bf16[4,16,4224]{2,1,0:T(8,128)(2,1)S(1)}, u32[]{:S(2)}, u32[]{:S(2)}) collective-permute-start(bf16[4,16,4224]{2,1,0:T(8,128)(2,1)S(1)} %get-tuple-element.57), channel_id=1, source_target_pairs={{0,64},{32,96},{64,0},{96,32},{8,72},{40,104},{72,8},{104,40},{16,... | collective-permute-start | bytes 1622024 | tf_op jit(solution)/shard_map/ppermute | solution.py:375
  26.5 4.6 %collective-permute-done.refs_1_ = bf16[4,16,4224]{2,1,0:T(8,128)(2,1)S(1)} collective-permute-done((bf16[4,16,4224]{2,1,0:T(8,128)(2,1)S(1)}, bf16[4,16,4224]{2,1,0:T(8,128)(2,1)S(1)}, u32[]{:S(2)}, u32[]{:S(2)}) %collective-permute-start) | collective-permute-done | bytes 540704 | tf_op jit(solution)/shard_map/ppermute | solution.py:375
  31.2 7.1 %collective-permute-done.1.refs_2_ = bf16[4,16,4224]{2,1,0:T(8,128)(2,1)S(1)} collective-permute-done((bf16[4,16,4224]{2,1,0:T(8,128)(2,1)S(1)}, bf16[4,16,4224]{2,1,0:T(8,128)(2,1)S(1)}, u32[]{:S(2)}, u32[]{:S(2)}) %collective-permute-start.1) | collective-permute-done | bytes 540704 | tf_op jit(solution)/shard_map/ppermute | solution.py:375
  41.6 3.6 %collective-permute-start.4 = (bf16[16,4224]{1,0:T(8,128)(2,1)S(1)}, bf16[16,4224]{1,0:T(8,128)(2,1)S(1)}, u32[]{:S(2)}, u32[]{:S(2)}) collective-permute-start(bf16[16,4224]{1,0:T(8,128)(2,1)S(1)} %get-tuple-element.61), channel_id=1, source_target_pairs={{0,16},{8,24},{16,0},{24,8},{32,48},{40,56},{48,32},{56,40},{64,80... | collective-permute-start | bytes 405512 | tf_op jit(solution)/shard_map/ppermute | solution.py:375
  46.7 2.9 %collective-permute-done.4.refs_2_ = bf16[16,4224]{1,0:T(8,128)(2,1)S(1)} collective-permute-done((bf16[16,4224]{1,0:T(8,128)(2,1)S(1)}, bf16[16,4224]{1,0:T(8,128)(2,1)S(1)}, u32[]{:S(2)}, u32[]{:S(2)}) %collective-permute-start.4) | collective-permute-done | bytes 135200 | tf_op jit(solution)/shard_map/ppermute | solution.py:375
  50.7 9.4 %all_to_all.15.both_ref = f32[8,16,128]{2,1,0:T(8,128)S(1)} all-to-all(f32[8,16,128]{2,1,0:T(8,128)S(1)} %get-tuple-element.64), channel_id=1, replica_groups={{0,2,4,6,1,3,5,7},{8,10,12,14,33,35,37,39},{16,18,20,22,65,67,69,71},{2..., dimensions={0} | all-to-all | bytes 131072 | tf_op jit(solution)/shard_map/all_to_all | solution.py:493
  60.6 6.1 %collective-permute-start.8 = (bf16[16,4224]{1,0:T(8,128)(2,1)S(1)}, bf16[16,4224]{1,0:T(8,128)(2,1)S(1)}, u32[]{:S(2)}, u32[]{:S(2)}) collective-permute-start(bf16[16,4224]{1,0:T(8,128)(2,1)S(1)} %tail.2.refs_0_), channel_id=1, source_target_pairs={{0,24},{8,0},{16,8},{24,16},{32,56},{40,32},{48,40},{56,48},{64,88... | collective-permute-start | bytes 405512 | tf_op jit(solution)/shard_map/ppermute | solution.py:375
  78.8 10.5 %collective-permute-done.11.refs_3_ = bf16[4,16,4224]{2,1,0:T(8,128)(2,1)S(1)} collective-permute-done((bf16[4,16,4224]{2,1,0:T(8,128)(2,1)S(1)}, bf16[4,16,4224]{2,1,0:T(8,128)(2,1)S(1)}, u32[]{:S(2)}, u32[]{:S(2)}) %collective-permute-start.11) | collective-permute-done | bytes 540704 | tf_op jit(solution)/shard_map/ppermute | solution.py:375
  89.3 3.9 %collective-permute-done.9.refs_1_ = bf16[4,16,4224]{2,1,0:T(8,128)(2,1)S(1)} collective-permute-done((bf16[4,16,4224]{2,1,0:T(8,128)(2,1)S(1)}, bf16[4,16,4224]{2,1,0:T(8,128)(2,1)S(1)}, u32[]{:S(2)}, u32[]{:S(2)}) %collective-permute-start.9) | collective-permute-done | bytes 540704 | tf_op jit(solution)/shard_map/ppermute | solution.py:375
  93.5 2.6 %gradient.5 = f32[1024,256]{1,0:T(8,128)S(1)} custom-call(bf16[2048,4096]{1,0:T(8,128)(2,1)S(1)} %get-tuple-element.54.p_ref, bf16[256,4096]{1,0:T(8,128)(2,1)S(1)} %get-tuple-element.66.weight_ref), custom_call_target="tpu_custom_call" | custom-call | flops 2147483648 | bytes 8388608 | tf_op jit(solution)/shard_map/gradient/pallas_call | solution.py:526
  96.8 2.6 %gradient.4.own_ref = f32[1024,256]{1,0:T(8,128)S(1)} custom-call(bf16[2048,4096]{1,0:T(8,128)(2,1)S(1)} %get-tuple-element.54.p_ref, bf16[256,4096]{1,0:T(8,128)(2,1)S(1)} %get-tuple-element.66.weight_ref), custom_call_target="tpu_custom_call" | custom-call | flops 2147483648 | bytes 8388608 | tf_op jit(solution)/shard_map/gradient/pallas_call | solution.py:526
  103.7 5.9 %collective-permute-done.14.refs_1_ = bf16[264,256]{1,0:T(8,128)(2,1)S(1)} collective-permute-done((bf16[264,256]{1,0:T(8,128)(2,1)S(1)}, bf16[264,256]{1,0:T(8,128)(2,1)S(1)}, u32[]{:S(2)}, u32[]{:S(2)}) %collective-permute-start.14) | collective-permute-done | bytes 135200 | tf_op jit(solution)/shard_map/ppermute | solution.py:555
  110.6 2.7 %collective-permute-start.19 = (bf16[264,256]{1,0:T(8,128)(2,1)S(1)}, bf16[264,256]{1,0:T(8,128)(2,1)S(1)}, u32[]{:S(2)}, u32[]{:S(2)}) collective-permute-start(bf16[264,256]{1,0:T(8,128)(2,1)S(1)} %get-tuple-element.72.refs_0_), channel_id=1, source_target_pairs={{0,6},{2,0},{4,2},{6,4},{1,7},{3,1},{5,3},{7,5},{8,14},{10,8},{12,... | collective-permute-start | bytes 405512 | tf_op jit(solution)/shard_map/ppermute | solution.py:568
  114.2 5.0 %collective-permute-done.19.refs_3_ = bf16[264,256]{1,0:T(8,128)(2,1)S(1)} collective-permute-done((bf16[264,256]{1,0:T(8,128)(2,1)S(1)}, bf16[264,256]{1,0:T(8,128)(2,1)S(1)}, u32[]{:S(2)}, u32[]{:S(2)}) %collective-permute-start.19) | collective-permute-done | bytes 135200 | tf_op jit(solution)/shard_map/ppermute | solution.py:568
  125.4 6.0 %losses.1 = (bf16[4,16,4224]{2,1,0:T(8,128)(2,1)S(1)}, bf16[4,16,4224]{2,1,0:T(8,128)(2,1)S(1)}, bf16[4,16,4224]{2,1,0:T(8,128)(2,1)S(1)}, bf16[4,16,4224]{2,1,0:T(8,128)(2,1)S(1)}) custom-call(bf16[2048,4096]{1,0:T(8,128)(2,1)S(1)} %get-tuple-element.54.p_ref, bf16[256,2048]{1,0:T(8,128)(2,1)S(1)} %get-tuple-element.75.expot_ref, ...), custom_call_target="tpu_custom_call" | custom-call | flops 4294967296 | bytes 16777216 | tf_op jit(solution)/shard_map/losses/pallas_call | solution.py:461
  136.1 11.7 %collective-permute-done.24.refs_1_ = bf16[4,16,4224]{2,1,0:T(8,128)(2,1)S(1)} collective-permute-done((bf16[4,16,4224]{2,1,0:T(8,128)(2,1)S(1)}, bf16[4,16,4224]{2,1,0:T(8,128)(2,1)S(1)}, u32[]{:S(2)}, u32[]{:S(2)}) %collective-permute-start.24) | collective-permute-done | bytes 540704 | tf_op jit(solution)/shard_map/ppermute | solution.py:375
  153.3 4.4 %collective-permute-done.27.refs_1_ = bf16[16,4224]{1,0:T(8,128)(2,1)S(1)} collective-permute-done((bf16[16,4224]{1,0:T(8,128)(2,1)S(1)}, bf16[16,4224]{1,0:T(8,128)(2,1)S(1)}, u32[]{:S(2)}, u32[]{:S(2)}) %collective-permute-start.27) | collective-permute-done | bytes 135200 | tf_op jit(solution)/shard_map/ppermute | solution.py:375
  159.1 7.7 %all_to_all.16.both_ref = f32[8,16,128]{2,1,0:T(8,128)S(1)} all-to-all(f32[8,16,128]{2,1,0:T(8,128)S(1)} %get-tuple-element.86), channel_id=1, replica_groups={{0,2,4,6,1,3,5,7},{8,10,12,14,33,35,37,39},{16,18,20,22,65,67,69,71},{2..., dimensions={0} | all-to-all | bytes 131072 | tf_op jit(solution)/shard_map/all_to_all | solution.py:493
  167.3 6.2 %collective-permute-start.32 = (bf16[16,4224]{1,0:T(8,128)(2,1)S(1)}, bf16[16,4224]{1,0:T(8,128)(2,1)S(1)}, u32[]{:S(2)}, u32[]{:S(2)}) collective-permute-start(bf16[16,4224]{1,0:T(8,128)(2,1)S(1)} %tail.3.refs_0_), channel_id=1, source_target_pairs={{0,24},{8,0},{16,8},{24,16},{32,56},{40,32},{48,40},{56,48},{64,88... | collective-permute-start | bytes 405512 | tf_op jit(solution)/shard_map/ppermute | solution.py:375
  174.6 2.9 %collective-permute-done.32.refs_3_ = bf16[16,4224]{1,0:T(8,128)(2,1)S(1)} collective-permute-done((bf16[16,4224]{1,0:T(8,128)(2,1)S(1)}, bf16[16,4224]{1,0:T(8,128)(2,1)S(1)}, u32[]{:S(2)}, u32[]{:S(2)}) %collective-permute-start.32) | collective-permute-done | bytes 135200 | tf_op jit(solution)/shard_map/ppermute | solution.py:375
  177.4 2.6 %collective-permute-done.31.refs_2_ = bf16[16,4224]{1,0:T(8,128)(2,1)S(1)} collective-permute-done((bf16[16,4224]{1,0:T(8,128)(2,1)S(1)}, bf16[16,4224]{1,0:T(8,128)(2,1)S(1)}, u32[]{:S(2)}, u32[]{:S(2)}) %collective-permute-start.31) | collective-permute-done | bytes 135200 | tf_op jit(solution)/shard_map/ppermute | solution.py:375
  185.3 10.7 %collective-permute-done.35.refs_3_ = bf16[4,16,4224]{2,1,0:T(8,128)(2,1)S(1)} collective-permute-done((bf16[4,16,4224]{2,1,0:T(8,128)(2,1)S(1)}, bf16[4,16,4224]{2,1,0:T(8,128)(2,1)S(1)}, u32[]{:S(2)}, u32[]{:S(2)}) %collective-permute-start.35) | collective-permute-done | bytes 540704 | tf_op jit(solution)/shard_map/ppermute | solution.py:375
  196.0 3.9 %collective-permute-done.33.refs_1_ = bf16[4,16,4224]{2,1,0:T(8,128)(2,1)S(1)} collective-permute-done((bf16[4,16,4224]{2,1,0:T(8,128)(2,1)S(1)}, bf16[4,16,4224]{2,1,0:T(8,128)(2,1)S(1)}, u32[]{:S(2)}, u32[]{:S(2)}) %collective-permute-start.33) | collective-permute-done | bytes 540704 | tf_op jit(solution)/shard_map/ppermute | solution.py:375
  200.2 2.6 %gradient.7 = f32[1024,256]{1,0:T(8,128)S(1)} custom-call(bf16[2048,4096]{1,0:T(8,128)(2,1)S(1)} %get-tuple-element.54.p_ref, bf16[256,4096]{1,0:T(8,128)(2,1)S(1)} %get-tuple-element.88.weight_ref), custom_call_target="tpu_custom_call" | custom-call | flops 2147483648 | bytes 8388608 | tf_op jit(solution)/shard_map/gradient/pallas_call | solution.py:526
  203.6 2.6 %gradient.6.own_ref = f32[1024,256]{1,0:T(8,128)S(1)} custom-call(bf16[2048,4096]{1,0:T(8,128)(2,1)S(1)} %get-tuple-element.54.p_ref, bf16[256,4096]{1,0:T(8,128)(2,1)S(1)} %get-tuple-element.88.weight_ref), custom_call_target="tpu_custom_call" | custom-call | flops 2147483648 | bytes 8388608 | tf_op jit(solution)/shard_map/gradient/pallas_call | solution.py:526
  210.6 5.9 %collective-permute-done.38.refs_1_ = bf16[264,256]{1,0:T(8,128)(2,1)S(1)} collective-permute-done((bf16[264,256]{1,0:T(8,128)(2,1)S(1)}, bf16[264,256]{1,0:T(8,128)(2,1)S(1)}, u32[]{:S(2)}, u32[]{:S(2)}) %collective-permute-start.38) | collective-permute-done | bytes 135200 | tf_op jit(solution)/shard_map/ppermute | solution.py:555
  217.5 2.7 %collective-permute-start.43 = (bf16[264,256]{1,0:T(8,128)(2,1)S(1)}, bf16[264,256]{1,0:T(8,128)(2,1)S(1)}, u32[]{:S(2)}, u32[]{:S(2)}) collective-permute-start(bf16[264,256]{1,0:T(8,128)(2,1)S(1)} %get-tuple-element.94.refs_0_), channel_id=1, source_target_pairs={{0,6},{2,0},{4,2},{6,4},{1,7},{3,1},{5,3},{7,5},{8,14},{10,8},{12,... | collective-permute-start | bytes 405512 | tf_op jit(solution)/shard_map/ppermute | solution.py:568
  221.1 5.0 %collective-permute-done.43.refs_3_ = bf16[264,256]{1,0:T(8,128)(2,1)S(1)} collective-permute-done((bf16[264,256]{1,0:T(8,128)(2,1)S(1)}, bf16[264,256]{1,0:T(8,128)(2,1)S(1)}, u32[]{:S(2)}, u32[]{:S(2)}) %collective-permute-start.43) | collective-permute-done | bytes 135200 | tf_op jit(solution)/shard_map/ppermute | solution.py:568
  232.3 3.5 %all-to-all-start.2 = ((f32[16,1,256]{2,1,0:T(1,128)}), f32[16,1,256]{2,1,0:T(1,128)S(1)}, u32[]{:S(2)}, u32[]{:S(2)}) async-start(f32[16,1,256]{2,1,0:T(1,128)} %get-tuple-element.97), calls=%async_computation.2 | async-start | bytes 32768 | tf_op jit(solution)/shard_map/all_to_all | solution.py:584
  236.4 7.0 %all-to-all-done.2.totals_ref = f32[16,1,256]{2,1,0:T(1,128)S(1)} async-done(((f32[16,1,256]{2,1,0:T(1,128)}), f32[16,1,256]{2,1,0:T(1,128)S(1)}, u32[]{:S(2)}, u32[]{:S(2)}) %all-to-all-start.2) | async-done | bytes 16416 | tf_op jit(solution)/shard_map/all_to_all | solution.py:584
  (102 shorter events, 70.6 us)
Async XLA Ops:
  20.5 10.6 %collective-permute-start = (bf16[4,16,4224]{2,1,0:T(8,128)(2,1)S(1)}, bf16[4,16,4224]{2,1,0:T(8,128)(2,1)S(1)}, u32[]{:S(2)}, u32[]{:S(2)}) collective-permute-start(bf16[4,16,4224]{2,1,0:T(8,128)(2,1)S(1)} %get-tuple-element.56), channel_id=1, source_target_pairs={{0,32},{32,64},{64,96},{96,0},{8,40},{40,72},{72,104},{104,8},{16,... | collective-permute-start | bytes 1622024 | tf_op jit(solution)/shard_map/ppermute | solution.py:375
  22.3 16.0 %collective-permute-start.1 = (bf16[4,16,4224]{2,1,0:T(8,128)(2,1)S(1)}, bf16[4,16,4224]{2,1,0:T(8,128)(2,1)S(1)}, u32[]{:S(2)}, u32[]{:S(2)}) collective-permute-start(bf16[4,16,4224]{2,1,0:T(8,128)(2,1)S(1)} %get-tuple-element.57), channel_id=1, source_target_pairs={{0,64},{32,96},{64,0},{96,32},{8,72},{40,104},{72,8},{104,40},{16,... | collective-permute-start | bytes 1622024 | tf_op jit(solution)/shard_map/ppermute | solution.py:375
  25.2 13.1 %collective-permute-start.2 = (bf16[4,16,4224]{2,1,0:T(8,128)(2,1)S(1)}, bf16[4,16,4224]{2,1,0:T(8,128)(2,1)S(1)}, u32[]{:S(2)}, u32[]{:S(2)}) collective-permute-start(bf16[4,16,4224]{2,1,0:T(8,128)(2,1)S(1)} %get-tuple-element.58), channel_id=1, source_target_pairs={{0,96},{32,0},{64,32},{96,64},{8,104},{40,8},{72,40},{104,72},{16,... | collective-permute-start | bytes 1622024 | tf_op jit(solution)/shard_map/ppermute | solution.py:375
  41.6 8.0 %collective-permute-start.4 = (bf16[16,4224]{1,0:T(8,128)(2,1)S(1)}, bf16[16,4224]{1,0:T(8,128)(2,1)S(1)}, u32[]{:S(2)}, u32[]{:S(2)}) collective-permute-start(bf16[16,4224]{1,0:T(8,128)(2,1)S(1)} %get-tuple-element.61), channel_id=1, source_target_pairs={{0,16},{8,24},{16,0},{24,8},{32,48},{40,56},{48,32},{56,40},{64,80... | collective-permute-start | bytes 405512 | tf_op jit(solution)/shard_map/ppermute | solution.py:375
  60.6 10.1 %collective-permute-start.8 = (bf16[16,4224]{1,0:T(8,128)(2,1)S(1)}, bf16[16,4224]{1,0:T(8,128)(2,1)S(1)}, u32[]{:S(2)}, u32[]{:S(2)}) collective-permute-start(bf16[16,4224]{1,0:T(8,128)(2,1)S(1)} %tail.2.refs_0_), channel_id=1, source_target_pairs={{0,24},{8,0},{16,8},{24,16},{32,56},{40,32},{48,40},{56,48},{64,88... | collective-permute-start | bytes 405512 | tf_op jit(solution)/shard_map/ppermute | solution.py:375
  74.7 14.6 %collective-permute-start.11 = (bf16[4,16,4224]{2,1,0:T(8,128)(2,1)S(1)}, bf16[4,16,4224]{2,1,0:T(8,128)(2,1)S(1)}, u32[]{:S(2)}, u32[]{:S(2)}) collective-permute-start(bf16[4,16,4224]{2,1,0:T(8,128)(2,1)S(1)} %join.2.refs_0_), channel_id=1, source_target_pairs={{0,96},{32,0},{64,32},{96,64},{8,104},{40,8},{72,40},{104,72},{16,... | collective-permute-start | bytes 1622024 | tf_op jit(solution)/shard_map/ppermute | solution.py:375
  76.6 12.7 %collective-permute-start.10 = (bf16[4,16,4224]{2,1,0:T(8,128)(2,1)S(1)}, bf16[4,16,4224]{2,1,0:T(8,128)(2,1)S(1)}, u32[]{:S(2)}, u32[]{:S(2)}) collective-permute-start(bf16[4,16,4224]{2,1,0:T(8,128)(2,1)S(1)} %join.2.refs_0_), channel_id=1, source_target_pairs={{0,64},{32,96},{64,0},{96,32},{8,72},{40,104},{72,8},{104,40},{16,... | collective-permute-start | bytes 1622024 | tf_op jit(solution)/shard_map/ppermute | solution.py:375
  78.8 14.5 %collective-permute-start.9 = (bf16[4,16,4224]{2,1,0:T(8,128)(2,1)S(1)}, bf16[4,16,4224]{2,1,0:T(8,128)(2,1)S(1)}, u32[]{:S(2)}, u32[]{:S(2)}) collective-permute-start(bf16[4,16,4224]{2,1,0:T(8,128)(2,1)S(1)} %join.2.refs_0_), channel_id=1, source_target_pairs={{0,32},{32,64},{64,96},{96,0},{8,40},{40,72},{72,104},{104,8},{16,... | collective-permute-start | bytes 1622024 | tf_op jit(solution)/shard_map/ppermute | solution.py:375
  99.9 9.8 %collective-permute-start.14 = (bf16[264,256]{1,0:T(8,128)(2,1)S(1)}, bf16[264,256]{1,0:T(8,128)(2,1)S(1)}, u32[]{:S(2)}, u32[]{:S(2)}) collective-permute-start(bf16[264,256]{1,0:T(8,128)(2,1)S(1)} %get-tuple-element.69), channel_id=1, source_target_pairs={{0,2},{2,4},{4,6},{6,0},{1,3},{3,5},{5,7},{7,1},{8,10},{10,12},{12... | collective-permute-start | bytes 405512 | tf_op jit(solution)/shard_map/ppermute | solution.py:555
  100.7 9.0 %collective-permute-start.15 = (bf16[264,256]{1,0:T(8,128)(2,1)S(1)}, bf16[264,256]{1,0:T(8,128)(2,1)S(1)}, u32[]{:S(2)}, u32[]{:S(2)}) collective-permute-start(bf16[264,256]{1,0:T(8,128)(2,1)S(1)} %get-tuple-element.70), channel_id=1, source_target_pairs={{0,4},{2,6},{4,0},{6,2},{1,5},{3,7},{5,1},{7,3},{8,12},{10,14},{12... | collective-permute-start | bytes 405512 | tf_op jit(solution)/shard_map/ppermute | solution.py:555
  102.6 7.6 %collective-permute-start.16 = (bf16[264,256]{1,0:T(8,128)(2,1)S(1)}, bf16[264,256]{1,0:T(8,128)(2,1)S(1)}, u32[]{:S(2)}, u32[]{:S(2)}) collective-permute-start(bf16[264,256]{1,0:T(8,128)(2,1)S(1)} %get-tuple-element.71), channel_id=1, source_target_pairs={{0,6},{2,0},{4,2},{6,4},{1,7},{3,1},{5,3},{7,5},{8,14},{10,8},{12,... | collective-permute-start | bytes 405512 | tf_op jit(solution)/shard_map/ppermute | solution.py:555
  110.6 8.6 %collective-permute-start.19 = (bf16[264,256]{1,0:T(8,128)(2,1)S(1)}, bf16[264,256]{1,0:T(8,128)(2,1)S(1)}, u32[]{:S(2)}, u32[]{:S(2)}) collective-permute-start(bf16[264,256]{1,0:T(8,128)(2,1)S(1)} %get-tuple-element.72.refs_0_), channel_id=1, source_target_pairs={{0,6},{2,0},{4,2},{6,4},{1,7},{3,1},{5,3},{7,5},{8,14},{10,8},{12,... | collective-permute-start | bytes 405512 | tf_op jit(solution)/shard_map/ppermute | solution.py:568
  113.3 8.0 %collective-permute-start.18 = (bf16[264,256]{1,0:T(8,128)(2,1)S(1)}, bf16[264,256]{1,0:T(8,128)(2,1)S(1)}, u32[]{:S(2)}, u32[]{:S(2)}) collective-permute-start(bf16[264,256]{1,0:T(8,128)(2,1)S(1)} %get-tuple-element.72.refs_0_), channel_id=1, source_target_pairs={{0,4},{2,6},{4,0},{6,2},{1,5},{3,7},{5,1},{7,3},{8,12},{10,14},{12... | collective-permute-start | bytes 405512 | tf_op jit(solution)/shard_map/ppermute | solution.py:568
  113.3 9.3 %collective-permute-start.17 = (bf16[264,256]{1,0:T(8,128)(2,1)S(1)}, bf16[264,256]{1,0:T(8,128)(2,1)S(1)}, u32[]{:S(2)}, u32[]{:S(2)}) collective-permute-start(bf16[264,256]{1,0:T(8,128)(2,1)S(1)} %get-tuple-element.72.refs_0_), channel_id=1, source_target_pairs={{0,2},{2,4},{4,6},{6,0},{1,3},{3,5},{5,7},{7,1},{8,10},{10,12},{12... | collective-permute-start | bytes 405512 | tf_op jit(solution)/shard_map/ppermute | solution.py:568
  114.2 8.4 %collective-permute-start.20 = (bf16[264,256]{1,0:T(8,128)(2,1)S(1)}, bf16[264,256]{1,0:T(8,128)(2,1)S(1)}, u32[]{:S(2)}, u32[]{:S(2)}) collective-permute-start(bf16[264,256]{1,0:T(8,128)(2,1)S(1)} %get-tuple-element.72.refs_0_), channel_id=1, source_target_pairs={{0,1},{1,0},{2,3},{3,2},{4,5},{5,4},{6,7},{7,6},{8,9},{9,8},{10,11... | collective-permute-start | bytes 405512 | tf_op jit(solution)/shard_map/ppermute | solution.py:569
  131.4 16.4 %collective-permute-start.24 = (bf16[4,16,4224]{2,1,0:T(8,128)(2,1)S(1)}, bf16[4,16,4224]{2,1,0:T(8,128)(2,1)S(1)}, u32[]{:S(2)}, u32[]{:S(2)}) collective-permute-start(bf16[4,16,4224]{2,1,0:T(8,128)(2,1)S(1)} %get-tuple-element.78), channel_id=1, source_target_pairs={{0,32},{32,64},{64,96},{96,0},{8,40},{40,72},{72,104},{104,8},{16,... | collective-permute-start | bytes 1622024 | tf_op jit(solution)/shard_map/ppermute | solution.py:375
  132.1 15.7 %collective-permute-start.25 = (bf16[4,16,4224]{2,1,0:T(8,128)(2,1)S(1)}, bf16[4,16,4224]{2,1,0:T(8,128)(2,1)S(1)}, u32[]{:S(2)}, u32[]{:S(2)}) collective-permute-start(bf16[4,16,4224]{2,1,0:T(8,128)(2,1)S(1)} %get-tuple-element.79), channel_id=1, source_target_pairs={{0,64},{32,96},{64,0},{96,32},{8,72},{40,104},{72,8},{104,40},{16,... | collective-permute-start | bytes 1622024 | tf_op jit(solution)/shard_map/ppermute | solution.py:375
  133.5 15.1 %collective-permute-start.26 = (bf16[4,16,4224]{2,1,0:T(8,128)(2,1)S(1)}, bf16[4,16,4224]{2,1,0:T(8,128)(2,1)S(1)}, u32[]{:S(2)}, u32[]{:S(2)}) collective-permute-start(bf16[4,16,4224]{2,1,0:T(8,128)(2,1)S(1)} %get-tuple-element.80), channel_id=1, source_target_pairs={{0,96},{32,0},{64,32},{96,64},{8,104},{40,8},{72,40},{104,72},{16,... | collective-permute-start | bytes 1622024 | tf_op jit(solution)/shard_map/ppermute | solution.py:375
  150.0 7.7 %collective-permute-start.27 = (bf16[16,4224]{1,0:T(8,128)(2,1)S(1)}, bf16[16,4224]{1,0:T(8,128)(2,1)S(1)}, u32[]{:S(2)}, u32[]{:S(2)}) collective-permute-start(bf16[16,4224]{1,0:T(8,128)(2,1)S(1)} %get-tuple-element.82), channel_id=1, source_target_pairs={{0,8},{8,16},{16,24},{24,0},{32,40},{40,48},{48,56},{56,32},{64,72... | collective-permute-start | bytes 405512 | tf_op jit(solution)/shard_map/ppermute | solution.py:375
  167.3 10.2 %collective-permute-start.32 = (bf16[16,4224]{1,0:T(8,128)(2,1)S(1)}, bf16[16,4224]{1,0:T(8,128)(2,1)S(1)}, u32[]{:S(2)}, u32[]{:S(2)}) collective-permute-start(bf16[16,4224]{1,0:T(8,128)(2,1)S(1)} %tail.3.refs_0_), channel_id=1, source_target_pairs={{0,24},{8,0},{16,8},{24,16},{32,56},{40,32},{48,40},{56,48},{64,88... | collective-permute-start | bytes 405512 | tf_op jit(solution)/shard_map/ppermute | solution.py:375
  173.4 7.7 %collective-permute-start.30 = (bf16[16,4224]{1,0:T(8,128)(2,1)S(1)}, bf16[16,4224]{1,0:T(8,128)(2,1)S(1)}, u32[]{:S(2)}, u32[]{:S(2)}) collective-permute-start(bf16[16,4224]{1,0:T(8,128)(2,1)S(1)} %tail.3.refs_0_), channel_id=1, source_target_pairs={{0,8},{8,16},{16,24},{24,0},{32,40},{40,48},{48,56},{56,32},{64,72... | collective-permute-start | bytes 405512 | tf_op jit(solution)/shard_map/ppermute | solution.py:375
  181.2 14.8 %collective-permute-start.35 = (bf16[4,16,4224]{2,1,0:T(8,128)(2,1)S(1)}, bf16[4,16,4224]{2,1,0:T(8,128)(2,1)S(1)}, u32[]{:S(2)}, u32[]{:S(2)}) collective-permute-start(bf16[4,16,4224]{2,1,0:T(8,128)(2,1)S(1)} %join.3.refs_0_), channel_id=1, source_target_pairs={{0,96},{32,0},{64,32},{96,64},{8,104},{40,8},{72,40},{104,72},{16,... | collective-permute-start | bytes 1622024 | tf_op jit(solution)/shard_map/ppermute | solution.py:375
  183.3 12.7 %collective-permute-start.34 = (bf16[4,16,4224]{2,1,0:T(8,128)(2,1)S(1)}, bf16[4,16,4224]{2,1,0:T(8,128)(2,1)S(1)}, u32[]{:S(2)}, u32[]{:S(2)}) collective-permute-start(bf16[4,16,4224]{2,1,0:T(8,128)(2,1)S(1)} %join.3.refs_0_), channel_id=1, source_target_pairs={{0,64},{32,96},{64,0},{96,32},{8,72},{40,104},{72,8},{104,40},{16,... | collective-permute-start | bytes 1622024 | tf_op jit(solution)/shard_map/ppermute | solution.py:375
  185.3 14.6 %collective-permute-start.33 = (bf16[4,16,4224]{2,1,0:T(8,128)(2,1)S(1)}, bf16[4,16,4224]{2,1,0:T(8,128)(2,1)S(1)}, u32[]{:S(2)}, u32[]{:S(2)}) collective-permute-start(bf16[4,16,4224]{2,1,0:T(8,128)(2,1)S(1)} %join.3.refs_0_), channel_id=1, source_target_pairs={{0,32},{32,64},{64,96},{96,0},{8,40},{40,72},{72,104},{104,8},{16,... | collective-permute-start | bytes 1622024 | tf_op jit(solution)/shard_map/ppermute | solution.py:375
  206.7 9.8 %collective-permute-start.38 = (bf16[264,256]{1,0:T(8,128)(2,1)S(1)}, bf16[264,256]{1,0:T(8,128)(2,1)S(1)}, u32[]{:S(2)}, u32[]{:S(2)}) collective-permute-start(bf16[264,256]{1,0:T(8,128)(2,1)S(1)} %get-tuple-element.91), channel_id=1, source_target_pairs={{0,2},{2,4},{4,6},{6,0},{1,3},{3,5},{5,7},{7,1},{8,10},{10,12},{12... | collective-permute-start | bytes 405512 | tf_op jit(solution)/shard_map/ppermute | solution.py:555
  207.5 9.0 %collective-permute-start.39 = (bf16[264,256]{1,0:T(8,128)(2,1)S(1)}, bf16[264,256]{1,0:T(8,128)(2,1)S(1)}, u32[]{:S(2)}, u32[]{:S(2)}) collective-permute-start(bf16[264,256]{1,0:T(8,128)(2,1)S(1)} %get-tuple-element.92), channel_id=1, source_target_pairs={{0,4},{2,6},{4,0},{6,2},{1,5},{3,7},{5,1},{7,3},{8,12},{10,14},{12... | collective-permute-start | bytes 405512 | tf_op jit(solution)/shard_map/ppermute | solution.py:555
  209.5 7.6 %collective-permute-start.40 = (bf16[264,256]{1,0:T(8,128)(2,1)S(1)}, bf16[264,256]{1,0:T(8,128)(2,1)S(1)}, u32[]{:S(2)}, u32[]{:S(2)}) collective-permute-start(bf16[264,256]{1,0:T(8,128)(2,1)S(1)} %get-tuple-element.93), channel_id=1, source_target_pairs={{0,6},{2,0},{4,2},{6,4},{1,7},{3,1},{5,3},{7,5},{8,14},{10,8},{12,... | collective-permute-start | bytes 405512 | tf_op jit(solution)/shard_map/ppermute | solution.py:555
  217.5 8.6 %collective-permute-start.43 = (bf16[264,256]{1,0:T(8,128)(2,1)S(1)}, bf16[264,256]{1,0:T(8,128)(2,1)S(1)}, u32[]{:S(2)}, u32[]{:S(2)}) collective-permute-start(bf16[264,256]{1,0:T(8,128)(2,1)S(1)} %get-tuple-element.94.refs_0_), channel_id=1, source_target_pairs={{0,6},{2,0},{4,2},{6,4},{1,7},{3,1},{5,3},{7,5},{8,14},{10,8},{12,... | collective-permute-start | bytes 405512 | tf_op jit(solution)/shard_map/ppermute | solution.py:568
  220.1 8.0 %collective-permute-start.42 = (bf16[264,256]{1,0:T(8,128)(2,1)S(1)}, bf16[264,256]{1,0:T(8,128)(2,1)S(1)}, u32[]{:S(2)}, u32[]{:S(2)}) collective-permute-start(bf16[264,256]{1,0:T(8,128)(2,1)S(1)} %get-tuple-element.94.refs_0_), channel_id=1, source_target_pairs={{0,4},{2,6},{4,0},{6,2},{1,5},{3,7},{5,1},{7,3},{8,12},{10,14},{12... | collective-permute-start | bytes 405512 | tf_op jit(solution)/shard_map/ppermute | solution.py:568
  220.1 9.3 %collective-permute-start.41 = (bf16[264,256]{1,0:T(8,128)(2,1)S(1)}, bf16[264,256]{1,0:T(8,128)(2,1)S(1)}, u32[]{:S(2)}, u32[]{:S(2)}) collective-permute-start(bf16[264,256]{1,0:T(8,128)(2,1)S(1)} %get-tuple-element.94.refs_0_), channel_id=1, source_target_pairs={{0,2},{2,4},{4,6},{6,0},{1,3},{3,5},{5,7},{7,1},{8,10},{10,12},{12... | collective-permute-start | bytes 405512 | tf_op jit(solution)/shard_map/ppermute | solution.py:568
  221.1 8.4 %collective-permute-start.44 = (bf16[264,256]{1,0:T(8,128)(2,1)S(1)}, bf16[264,256]{1,0:T(8,128)(2,1)S(1)}, u32[]{:S(2)}, u32[]{:S(2)}) collective-permute-start(bf16[264,256]{1,0:T(8,128)(2,1)S(1)} %get-tuple-element.94.refs_0_), channel_id=1, source_target_pairs={{0,1},{1,0},{2,3},{3,2},{4,5},{5,4},{6,7},{7,6},{8,9},{9,8},{10,11... | collective-permute-start | bytes 405512 | tf_op jit(solution)/shard_map/ppermute | solution.py:569
  232.3 11.1 %all-to-all-start.2 = ((f32[16,1,256]{2,1,0:T(1,128)}), f32[16,1,256]{2,1,0:T(1,128)S(1)}, u32[]{:S(2)}, u32[]{:S(2)}) async-start(f32[16,1,256]{2,1,0:T(1,128)} %get-tuple-element.97), calls=%async_computation.2 | async-start | bytes 32768 | tf_op jit(solution)/shard_map/all_to_all | solution.py:584
  (19 other events, 77.7 us)
